TPU v7x, 32 devices: a whole 2x2x4 slice. The times are simulated.
32 devices in a mesh: dp: 8 (over z, core), tensor: 4 (over y, x).
Axes of the slice: x: 2, y: 2, z: 4, core: 2. Of those that a mesh axis runs over, the one named last changes fastest.
Arguments:
- activations: bfloat16 [18432, 8192], P('dp', 'tensor'), may hold values from -6 to 6
- out_grads: bfloat16 [18432, 28672], P('dp', 'tensor'), may hold values from -0.078125 to 0.078125
- basis: bfloat16 [8192, 256], P('tensor'), may hold values from -0.375 to 0.375
- first_moment: float32 [256, 28672], P('dp', 'tensor'), may hold values from -6 to 6
- second_moment: float32 [256, 28672], P('dp', 'tensor'), may hold values from 0.05 to 0.8
- reward_codes: int32 [18432], P('dp'), may hold values from 0 to 15
- token_ids: int32 [18432], P('dp'), may hold values from 0 to 128004, as said below
Outputs:
- new_first: float32 [256, 28672], P('dp', 'tensor')
- new_second: float32 [256, 28672], P('dp', 'tensor')
- weight_update: bfloat16 [8192, 28672], P('dp', 'tensor')
Inputs may be any that keep to these rules, and one draw needn't show every extreme that they name: `token_ids`: the id 128004 is the padding token; the first of each 2304 consecutive tokens is never padding.
All inputs are finite; a program needn't handle non-finite values.
Results may differ from a plain program's by a relative error of at most 0.019.
Values may be sent and summed in bfloat16 or wider, within the bound.
No kernel may reach another device: no remote copies, remote signals or barrier semaphores. Data moves between devices by JAX's collectives and lax.ppermute only.
A program may use at most 128 MiB of HBM per device.

v0:
```python
import jax
import jax.numpy as jnp
from jax import lax
from jax.sharding import PartitionSpec as P

ADAM_STEP = 100


pad_token = 128004
reward_temp = 0.2
beta_one = 0.9
beta_two = 0.999
adam_eps = 1e-08


def from_root(block, axis, owner):
    block = jnp.where(lax.axis_index(axis) == owner, block, jnp.zeros_like(block))
    return lax.psum(block, axis)


def local(activations, out_grads, basis, first_moment, second_moment, reward_codes, token_ids):
    data_count = lax.axis_size("dp")
    tensor_count = lax.axis_size("tensor")
    partial_value = jnp.dot(activations, basis, preferred_element_type=jnp.float32)
    projected = lax.psum(partial_value.astype(jnp.bfloat16), "tensor").astype(jnp.float32)
    unmasked = (token_ids != pad_token).astype(jnp.float32)
    weights = unmasked * jnp.exp(reward_temp * reward_codes.astype(jnp.float32))
    local_total = jnp.sum(weights)
    weighted = (weights[:, None] * projected).astype(jnp.bfloat16)
    raw_grad = lax.dot_general(
        weighted, out_grads, (((0,), (0,)), ((), ())), preferred_element_type=jnp.float32
    )
    normalizer = lax.psum(local_total, "dp")
    grad_rows = lax.psum_scatter(
        raw_grad.astype(jnp.bfloat16), "dp", scatter_dimension=0, tiled=True
    ).astype(jnp.float32)
    token_count = activations.shape[0] * data_count
    gradient = grad_rows * (token_count / normalizer)
    new_first = beta_one * first_moment + (1.0 - beta_one) * gradient
    new_second = beta_two * second_moment + (1.0 - beta_two) * gradient * gradient
    bias_one = 1.0 - beta_one**ADAM_STEP
    bias_two = 1.0 - beta_two**ADAM_STEP
    update = (new_first / bias_one / (jnp.sqrt(new_second / bias_two) + adam_eps)).astype(
        jnp.bfloat16
    )
    row_count = basis.shape[0] * tensor_count // data_count
    data_index = lax.axis_index("dp")
    owner_index = data_index * tensor_count // data_count
    owner_rows = from_root(basis, "tensor", owner_index)
    offset = data_index % (data_count // tensor_count) * row_count
    basis_rows = lax.dynamic_slice_in_dim(owner_rows, offset, row_count, 0)
    summed = jnp.dot(
        basis_rows,
        lax.all_gather(update, "dp", axis=0, tiled=True),
        preferred_element_type=jnp.float32,
    )
    return (new_first, new_second, summed.astype(jnp.bfloat16))


def solution(mesh):
    return jax.shard_map(
        local,
        mesh=mesh,
        in_specs=(
            P("dp", "tensor"),
            P("dp", "tensor"),
            P("tensor", None),
            P("dp", "tensor"),
            P("dp", "tensor"),
            P("dp"),
            P("dp"),
        ),
        out_specs=(P("dp", "tensor"), P("dp", "tensor"), P("dp", "tensor")),
        check_vma=False,
    )
```

profile of v0, /device:TPU:0, one launch (start us, length us, event | category | flops | bytes accessed | tf_op | source)
XLA Modules:
  0.0 213.5 jit_solution(15138136862302459655)
XLA Ops:
  7.2 0.0 all-reduce.3.cloned.1.call-start
  7.2 2.3 %broadcast_select_fusion = bf16[2048,256]{1,0:T(8,128)(2,1)} fusion(bf16[2048,256]{1,0:T(8,128)(2,1)} %param.9, pred[]{:T(512)S(6)} %eq.5), kind=kLoop, calls=%fused_computation.6 | loop fusion | flops 524288 | bytes 2097153 | tf_op jit(solution)/shard_map/jit(_where)/select_n | solution.py:17
  9.5 0.0 copy-start.3
  9.5 0.0 copy-start.4
  9.5 7.6 %convolution_convert_fusion.2 = bf16[2304,256]{1,0:T(8,128)(2,1)} fusion(bf16[2304,2048]{1,0:T(8,128)(2,1)} %param.7, bf16[2048,256]{1,0:T(8,128)(2,1)} %param.9), kind=kOutput, calls=%fused_computation.2 | convolution fusion | flops 2416508928 | bytes 11665408 | tf_op jit(solution)/shard_map/dot_general | solution.py:24
  17.1 0.0 all-reduce.3.cloned.1.call-update
  17.1 0.0 reduce-scatter.2.cloned.1.call-start
  17.2 0.0 copy-done.3
  17.2 0.0 copy-done.4
  17.2 0.6 fusion.5
  17.8 73.9 %all-reduce.3.cloned.1.call-done = (bf16[2304,256]{1,0:T(8,128)(2,1)}, bf16[2048,256]{1,0:T(8,128)(2,1)}) async-done(((bf16[2304,256]{1,0:T(8,128)(2,1)}, bf16[2048,256]{1,0:T(8,128)(2,1)}), (bf16[2304,256]{1,0:T(8,128)(2,1)}, bf16[2048,256]{1,0:T(8,128)(2,1)})) %all-reduce.3.cloned.1.call-update) | async-done | bytes 2228240 | tf_op jit(solution)/shard_map/psum | solution.py:25
  91.7 16.6 %convolution_convert_fusion.1 = bf16[256,7168]{1,0:T(8,128)(2,1)} fusion(bf16[2304,7168]{1,0:T(8,128)(2,1)} %param.8, bf16[2304,256]{1,0:T(8,128)(2,1)} %get-tuple-element.3, f32[2304]{0:T(1024)S(1)} %get-tuple-element.9), kind=kOutput, calls=%fused_computation.1 | convolution fusion | flops 8459321344 | bytes 37889024 | tf_op jit(solution)/shard_map/dot_general | solution.py:30
  108.3 0.0 copy-start
  108.3 0.0 reduce-scatter.2.cloned.1.call-update
  108.3 0.0 all-gather.2.cloned.1.call-start
  108.4 17.4 %psum.22 = f32[]{:T(128)} all-reduce(f32[]{:T(128)} %get-tuple-element.8), channel_id=1, replica_groups=mesh['dp'=8,'tensor'=4] {'dp'}, use_global_device_ids=true, to_apply=%region_3.0 | all-reduce | flops 1 | bytes 8 | tf_op jit(solution)/shard_map/psum | solution.py:33
  126.4 27.2 %reduce-scatter.2.cloned.1.call-done = bf16[32,7168]{1,0:T(8,128)(2,1)} async-done(((bf16[256,7168]{1,0:T(8,128)(2,1)}), bf16[32,7168]{1,0:T(8,128)(2,1)}) %reduce-scatter.2.cloned.1.call-update) | async-done | bytes 458768 | tf_op jit(solution)/shard_map/reduce_scatter | solution.py:34
  153.6 0.0 copy-done
  153.6 0.0 copy-done.1
  153.6 2.7 %divide_convert_fusion = (bf16[32,7168]{1,0:T(8,128)(2,1)}, f32[32,7168]{1,0:T(8,128)}, f32[32,7168]{1,0:T(8,128)}) fusion(f32[]{:T(128)S(6)} %div.26, bf16[32,7168]{1,0:T(8,128)(2,1)} %reduce-scatter.2.cloned.1.call-done, f32[32,7168]{1,0:T(8,128)S(1)} %copy-done, f32[32,7168]{1,0:T(8,128)S(1)} %copy-done.1), kind=kLoop, calls=%fused_computation.8 | loop fusion | flops 3211264 | bytes 4587524 | tf_op jit(solution)/shard_map/convert_element_type | solution.py:43
  156.4 0.0 all-gather.2.cloned.1.call-update
  156.4 41.0 %all-gather.2.cloned.1.call-done = bf16[256,7168]{1,0:T(8,128)(2,1)} async-done(((bf16[32,7168]{1,0:T(8,128)(2,1)}), bf16[256,7168]{1,0:T(8,128)(2,1)}) %all-gather.2.cloned.1.call-update) | async-done | bytes 3670032 | tf_op jit(solution)/shard_map/all_gather | solution.py:54
  197.4 0.0 copy-done.2
  197.4 9.6 %convolution_convert_fusion = bf16[1024,7168]{1,0:T(8,128)(2,1)} fusion(bf16[256,7168]{1,0:T(8,128)(2,1)} %all-gather.2.cloned.1.call-done, bf16[2048,256]{1,0:T(8,128)(2,1)S(1)} %copy-done.2, s32[]{:T(128)S(6)} %select_n.26), kind=kOutput, calls=%fused_computation | convolution fusion | flops 3765436416 | bytes 18874372 | tf_op jit(solution)/shard_map/dot_general | solution.py:52
  (2 shorter events, 0.0 us)
Async XLA Ops:
  7.2 84.5 %all-reduce.3.cloned.1.call-start = ((), (), s32[]{:S(2)}) async-start(), calls=%async_computation.3 | async-start | bytes 4456448 | tf_op jit(solution)/shard_map/psum | solution.py:25
  9.5 7.6 %copy-start.3 = (s32[2304]{0:T(1024)S(1)}, s32[2304]{0:T(1024)}, u32[]{:S(2)}) copy-start(s32[2304]{0:T(1024)} %param.12) | copy-start | bytes 27652
  9.5 7.7 %copy-start.4 = (s32[2304]{0:T(1024)S(1)}, s32[2304]{0:T(1024)}, u32[]{:S(2)}) copy-start(s32[2304]{0:T(1024)} %param.13) | copy-start | bytes 27652
  17.1 136.5 %reduce-scatter.2.cloned.1.call-start = ((), (), s32[]{:S(2)}) async-start(), calls=%async_computation.1 | async-start | bytes 4128768 | tf_op jit(solution)/shard_map/reduce_scatter | solution.py:34
  108.3 45.4 %copy-start = (f32[32,7168]{1,0:T(8,128)S(1)}, f32[32,7168]{1,0:T(8,128)}, u32[]{:S(2)}) copy-start(f32[32,7168]{1,0:T(8,128)} %param.11) | copy-start | bytes 2752516
  108.3 45.4 %copy-start.1 = (f32[32,7168]{1,0:T(8,128)S(1)}, f32[32,7168]{1,0:T(8,128)}, u32[]{:S(2)}) copy-start(f32[32,7168]{1,0:T(8,128)} %param.10) | copy-start | bytes 2752516
  108.3 89.1 %copy-start.2 = (bf16[2048,256]{1,0:T(8,128)(2,1)S(1)}, bf16[2048,256]{1,0:T(8,128)(2,1)}, u32[]{:S(2)}) copy-start(bf16[2048,256]{1,0:T(8,128)(2,1)} %get-tuple-element.4) | copy-start | bytes 3145732
  108.3 89.1 %all-gather.2.cloned.1.call-start = ((), (), s32[]{:S(2)}) async-start(), calls=%async_computation.2 | async-start | bytes 4128768 | tf_op jit(solution)/shard_map/all_gather | solution.py:54
Sparse Core Ops, SparseCore 0:
  17.2 74.3 all-reduce.2
  108.4 45.1 reduce-scatter.1
  156.5 40.8 all-gather.1
where the time goes:
time: 214 us
  waiting for transfers between devices  142 us (66%)
  matrix products  33.7 us (16%)
  blocking collectives  17.4 us (8%)
  between operations  14.5 us (7%)
  other arithmetic  5.65 us (3%)
    psum x1, waiting for transfers between devices, local(): lax.psum(partial_value.astype(jnp.bfloat16), 'tensor').astype(jnp.float32)  73.9 us
    all_gather x1, waiting for transfers between devices, local(): lax.all_gather(update, 'dp', axis=0, tiled=True)  41 us
    reduce_scatter x1, waiting for transfers between devices, local(): lax.psum_scatter(raw_grad.astype(jnp.bfloat16), 'dp', scatter_dimension=0...  27.2 us
    psum x1, blocking collectives, local(): normalizer = lax.psum(local_total, 'dp')  17.4 us
    dot_general x1, matrix products, local(): lax.dot_general(weighted, out_grads, (((0,), (0,)), ((), ())), preferred_...  16.6 us
    dot_general x1, matrix products, local(): jnp.dot(basis_rows, lax.all_gather(update, 'dp', axis=0, tiled=True), pre...  9.58 us
    dot_general x1, matrix products, local(): jnp.dot(activations, basis, preferred_element_type=jnp.float32)  7.57 us
  transfers between devices with their start and end apart: 3, of which 3 were waited for; matrix products, arithmetic and copies ran while one was open for 0% of the time, Pallas kernels for 0%

commit v1 on v0

--- a/solution.py
+++ b/solution.py
@@ -1,6 +1,10 @@
+import functools
+
 import jax
 import jax.numpy as jnp
 from jax import lax
+from jax.experimental import pallas as pl
+from jax.experimental.pallas import tpu as pltpu
 from jax.sharding import PartitionSpec as P
 
 ADAM_STEP = 100
@@ -12,13 +16,21 @@
 beta_two = 0.999
 adam_eps = 1e-08
 
+bias_one = 1.0 - beta_one**ADAM_STEP
+bias_two = 1.0 - beta_two**ADAM_STEP
+
+F32, BF16 = jnp.float32, jnp.bfloat16
+CORES = 2
+CHUNKS = (4, 4, 3, 3)
+MIB = 1 << 20
+
 
 def from_root(block, axis, owner):
     block = jnp.where(lax.axis_index(axis) == owner, block, jnp.zeros_like(block))
     return lax.psum(block, axis)
 
 
-def local(activations, out_grads, basis, first_moment, second_moment, reward_codes, token_ids):
+def local_general(activations, out_grads, basis, first_moment, second_moment, reward_codes, token_ids):
     data_count = lax.axis_size("dp")
     tensor_count = lax.axis_size("tensor")
     partial_value = jnp.dot(activations, basis, preferred_element_type=jnp.float32)
@@ -38,8 +50,6 @@
     gradient = grad_rows * (token_count / normalizer)
     new_first = beta_one * first_moment + (1.0 - beta_one) * gradient
     new_second = beta_two * second_moment + (1.0 - beta_two) * gradient * gradient
-    bias_one = 1.0 - beta_one**ADAM_STEP
-    bias_two = 1.0 - beta_two**ADAM_STEP
     update = (new_first / bias_one / (jnp.sqrt(new_second / bias_two) + adam_eps)).astype(
         jnp.bfloat16
     )
@@ -57,9 +67,356 @@
     return (new_first, new_second, summed.astype(jnp.bfloat16))
 
 
+def pick(value, width):
+    best = 128
+    for w in range(128, width + 1, 128):
+        if value % w == 0:
+            best = w
+    return best
+
+
+def params(limit_mib):
+    return pltpu.CompilerParams(
+        dimension_semantics=("arbitrary",), vmem_limit_bytes=limit_mib * MIB
+    )
+
+
+def project_kernel(slot_ref, basis_ref, act_ref, out_ref, turned):
+    rows = basis_ref.shape[1] // slot_ref.shape[0]
+
+    @pl.when(pl.program_id(0) == 0)
+    def _():
+        flipped = basis_ref[...].T
+        for n in range(slot_ref.shape[0]):
+            at = pl.multiple_of(slot_ref[n] * rows, rows)
+            turned[pl.ds(at, rows), :] = flipped[n * rows : (n + 1) * rows, :]
+
+    out_ref[...] = lax.dot_general(
+        turned[...], act_ref[...], (((1,), (1,)), ((), ())), preferred_element_type=F32
+    ).astype(out_ref.dtype)
+
+
+def project(slots, basis, activations, start, count):
+    depth, rank = basis.shape
+    block = pick(count, 384)
+    return pl.pallas_call(
+        project_kernel,
+        out_shape=jax.ShapeDtypeStruct((rank, count), BF16),
+        grid_spec=pltpu.PrefetchScalarGridSpec(
+            num_scalar_prefetch=1,
+            grid=(count // block,),
+            in_specs=[
+                pl.BlockSpec((depth, rank), lambda i, s: (0, 0)),
+                pl.BlockSpec((block, depth), lambda i, s: (start // block + i, 0)),
+            ],
+            out_specs=pl.BlockSpec((rank, block), lambda i, s: (0, i)),
+            scratch_shapes=[pltpu.VMEM((rank, depth), BF16)],
+        ),
+        compiler_params=params(20),
+        cost_estimate=pl.CostEstimate(
+            flops=2 * depth * rank * count,
+            bytes_accessed=2 * (depth * rank + depth * count + rank * count),
+            transcendentals=0,
+        ),
+        name="project",
+    )(slots, basis, activations)
+
+
+def gradient_kernel(left_a, left_b, grads_ref, keep_ref, give_ref):
+    half = left_a.shape[1]
+    total = jnp.dot(left_a[...], grads_ref[:half, :], preferred_element_type=F32)
+    total += jnp.dot(left_b[...], grads_ref[half:, :], preferred_element_type=F32)
+    rows = keep_ref.shape[0]
+    keep_ref[...] = total[:rows].astype(BF16)
+    give_ref[...] = total[rows:].astype(BF16)
+
+
+def gradient_chunk(left_a, left_b, out_grads, start, width):
+    rank, half = left_a.shape
+    tokens = out_grads.shape[0]
+    tile = pick(width, 512)
+    while start % tile:
+        tile -= 128
+    return pl.pallas_call(
+        gradient_kernel,
+        out_shape=[jax.ShapeDtypeStruct((rank // 2, width), BF16)] * 2,
+        grid=(width // tile,),
+        in_specs=[
+            pl.BlockSpec((rank, half), lambda i: (0, 0)),
+            pl.BlockSpec((rank, half), lambda i: (0, 0)),
+            pl.BlockSpec((tokens, tile), lambda i: (0, start // tile + i)),
+        ],
+        out_specs=[pl.BlockSpec((rank // 2, tile), lambda i: (0, i))] * 2,
+        compiler_params=params(20),
+        cost_estimate=pl.CostEstimate(
+            flops=2 * rank * tokens * width,
+            bytes_accessed=2 * (rank * tokens + tokens * width + rank * width),
+            transcendentals=0,
+        ),
+        name="gradient",
+    )(left_a, left_b, out_grads)
+
+
+def moments(gradient, first, second):
+    new_first = beta_one * first + (1.0 - beta_one) * gradient
+    new_second = beta_two * second + (1.0 - beta_two) * gradient * gradient
+    update = new_first / bias_one / (jnp.sqrt(new_second / bias_two) + adam_eps)
+    return new_first, new_second, update
+
+
+def hub_kernel(scale_ref, own_ref, outer_ref, far_ref, m_ref, v_ref, mv_ref, update_ref, sum_ref):
+    rows = m_ref.shape[0]
+    total = own_ref[...].astype(F32) + outer_ref[...].astype(F32) + far_ref[...].astype(F32)
+    sum_ref[...] = total[:rows].astype(BF16)
+    gradient = total * scale_ref[0, 0]
+    mv = mv_ref[...].astype(F32)
+    update_ref[:rows] = moments(gradient[:rows], mv[:rows], mv[rows:])[2].astype(BF16)
+    update_ref[rows:] = moments(gradient[rows:], m_ref[...], v_ref[...])[2].astype(BF16)
+
+
+def hub_chunk(scale, own, outer, far, first, second, moved, start):
+    rows = first.shape[0]
+    width = own.shape[1]
+    tile = pick(width, 1024)
+    while start % tile:
+        tile -= 128
+    there = lambda i: (0, i)
+    shifted = lambda i: (0, start // tile + i)
+    two = pl.BlockSpec((2 * rows, tile), there)
+    return pl.pallas_call(
+        hub_kernel,
+        out_shape=[
+            jax.ShapeDtypeStruct((2 * rows, width), BF16),
+            jax.ShapeDtypeStruct((rows, width), BF16),
+        ],
+        grid=(width // tile,),
+        in_specs=[
+            pl.BlockSpec(memory_space=pltpu.SMEM),
+            two,
+            two,
+            two,
+            pl.BlockSpec((rows, tile), shifted),
+            pl.BlockSpec((rows, tile), shifted),
+            pl.BlockSpec((2 * rows, tile), shifted),
+        ],
+        out_specs=[two, pl.BlockSpec((rows, tile), there)],
+        compiler_params=params(8),
+        cost_estimate=pl.CostEstimate(
+            flops=40 * rows * width * 100, bytes_accessed=30 * rows * width, transcendentals=0
+        ),
+        name="hub",
+    )(scale, own, outer, far, first, second, moved)
+
+
+def settle_kernel(
+    scale_ref, hub_ref, own_ref, outer_ref, far_ref, m_ref, v_ref, near_ref, across_ref, sent_ref, *rest
+):
+    all_ref, first_ref, second_ref = rest[-3:]
+    rows = m_ref.shape[0]
+    hub = hub_ref[0, 0] == 1
+    total = own_ref[...].astype(F32) + outer_ref[...].astype(F32) + far_ref[...].astype(F32)
+    total = jnp.where(hub, total, sent_ref[:rows].astype(F32))
+    new_first, new_second, update = moments(total * scale_ref[0, 0], m_ref[...], v_ref[...])
+    first_ref[...] = new_first
+    second_ref[...] = new_second
+    all_ref[:rows] = jnp.where(hub, near_ref[:rows], update.astype(BF16))
+    all_ref[rows : 2 * rows] = jnp.where(hub, update.astype(BF16), sent_ref[rows : 2 * rows])
+    all_ref[2 * rows :] = jnp.where(hub, across_ref[...], sent_ref[2 * rows :])
+
+
+def settle_chunk(scale, hub, own, outer, far, first, second, near, across, sent, start, results):
+    rows, full = first.shape
+    width = own.shape[1]
+    tile = pick(width, 1024)
+    while start % tile:
+        tile -= 128
+    there = lambda i: (0, i)
+    second_rows = lambda i: (1, i)
+    shifted = lambda i: (0, start // tile + i)
+    one = pl.BlockSpec((rows, tile), second_rows)
+    moment = pl.BlockSpec((rows, tile), shifted)
+    smem = pl.BlockSpec(memory_space=pltpu.SMEM)
+    whole = [pl.BlockSpec(memory_space=pl.ANY)] * len(results)
+    return pl.pallas_call(
+        settle_kernel,
+        out_shape=[
+            jax.ShapeDtypeStruct((4 * rows, width), BF16),
+            jax.ShapeDtypeStruct((rows, full), F32),
+            jax.ShapeDtypeStruct((rows, full), F32),
+        ],
+        grid=(width // tile,),
+        in_specs=[
+            smem,
+            smem,
+            one,
+            one,
+            one,
+            moment,
+            moment,
+            pl.BlockSpec((2 * rows, tile), there),
+            pl.BlockSpec((2 * rows, tile), there),
+            pl.BlockSpec((4 * rows, tile), there),
+            *whole,
+        ],
+        out_specs=[pl.BlockSpec((4 * rows, tile), there), moment, moment],
+        input_output_aliases={10: 1, 11: 2} if results else {},
+        compiler_params=params(8),
+        cost_estimate=pl.CostEstimate(
+            flops=30 * rows * width * 100, bytes_accessed=40 * rows * width, transcendentals=0
+        ),
+        name="settle",
+    )(scale, hub, own, outer, far, first, second, near, across, sent, *results)
+
+
+def spread_kernel(slot_ref, basis_ref, mine_ref, other_ref, *rest):
+    out_ref, updates = rest[-2:]
+    blocks = slot_ref.shape[0]
+    rows = 2 * mine_ref.shape[0] // blocks
+    side = blocks // 2
+    for n in range(blocks):
+        at = slot_ref[n]
+        inner = pl.multiple_of((at % side) * rows, rows)
+        updates[n * rows : (n + 1) * rows, :] = jnp.where(
+            at < side, mine_ref[pl.ds(inner, rows), :], other_ref[pl.ds(inner, rows), :]
+        )
+    out_ref[...] = jnp.dot(
+        basis_ref[...], updates[...], preferred_element_type=F32
+    ).astype(BF16)
+
+
+def spread_chunk(slots, basis_rows, mine, other, start, full, results):
+    count, rank = basis_rows.shape
+    width = mine.shape[1]
+    tile = pick(width, 512)
+    while start % tile:
+        tile -= 128
+    there = lambda i, s: (0, i)
+    return pl.pallas_call(
+        spread_kernel,
+        out_shape=jax.ShapeDtypeStruct((count, full), BF16),
+        grid_spec=pltpu.PrefetchScalarGridSpec(
+            num_scalar_prefetch=1,
+            grid=(width // tile,),
+            in_specs=[
+                pl.BlockSpec((count, rank), lambda i, s: (0, 0)),
+                pl.BlockSpec((rank // 2, tile), there),
+                pl.BlockSpec((rank // 2, tile), there),
+                *([pl.BlockSpec(memory_space=pl.ANY)] * len(results)),
+            ],
+            out_specs=pl.BlockSpec((count, tile), lambda i, s: (0, start // tile + i)),
+            scratch_shapes=[pltpu.VMEM((rank, tile), BF16)],
+        ),
+        input_output_aliases={4: 0} if results else {},
+        compiler_params=params(12),
+        cost_estimate=pl.CostEstimate(
+            flops=2 * count * rank * width,
+            bytes_accessed=2 * (count * rank + rank * width + count * width),
+            transcendentals=0,
+        ),
+        name="spread",
+    )(slots, basis_rows, mine, other, *results)
+
+
+def doubling(part, bits):
+    count = lax.axis_size("tensor")
+    for step, bit in enumerate(bits):
+        got = lax.ppermute(part, "tensor", [(t, t ^ bit) for t in range(count)])
+        if step == len(bits) - 1:
+            return part, got
+        part = (part.astype(F32) + got.astype(F32)).astype(BF16)
+
+
+def local_line(activations, out_grads, basis, first_moment, second_moment, reward_codes, token_ids):
+    data_count = lax.axis_size("dp")
+    tensor_count = lax.axis_size("tensor")
+    data_index = lax.axis_index("dp")
+    tensor_index = lax.axis_index("tensor")
+    chips = data_count // CORES
+    chip, core = data_index // CORES, data_index % CORES
+    tokens = activations.shape[0]
+    full = out_grads.shape[1]
+    rows = first_moment.shape[0]
+
+    def on_chips(pairs):
+        return [(a * CORES + c, b * CORES + c) for a, b in pairs for c in range(CORES)]
+
+    inward = on_chips([(0, 1), (3, 2)])
+    outward = on_chips([(1, 0), (2, 3)])
+    middle = on_chips([(1, 2), (2, 1)])
+    sibling = [(i, i ^ 1) for i in range(data_count)]
+    hub = ((chip == 1) | (chip == 2)).astype(jnp.int32).reshape(1, 1)
+
+    block = jnp.arange(data_count, dtype=jnp.int32)
+    block_chip = block // CORES
+    far = (block_chip // 2 != chip // 2).astype(jnp.int32)
+    is_hub = ((block_chip == 1) | (block_chip == 2)).astype(jnp.int32)
+    slots = ((block % CORES) ^ core).astype(jnp.int32) * chips + 2 * far + is_hub
+
+    bits = [1 << b for b in range(tensor_count.bit_length() - 1)]
+    half = tokens // 2
+    part_a = project(slots, basis, activations, 0, half)
+    part_b = project(slots, basis, activations, half, half)
+    sum_a, got_a = doubling(part_a, bits)
+    sum_b, got_b = doubling(part_b, bits[::-1])
+
+    unmasked = (token_ids != pad_token).astype(F32)
+    weights = unmasked * jnp.exp(reward_temp * reward_codes.astype(F32))
+    normalizer = jnp.full((8, 128), jnp.sum(weights), F32)
+    for b in range(data_count.bit_length() - 1):
+        normalizer = normalizer + lax.ppermute(
+            normalizer, "dp", [(i, i ^ (1 << b)) for i in range(data_count)]
+        )
+    scale = (tokens * data_count) / normalizer[:1, :1]
+
+    left_a = (weights[None, :half] * (sum_a.astype(F32) + got_a.astype(F32))).astype(BF16)
+    left_b = (weights[None, half:] * (sum_b.astype(F32) + got_b.astype(F32))).astype(BF16)
+
+    moved = lax.ppermute(
+        jnp.concatenate([first_moment, second_moment]).astype(BF16), "dp", inward
+    )
+
+    row_count = basis.shape[0] * tensor_count // data_count
+    per_owner = data_count // tensor_count
+    owner = data_index // per_owner
+    basis_rows = lax.dynamic_slice_in_dim(basis, data_index % per_owner * row_count, row_count, 0)
+    basis_rows = jnp.where(tensor_index == owner, basis_rows, jnp.zeros_like(basis_rows))
+
+    unit = full // sum(CHUNKS)
+    starts = [unit * sum(CHUNKS[:i]) for i in range(len(CHUNKS))]
+    own, outer = [], []
+    for start, parts in zip(starts, CHUNKS):
+        keep, give = gradient_chunk(left_a, left_b, out_grads, start, unit * parts)
+        own.append(keep + lax.ppermute(give, "dp", sibling))
+        outer.append(lax.ppermute(own[-1], "dp", inward))
+
+    for bit in bits:
+        pairs = [
+            (d * tensor_count + (d // per_owner ^ s), d * tensor_count + (d // per_owner ^ s ^ bit))
+            for d in range(data_count)
+            for s in range(bit)
+        ]
+        basis_rows = basis_rows + lax.ppermute(basis_rows, ("dp", "tensor"), pairs)
+
+    settled, spread = (), ()
+    for start, mine, came in zip(starts, own, outer):
+        across = lax.ppermute(mine[2 * rows :] + came[2 * rows :], "dp", middle)
+        near, total = hub_chunk(scale, mine, came, across, first_moment, second_moment, moved, start)
+        beyond = lax.ppermute(near, "dp", middle)
+        sent = lax.ppermute(jnp.concatenate([total, near[rows:], beyond]), "dp", outward)
+        updates, *settled = settle_chunk(
+            scale, hub, mine, came, across, first_moment, second_moment, near, beyond, sent, start, settled
+        )
+        other = lax.ppermute(updates, "dp", sibling)
+        spread = (spread_chunk(slots, basis_rows, updates, other, start, full, spread),)
+    return (*settled, *spread)
+
+
 def solution(mesh):
+    data_count, tensor_count = mesh.shape["dp"], mesh.shape["tensor"]
+    line = data_count == 4 * CORES and tensor_count > 1 and tensor_count & (tensor_count - 1) == 0
+    line = line and data_count % tensor_count == 0
     return jax.shard_map(
-        local,
+        local_line if line else local_general,
         mesh=mesh,
         in_specs=(
             P("dp", "tensor"),

time: 214 us -> 222 us (1.037)
  Pallas kernels: 0 us -> 49.2 us
  waiting for transfers between devices: 142 us -> 97.1 us
  starting transfers between devices: 0.12 us -> 42.7 us
  matrix products: 33.7 us -> 0 us
  local copies, waits for them, and re-layouts: 0.02 us -> 18.1 us
  blocking collectives: 17.4 us -> 0 us
  between operations: 14.5 us -> 1.94 us
  other arithmetic: 5.65 us -> 11.8 us
    ppermute x0 -> x34, waiting for transfers between devices: none -> 97.1 us  [the longest x4 39.2 us: local_line(): lax.ppermute(jnp.concatenate([total, near[rows:], beyond]), 'dp', outward)]
    psum x1 -> x0, waiting for transfers between devices: 73.9 us -> none  [local(): lax.psum(partial_value.astype(jnp.bfloat16), 'tensor').astype(jnp.float32)]
    pallas_call x0 -> x18, Pallas kernels: none -> 49.2 us  [the longest x4 15.7 us: gradient_chunk(): pl.pallas_call(gradient_kernel, out_shape=[jax.ShapeDtypeStruct((rank //...]
    ppermute x0 -> x34, starting transfers between devices: none -> 42.7 us  [the longest x4 12.6 us: local_line(): outer.append(lax.ppermute(own[-1], 'dp', inward))]
    all_gather x1 -> x0, waiting for transfers between devices: 41 us -> none  [local(): lax.all_gather(update, 'dp', axis=0, tiled=True)]
    dot_general x3 -> x0, matrix products: 33.7 us -> none  [the longest x1 16.6 us: local(): lax.dot_general(weighted, out_grads, (((0,), (0,)), ((), ())), preferred_...]
    reduce_scatter x1 -> x0, waiting for transfers between devices: 27.2 us -> none  [local(): lax.psum_scatter(raw_grad.astype(jnp.bfloat16), 'dp', scatter_dimension=0...]
    psum x1 -> x0, blocking collectives: 17.4 us -> none  [local(): normalizer = lax.psum(local_total, 'dp')]
  transfers between devices with their start and end apart: 3 -> 34, of which waited for: 3 -> 9; matrix products, arithmetic and copies ran while one was open for 0% -> 6% of each run, Pallas kernels for 0% -> 19%
where the time goes in v1:
time: 222 us; the launch traced here: 221 us
  waiting for transfers between devices  97.1 us (44%)
  Pallas kernels  49.2 us (22%)
  starting transfers between devices  42.7 us (19%)
  local copies, waits for them, and re-layouts  18.1 us (8%)
  other arithmetic  11.8 us (5%)
    ppermute x4, waiting for transfers between devices, local_line(): lax.ppermute(jnp.concatenate([total, near[rows:], beyond]), 'dp', outward)  39.2 us
    ppermute x4, waiting for transfers between devices, local_line(): outer.append(lax.ppermute(own[-1], 'dp', inward))  33.8 us
    ppermute x4, waiting for transfers between devices, doubling(): got = lax.ppermute(part, 'tensor', [(t, t ^ bit) for t in range(count)])  24 us
    unnamed x24, local copies, waits for them, and re-layouts  16.9 us
    pallas_call x4, Pallas kernels, gradient_chunk(): pl.pallas_call(gradient_kernel, out_shape=[jax.ShapeDtypeStruct((rank //...  15.7 us
    pallas_call x4, Pallas kernels, spread_chunk(): pl.pallas_call(spread_kernel, out_shape=jax.ShapeDtypeStruct((count, full...  14.8 us
    ppermute x4, starting transfers between devices, local_line(): outer.append(lax.ppermute(own[-1], 'dp', inward))  12.6 us
    pallas_call x4, Pallas kernels, settle_chunk(): pl.pallas_call(settle_kernel, out_shape=[jax.ShapeDtypeStruct((4 * rows,...  7.32 us
  transfers between devices with their start and end apart: 34, of which 9 were waited for; matrix products, arithmetic and copies ran while one was open for 6% of the time, Pallas kernels for 19%

profile of v1, /device:TPU:0, one launch (start us, length us, event | category | flops | bytes accessed | tf_op | source)
XLA Modules:
  0.0 220.7 jit_solution(7289478084295747128)
XLA Ops:
  0.7 3.7 %copy-done.3 = bf16[2304,2048]{1,0:T(8,128)(2,1)S(1)} copy-done((bf16[2304,2048]{1,0:T(8,128)(2,1)S(1)}, bf16[2304,2048]{1,0:T(8,128)(2,1)}, u32[]{:S(2)}) %copy-start.3) | copy-done | bytes 9437208
  5.6 3.2 %project.2 = bf16[256,1152]{1,0:T(8,128)(2,1)S(1)} custom-call(s32[8]{0:T(128)S(1)} %fusion.slot_ref, bf16[2048,256]{1,0:T(8,128)(2,1)S(1)} %copy-done.4, bf16[2304,2048]{1,0:T(8,128)(2,1)S(1)} %copy-done.3), custom_call_target="tpu_custom_call" | custom-call | flops 1207959552 | bytes 6356992 | tf_op jit(solution)/shard_map/project/pallas_call | solution.py:102
  8.8 3.0 %collective-permute-start.3 = (bf16[256,1152]{1,0:T(8,128)(2,1)S(1)}, bf16[256,1152]{1,0:T(8,128)(2,1)S(1)}, u32[]{:S(2)}, u32[]{:S(2)}) collective-permute-start(bf16[256,1152]{1,0:T(8,128)(2,1)S(1)} %project.2), channel_id=1, source_target_pairs={{0,1},{1,0},{2,3},{3,2},{4,5},{5,4},{6,7},{7,6},{8,9},{9,8},{10,11... | collective-permute-start | bytes 1769480 | tf_op jit(solution)/shard_map/ppermute | solution.py:323
  13.3 3.2 %project.3 = bf16[256,1152]{1,0:T(8,128)(2,1)S(1)} custom-call(s32[8]{0:T(128)S(1)} %fusion.slot_ref, bf16[2048,256]{1,0:T(8,128)(2,1)S(1)} %copy-done.4, bf16[2304,2048]{1,0:T(8,128)(2,1)S(1)} %copy-done.3), custom_call_target="tpu_custom_call" | custom-call | flops 1207959552 | bytes 6356992 | tf_op jit(solution)/shard_map/project/pallas_call | solution.py:102
  18.2 7.0 %collective-permute-done.3 = bf16[256,1152]{1,0:T(8,128)(2,1)S(1)} collective-permute-done((bf16[256,1152]{1,0:T(8,128)(2,1)S(1)}, bf16[256,1152]{1,0:T(8,128)(2,1)S(1)}, u32[]{:S(2)}, u32[]{:S(2)}) %collective-permute-start.3) | collective-permute-done | bytes 589856 | tf_op jit(solution)/shard_map/ppermute | solution.py:323
  27.2 5.6 %collective-permute-done.5 = bf16[256,1152]{1,0:T(8,128)(2,1)S(1)} collective-permute-done((bf16[256,1152]{1,0:T(8,128)(2,1)S(1)}, bf16[256,1152]{1,0:T(8,128)(2,1)S(1)}, u32[]{:S(2)}, u32[]{:S(2)}) %collective-permute-start.5) | collective-permute-done | bytes 589856 | tf_op jit(solution)/shard_map/ppermute | solution.py:323
  35.8 9.1 %collective-permute-done.4 = bf16[256,1152]{1,0:T(8,128)(2,1)S(1)} collective-permute-done((bf16[256,1152]{1,0:T(8,128)(2,1)S(1)}, bf16[256,1152]{1,0:T(8,128)(2,1)S(1)}, u32[]{:S(2)}, u32[]{:S(2)}) %collective-permute-start.4) | collective-permute-done | bytes 589856 | tf_op jit(solution)/shard_map/ppermute | solution.py:323
  47.6 10.4 %copy-done = bf16[2304,7168]{1,0:T(8,128)(2,1)S(1)} copy-done((bf16[2304,7168]{1,0:T(8,128)(2,1)S(1)}, bf16[2304,7168]{1,0:T(8,128)(2,1)}, u32[]{:S(2)}) %copy-start) | copy-done | bytes 33030168
  58.0 3.1 %gradient.5 = (bf16[128,1536]{1,0:T(8,128)(2,1)S(1)}, bf16[128,1536]{1,0:T(8,128)(2,1)S(1)}) custom-call(bf16[256,1152]{1,0:T(8,128)(2,1)S(1)} %multiply_convert_fusion.1.left_a, bf16[256,1152]{1,0:T(8,128)(2,1)S(1)} %multiply_convert_fusion.left_b, bf16[2304,7168]{1,0:T(8,128)(2,1)S(1)} %copy-done), custom_call_target="tpu_custom_call" | custom-call | flops 1811939328 | bytes 9043968 | tf_op jit(solution)/shard_map/gradient/pallas_call | solution.py:140
  61.1 3.7 %gradient.4 = (bf16[128,1536]{1,0:T(8,128)(2,1)S(1)}, bf16[128,1536]{1,0:T(8,128)(2,1)}) custom-call(bf16[256,1152]{1,0:T(8,128)(2,1)S(1)} %multiply_convert_fusion.1.left_a, bf16[256,1152]{1,0:T(8,128)(2,1)S(1)} %multiply_convert_fusion.left_b, bf16[2304,7168]{1,0:T(8,128)(2,1)S(1)} %copy-done), custom_call_target="tpu_custom_call" | custom-call | flops 1811939328 | bytes 9043968 | tf_op jit(solution)/shard_map/gradient/pallas_call | solution.py:140
  66.1 4.1 %gradient.7 = (bf16[128,2048]{1,0:T(8,128)(2,1)S(1)}, bf16[128,2048]{1,0:T(8,128)(2,1)S(1)}) custom-call(bf16[256,1152]{1,0:T(8,128)(2,1)S(1)} %multiply_convert_fusion.1.left_a, bf16[256,1152]{1,0:T(8,128)(2,1)S(1)} %multiply_convert_fusion.left_b, bf16[2304,7168]{1,0:T(8,128)(2,1)S(1)} %copy-done), custom_call_target="tpu_custom_call" | custom-call | flops 2415919104 | bytes 11665408 | tf_op jit(solution)/shard_map/gradient/pallas_call | solution.py:140
  71.0 4.7 %gradient.6 = (bf16[128,2048]{1,0:T(8,128)(2,1)S(1)}, bf16[128,2048]{1,0:T(8,128)(2,1)}) custom-call(bf16[256,1152]{1,0:T(8,128)(2,1)S(1)} %multiply_convert_fusion.1.left_a, bf16[256,1152]{1,0:T(8,128)(2,1)S(1)} %multiply_convert_fusion.left_b, bf16[2304,7168]{1,0:T(8,128)(2,1)S(1)} %copy-done), custom_call_target="tpu_custom_call" | custom-call | flops 2415919104 | bytes 11665408 | tf_op jit(solution)/shard_map/gradient/pallas_call | solution.py:140
  77.1 4.2 %collective-permute-start.14 = (bf16[128,1536]{1,0:T(8,128)(2,1)}, bf16[128,1536]{1,0:T(8,128)(2,1)}, u32[]{:S(2)}, u32[]{:S(2)}) collective-permute-start(bf16[128,1536]{1,0:T(8,128)(2,1)} %add.88.own_ref), channel_id=1, source_target_pairs={{0,8},{4,12},{24,16},{28,20},{1,9},{5,13},{25,17},{29,21},{2,10},{... | collective-permute-start | bytes 1179656 | tf_op jit(solution)/shard_map/ppermute | solution.py:390
  84.5 5.7 %collective-permute-start.24 = (bf16[128,2048]{1,0:T(8,128)(2,1)S(1)}, bf16[128,2048]{1,0:T(8,128)(2,1)}, u32[]{:S(2)}, u32[]{:S(2)}) collective-permute-start(bf16[128,2048]{1,0:T(8,128)(2,1)S(1)} %add.92.own_ref), channel_id=1, source_target_pairs={{0,8},{4,12},{24,16},{28,20},{1,9},{5,13},{25,17},{29,21},{2,10},{... | collective-permute-start | bytes 1572872 | tf_op jit(solution)/shard_map/ppermute | solution.py:390
  95.0 3.4 %collective-permute-start.10 = (bf16[64,7168]{1,0:T(8,128)(2,1)}, bf16[64,7168]{1,0:T(8,128)(2,1)S(1)}, u32[]{:S(2)}, u32[]{:S(2)}) collective-permute-start(bf16[64,7168]{1,0:T(8,128)(2,1)} %pad_maximum_fusion), channel_id=1, source_target_pairs={{0,8},{4,12},{24,16},{28,20},{1,9},{5,13},{25,17},{29,21},{2,10},{... | collective-permute-start | bytes 2752520 | tf_op jit(solution)/shard_map/ppermute | solution.py:374
  106.2 33.8 %collective-permute-done.19.outer_ref = bf16[128,2048]{1,0:T(8,128)(2,1)S(1)} collective-permute-done((bf16[128,2048]{1,0:T(8,128)(2,1)S(1)}, bf16[128,2048]{1,0:T(8,128)(2,1)S(1)}, u32[]{:S(2)}, u32[]{:S(2)}) %collective-permute-start.19) | collective-permute-done | bytes 524320 | tf_op jit(solution)/shard_map/ppermute | solution.py:390
  147.4 3.5 %collective-permute-start.29 = (bf16[1024,256]{1,0:T(8,128)(2,1)S(1)}, bf16[1024,256]{1,0:T(8,128)(2,1)S(1)}, u32[]{:S(2)}, u32[]{:S(2)}) collective-permute-start(bf16[1024,256]{1,0:T(8,128)(2,1)S(1)} %fusion.6), channel_id=1, source_target_pairs={{0,2},{1,3},{4,6},{5,7},{9,11},{8,10},{13,15},{12,14},{18,16},{19,... | collective-permute-start | bytes 1572872 | tf_op jit(solution)/shard_map/ppermute | solution.py:398
  157.7 16.9 %collective-permute-done.27.sent_ref = bf16[128,2048]{1,0:T(8,128)(2,1)S(1)} collective-permute-done((bf16[128,2048]{1,0:T(8,128)(2,1)S(1)}, bf16[128,2048]{1,0:T(8,128)(2,1)S(1)}, u32[]{:S(2)}, u32[]{:S(2)}) %collective-permute-start.27) | collective-permute-done | bytes 524320 | tf_op jit(solution)/shard_map/ppermute | solution.py:405
  178.1 15.8 %collective-permute-done.22.sent_ref = bf16[128,2048]{1,0:T(8,128)(2,1)S(1)} collective-permute-done((bf16[128,2048]{1,0:T(8,128)(2,1)S(1)}, bf16[128,2048]{1,0:T(8,128)(2,1)S(1)}, u32[]{:S(2)}, u32[]{:S(2)}) %collective-permute-start.22) | collective-permute-done | bytes 524320 | tf_op jit(solution)/shard_map/ppermute | solution.py:405
  195.3 4.7 %collective-permute-done.17.sent_ref = bf16[128,1536]{1,0:T(8,128)(2,1)S(1)} collective-permute-done((bf16[128,1536]{1,0:T(8,128)(2,1)S(1)}, bf16[128,1536]{1,0:T(8,128)(2,1)S(1)}, u32[]{:S(2)}, u32[]{:S(2)}) %collective-permute-start.17) | collective-permute-done | bytes 393248 | tf_op jit(solution)/shard_map/ppermute | solution.py:405
  205.9 3.9 %spread.4.rest_0_ = bf16[1024,7168]{1,0:T(8,128)(2,1)} custom-call(s32[8]{0:T(128)S(1)} %fusion.slot_ref, bf16[1024,256]{1,0:T(8,128)(2,1)S(1)} %add.96.basis_ref, bf16[128,2048]{1,0:T(8,128)(2,1)S(1)} %get-tuple-element.58.mine_ref, bf16[128,2048]{1,0:T(8,128)(2,1)S(1)} %collective-permute-done.33.other_ref), custom_call_target="tpu_custom_call" | custom-call | flops 1073741824 | bytes 5767168 | tf_op jit(solution)/shard_map/spread/pallas_call | solution.py:294
  209.9 3.9 %spread.5.rest_0_ = bf16[1024,7168]{1,0:T(8,128)(2,1)} custom-call(s32[8]{0:T(128)S(1)} %fusion.slot_ref, bf16[1024,256]{1,0:T(8,128)(2,1)S(1)} %add.96.basis_ref, bf16[128,2048]{1,0:T(8,128)(2,1)S(1)} %get-tuple-element.57.mine_ref, bf16[128,2048]{1,0:T(8,128)(2,1)S(1)} %collective-permute-done.32.other_ref, ...), custom_call_target="tpu_custom_call", output_to_operand_aliasing={{}: (4, {})} | custom-call | flops 1073741824 | bytes 5767168 | tf_op jit(solution)/shard_map/spread/pallas_call | solution.py:294
  213.8 3.5 %spread.6.rest_0_ = bf16[1024,7168]{1,0:T(8,128)(2,1)} custom-call(s32[8]{0:T(128)S(1)} %fusion.slot_ref, bf16[1024,256]{1,0:T(8,128)(2,1)S(1)} %add.96.basis_ref, bf16[128,1536]{1,0:T(8,128)(2,1)S(1)} %get-tuple-element.56.mine_ref, bf16[128,1536]{1,0:T(8,128)(2,1)S(1)} %collective-permute-done.31.other_ref, ...), custom_call_target="tpu_custom_call", output_to_operand_aliasing={{}: (4, {})} | custom-call | flops 805306368 | bytes 4456448 | tf_op jit(solution)/shard_map/spread/pallas_call | solution.py:294
  217.3 3.4 %spread.7 = bf16[1024,7168]{1,0:T(8,128)(2,1)} custom-call(s32[8]{0:T(128)S(1)} %fusion.slot_ref, bf16[1024,256]{1,0:T(8,128)(2,1)S(1)} %add.96.basis_ref, bf16[128,1536]{1,0:T(8,128)(2,1)S(1)} %get-tuple-element.55.mine_ref, bf16[128,1536]{1,0:T(8,128)(2,1)S(1)} %collective-permute-done.30.other_ref, ...), custom_call_target="tpu_custom_call", output_to_operand_aliasing={{}: (4, {})} | custom-call | flops 805306368 | bytes 4456448 | tf_op jit(solution)/shard_map/spread/pallas_call | solution.py:294
  (120 shorter events, 54.9 us)
Async XLA Ops:
  8.8 16.4 %collective-permute-start.3 = (bf16[256,1152]{1,0:T(8,128)(2,1)S(1)}, bf16[256,1152]{1,0:T(8,128)(2,1)S(1)}, u32[]{:S(2)}, u32[]{:S(2)}) collective-permute-start(bf16[256,1152]{1,0:T(8,128)(2,1)S(1)} %project.2), channel_id=1, source_target_pairs={{0,1},{1,0},{2,3},{3,2},{4,5},{5,4},{6,7},{7,6},{8,9},{9,8},{10,11... | collective-permute-start | bytes 1769480 | tf_op jit(solution)/shard_map/ppermute | solution.py:323
  13.2 19.9 %collective-permute-start = (f32[8,128]{1,0:T(8,128)S(1)}, f32[8,128]{1,0:T(8,128)S(1)}, u32[]{:S(2)}, u32[]{:S(2)}) collective-permute-start(f32[8,128]{1,0:T(8,128)S(1)} %broadcast_in_dim.8), channel_id=1, source_target_pairs={{0,4},{4,0},{8,12},{12,8},{16,20},{20,16},{24,28},{28,24},{1,5},{5... | collective-permute-start | bytes 12296 | tf_op jit(solution)/shard_map/ppermute | solution.py:366
  16.5 16.3 %collective-permute-start.5 = (bf16[256,1152]{1,0:T(8,128)(2,1)S(1)}, bf16[256,1152]{1,0:T(8,128)(2,1)S(1)}, u32[]{:S(2)}, u32[]{:S(2)}) collective-permute-start(bf16[256,1152]{1,0:T(8,128)(2,1)S(1)} %project.3), channel_id=1, source_target_pairs={{0,2},{1,3},{2,0},{3,1},{4,6},{5,7},{6,4},{7,5},{8,10},{9,11},{10,... | collective-permute-start | bytes 1769480 | tf_op jit(solution)/shard_map/ppermute | solution.py:323
  25.4 19.6 %collective-permute-start.4 = (bf16[256,1152]{1,0:T(8,128)(2,1)S(1)}, bf16[256,1152]{1,0:T(8,128)(2,1)S(1)}, u32[]{:S(2)}, u32[]{:S(2)}) collective-permute-start(bf16[256,1152]{1,0:T(8,128)(2,1)S(1)} %add_convert_fusion.1), channel_id=1, source_target_pairs={{0,2},{1,3},{2,0},{3,1},{4,6},{5,7},{6,4},{7,5},{8,10},{9,11},{10,... | collective-permute-start | bytes 1769480 | tf_op jit(solution)/shard_map/ppermute | solution.py:323
  32.9 14.5 %collective-permute-start.6 = (bf16[256,1152]{1,0:T(8,128)(2,1)S(1)}, bf16[256,1152]{1,0:T(8,128)(2,1)S(1)}, u32[]{:S(2)}, u32[]{:S(2)}) collective-permute-start(bf16[256,1152]{1,0:T(8,128)(2,1)S(1)} %add_convert_fusion), channel_id=1, source_target_pairs={{0,1},{1,0},{2,3},{3,2},{4,5},{5,4},{6,7},{7,6},{8,9},{9,8},{10,11... | collective-permute-start | bytes 1769480 | tf_op jit(solution)/shard_map/ppermute | solution.py:323
  33.7 48.7 %collective-permute-start.1 = (f32[8,128]{1,0:T(8,128)S(1)}, f32[8,128]{1,0:T(8,128)S(1)}, u32[]{:S(2)}, u32[]{:S(2)}) collective-permute-start(f32[8,128]{1,0:T(8,128)S(1)} %broadcast_add_fusion), channel_id=1, source_target_pairs={{0,8},{4,12},{8,0},{12,4},{16,24},{20,28},{24,16},{28,20},{1,9},{5... | collective-permute-start | bytes 12296 | tf_op jit(solution)/shard_map/ppermute | solution.py:366
  65.6 29.3 %collective-permute-start.7 = (bf16[128,1536]{1,0:T(8,128)(2,1)}, bf16[128,1536]{1,0:T(8,128)(2,1)}, u32[]{:S(2)}, u32[]{:S(2)}) collective-permute-start(bf16[128,1536]{1,0:T(8,128)(2,1)} %get-tuple-element.32), channel_id=1, source_target_pairs={{0,4},{4,0},{8,12},{12,8},{16,20},{20,16},{24,28},{28,24},{1,5},{5... | collective-permute-start | bytes 1179656 | tf_op jit(solution)/shard_map/ppermute | solution.py:389
  71.0 12.1 %collective-permute-start.23 = (bf16[128,2048]{1,0:T(8,128)(2,1)S(1)}, bf16[128,2048]{1,0:T(8,128)(2,1)}, u32[]{:S(2)}, u32[]{:S(2)}) collective-permute-start(bf16[128,2048]{1,0:T(8,128)(2,1)S(1)} %get-tuple-element.44), channel_id=1, source_target_pairs={{0,4},{4,0},{8,12},{12,8},{16,20},{20,16},{24,28},{28,24},{1,5},{5... | collective-permute-start | bytes 1572872 | tf_op jit(solution)/shard_map/ppermute | solution.py:389
  75.8 23.8 %collective-permute-start.18 = (bf16[128,2048]{1,0:T(8,128)(2,1)}, bf16[128,2048]{1,0:T(8,128)(2,1)}, u32[]{:S(2)}, u32[]{:S(2)}) collective-permute-start(bf16[128,2048]{1,0:T(8,128)(2,1)} %get-tuple-element.40), channel_id=1, source_target_pairs={{0,4},{4,0},{8,12},{12,8},{16,20},{20,16},{24,28},{28,24},{1,5},{5... | collective-permute-start | bytes 1572872 | tf_op jit(solution)/shard_map/ppermute | solution.py:389
  77.1 25.0 %collective-permute-start.14 = (bf16[128,1536]{1,0:T(8,128)(2,1)}, bf16[128,1536]{1,0:T(8,128)(2,1)}, u32[]{:S(2)}, u32[]{:S(2)}) collective-permute-start(bf16[128,1536]{1,0:T(8,128)(2,1)} %add.88.own_ref), channel_id=1, source_target_pairs={{0,8},{4,12},{24,16},{28,20},{1,9},{5,13},{25,17},{29,21},{2,10},{... | collective-permute-start | bytes 1179656 | tf_op jit(solution)/shard_map/ppermute | solution.py:390
  84.5 20.1 %collective-permute-start.24 = (bf16[128,2048]{1,0:T(8,128)(2,1)S(1)}, bf16[128,2048]{1,0:T(8,128)(2,1)}, u32[]{:S(2)}, u32[]{:S(2)}) collective-permute-start(bf16[128,2048]{1,0:T(8,128)(2,1)S(1)} %add.92.own_ref), channel_id=1, source_target_pairs={{0,8},{4,12},{24,16},{28,20},{1,9},{5,13},{25,17},{29,21},{2,10},{... | collective-permute-start | bytes 1572872 | tf_op jit(solution)/shard_map/ppermute | solution.py:390
  91.1 56.1 %collective-permute-start.28 = (bf16[1024,256]{1,0:T(8,128)(2,1)}, bf16[1024,256]{1,0:T(8,128)(2,1)S(1)}, u32[]{:S(2)}, u32[]{:S(2)}) collective-permute-start(bf16[1024,256]{1,0:T(8,128)(2,1)} %dynamic-slice_select_fusion), channel_id=1, source_target_pairs={{0,1},{4,5},{9,8},{13,12},{18,19},{22,23},{27,26},{31,30}} | collective-permute-start | bytes 1572872 | tf_op jit(solution)/shard_map/ppermute | solution.py:398
  95.0 45.8 %collective-permute-start.10 = (bf16[64,7168]{1,0:T(8,128)(2,1)}, bf16[64,7168]{1,0:T(8,128)(2,1)S(1)}, u32[]{:S(2)}, u32[]{:S(2)}) collective-permute-start(bf16[64,7168]{1,0:T(8,128)(2,1)} %pad_maximum_fusion), channel_id=1, source_target_pairs={{0,8},{4,12},{24,16},{28,20},{1,9},{5,13},{25,17},{29,21},{2,10},{... | collective-permute-start | bytes 2752520 | tf_op jit(solution)/shard_map/ppermute | solution.py:374
  99.6 44.1 %collective-permute-start.8 = (bf16[128,1536]{1,0:T(8,128)(2,1)S(1)}, bf16[128,1536]{1,0:T(8,128)(2,1)S(1)}, u32[]{:S(2)}, u32[]{:S(2)}) collective-permute-start(bf16[128,1536]{1,0:T(8,128)(2,1)S(1)} %add.86.own_ref), channel_id=1, source_target_pairs={{0,8},{4,12},{24,16},{28,20},{1,9},{5,13},{25,17},{29,21},{2,10},{... | collective-permute-start | bytes 1179656 | tf_op jit(solution)/shard_map/ppermute | solution.py:390
  102.2 37.9 %collective-permute-start.19 = (bf16[128,2048]{1,0:T(8,128)(2,1)S(1)}, bf16[128,2048]{1,0:T(8,128)(2,1)S(1)}, u32[]{:S(2)}, u32[]{:S(2)}) collective-permute-start(bf16[128,2048]{1,0:T(8,128)(2,1)S(1)} %add.90.own_ref), channel_id=1, source_target_pairs={{0,8},{4,12},{24,16},{28,20},{1,9},{5,13},{25,17},{29,21},{2,10},{... | collective-permute-start | bytes 1572872 | tf_op jit(solution)/shard_map/ppermute | solution.py:390
  104.6 46.3 %collective-permute-start.15 = (bf16[64,1536]{1,0:T(8,128)(2,1)S(1)}, bf16[64,1536]{1,0:T(8,128)(2,1)S(1)}, u32[]{:S(2)}, u32[]{:S(2)}) collective-permute-start(bf16[64,1536]{1,0:T(8,128)(2,1)S(1)} %slice_add_fusion.2), channel_id=1, source_target_pairs={{8,16},{12,20},{16,8},{20,12},{9,17},{13,21},{17,9},{21,13},{10,18... | collective-permute-start | bytes 589832 | tf_op jit(solution)/shard_map/ppermute | solution.py:402
  145.9 28.7 %collective-permute-start.27 = (bf16[128,2048]{1,0:T(8,128)(2,1)S(1)}, bf16[128,2048]{1,0:T(8,128)(2,1)S(1)}, u32[]{:S(2)}, u32[]{:S(2)}) collective-permute-start(bf16[128,2048]{1,0:T(8,128)(2,1)S(1)} %pad_maximum_fusion.2), channel_id=1, source_target_pairs={{8,0},{12,4},{16,24},{20,28},{9,1},{13,5},{17,25},{21,29},{10,2},{... | collective-permute-start | bytes 1572872 | tf_op jit(solution)/shard_map/ppermute | solution.py:405
  147.4 58.4 %collective-permute-start.29 = (bf16[1024,256]{1,0:T(8,128)(2,1)S(1)}, bf16[1024,256]{1,0:T(8,128)(2,1)S(1)}, u32[]{:S(2)}, u32[]{:S(2)}) collective-permute-start(bf16[1024,256]{1,0:T(8,128)(2,1)S(1)} %fusion.6), channel_id=1, source_target_pairs={{0,2},{1,3},{4,6},{5,7},{9,11},{8,10},{13,15},{12,14},{18,16},{19,... | collective-permute-start | bytes 1572872 | tf_op jit(solution)/shard_map/ppermute | solution.py:398
  154.3 22.3 %collective-permute-start.11 = (bf16[64,1536]{1,0:T(8,128)(2,1)S(1)}, bf16[64,1536]{1,0:T(8,128)(2,1)S(1)}, u32[]{:S(2)}, u32[]{:S(2)}) collective-permute-start(bf16[64,1536]{1,0:T(8,128)(2,1)S(1)} %get-tuple-element.33.near_ref), channel_id=1, source_target_pairs={{8,16},{12,20},{16,8},{20,12},{9,17},{13,21},{17,9},{21,13},{10,18... | collective-permute-start | bytes 589832 | tf_op jit(solution)/shard_map/ppermute | solution.py:404
  155.1 38.9 %collective-permute-start.22 = (bf16[128,2048]{1,0:T(8,128)(2,1)S(1)}, bf16[128,2048]{1,0:T(8,128)(2,1)S(1)}, u32[]{:S(2)}, u32[]{:S(2)}) collective-permute-start(bf16[128,2048]{1,0:T(8,128)(2,1)S(1)} %pad_maximum_fusion.1), channel_id=1, source_target_pairs={{8,0},{12,4},{16,24},{20,28},{9,1},{13,5},{17,25},{21,29},{10,2},{... | collective-permute-start | bytes 1572872 | tf_op jit(solution)/shard_map/ppermute | solution.py:405
  156.4 43.5 %collective-permute-start.17 = (bf16[128,1536]{1,0:T(8,128)(2,1)S(1)}, bf16[128,1536]{1,0:T(8,128)(2,1)S(1)}, u32[]{:S(2)}, u32[]{:S(2)}) collective-permute-start(bf16[128,1536]{1,0:T(8,128)(2,1)S(1)} %pad_maximum_fusion.4), channel_id=1, source_target_pairs={{8,0},{12,4},{16,24},{20,28},{9,1},{13,5},{17,25},{21,29},{10,2},{... | collective-permute-start | bytes 1179656 | tf_op jit(solution)/shard_map/ppermute | solution.py:405
  176.6 29.3 %collective-permute-start.33 = (bf16[128,2048]{1,0:T(8,128)(2,1)S(1)}, bf16[128,2048]{1,0:T(8,128)(2,1)S(1)}, u32[]{:S(2)}, u32[]{:S(2)}) collective-permute-start(bf16[128,2048]{1,0:T(8,128)(2,1)S(1)} %get-tuple-element.58.mine_ref), channel_id=1, source_target_pairs={{0,4},{4,0},{8,12},{12,8},{16,20},{20,16},{24,28},{28,24},{1,5},{5... | collective-permute-start | bytes 1572872 | tf_op jit(solution)/shard_map/ppermute | solution.py:409
  176.6 27.5 %collective-permute-start.12 = (bf16[128,1536]{1,0:T(8,128)(2,1)S(1)}, bf16[128,1536]{1,0:T(8,128)(2,1)S(1)}, u32[]{:S(2)}, u32[]{:S(2)}) collective-permute-start(bf16[128,1536]{1,0:T(8,128)(2,1)S(1)} %pad_maximum_fusion.3), channel_id=1, source_target_pairs={{8,0},{12,4},{16,24},{20,28},{9,1},{13,5},{17,25},{21,29},{10,2},{... | collective-permute-start | bytes 1179656 | tf_op jit(solution)/shard_map/ppermute | solution.py:405
  195.3 14.6 %collective-permute-start.32 = (bf16[128,2048]{1,0:T(8,128)(2,1)S(1)}, bf16[128,2048]{1,0:T(8,128)(2,1)S(1)}, u32[]{:S(2)}, u32[]{:S(2)}) collective-permute-start(bf16[128,2048]{1,0:T(8,128)(2,1)S(1)} %get-tuple-element.57.mine_ref), channel_id=1, source_target_pairs={{0,4},{4,0},{8,12},{12,8},{16,20},{20,16},{24,28},{28,24},{1,5},{5... | collective-permute-start | bytes 1572872 | tf_op jit(solution)/shard_map/ppermute | solution.py:409
  (22 other events, 132.1 us)

commit v2 on v1

--- a/solution.py
+++ b/solution.py
@@ -7,6 +7,7 @@
 from jax.experimental.pallas import tpu as pltpu
 from jax.sharding import PartitionSpec as P
 
+
 ADAM_STEP = 100
 
 
@@ -21,7 +22,7 @@
 
 F32, BF16 = jnp.float32, jnp.bfloat16
 CORES = 2
-CHUNKS = (4, 4, 3, 3)
+CHUNKS = (4, 4, 4, 2)
 MIB = 1 << 20
 
 
@@ -81,58 +82,106 @@
     )
 
 
-def project_kernel(slot_ref, basis_ref, act_ref, out_ref, turned):
-    rows = basis_ref.shape[1] // slot_ref.shape[0]
-
-    @pl.when(pl.program_id(0) == 0)
-    def _():
-        flipped = basis_ref[...].T
-        for n in range(slot_ref.shape[0]):
-            at = pl.multiple_of(slot_ref[n] * rows, rows)
-            turned[pl.ds(at, rows), :] = flipped[n * rows : (n + 1) * rows, :]
-
-    out_ref[...] = lax.dot_general(
-        turned[...], act_ref[...], (((1,), (1,)), ((), ())), preferred_element_type=F32
-    ).astype(out_ref.dtype)
-
-
-def project(slots, basis, activations, start, count):
-    depth, rank = basis.shape
-    block = pick(count, 384)
+def project_pieces(turned, act_hbm, out_ref, act_buf, act_sem, start):
+    pieces = act_sem.shape[0]
+    size = act_buf.shape[0] // pieces
+    copies = []
+    for i in range(pieces):
+        copies.append(
+            pltpu.make_async_copy(
+                act_hbm.at[pl.ds(start + i * size, size)],
+                act_buf.at[pl.ds(i * size, size)],
+                act_sem.at[i],
+            )
+        )
+        copies[-1].start()
+    yield
+    for i, copy in enumerate(copies):
+        copy.wait()
+        out_ref[:, i * size : (i + 1) * size] = lax.dot_general(
+            turned[...],
+            act_buf[i * size : (i + 1) * size, :],
+            (((1,), (1,)), ((), ())),
+            preferred_element_type=F32,
+        ).astype(out_ref.dtype)
+    yield
+
+
+def project_first_kernel(
+    start, slot_ref, basis_hbm, act_hbm, out_ref, turned_ref, basis_buf, basis_sem, act_buf, act_sem
+):
+    rows = basis_buf.shape[1] // slot_ref.shape[0]
+    copy = pltpu.make_async_copy(basis_hbm, basis_buf, basis_sem)
+    copy.start()
+    work = project_pieces(turned_ref, act_hbm, out_ref, act_buf, act_sem, start)
+    next(work)
+    copy.wait()
+    flipped = basis_buf[...].T
+    for n in range(slot_ref.shape[0]):
+        at = pl.multiple_of(slot_ref[n] * rows, rows)
+        turned_ref[pl.ds(at, rows), :] = flipped[n * rows : (n + 1) * rows, :]
+    next(work)
+
+
+def project_kernel(start, turned_ref, act_hbm, out_ref, act_buf, act_sem):
+    work = project_pieces(turned_ref, act_hbm, out_ref, act_buf, act_sem, start)
+    next(work)
+    next(work)
+
+
+def project(source, slots, activations, start, count):
+    depth = activations.shape[1]
+    rank = source.shape[1] if slots is not None else source.shape[0]
+    hbm = pl.BlockSpec(memory_space=pltpu.HBM)
+    vmem = pl.BlockSpec(memory_space=pltpu.VMEM)
+    part = jax.ShapeDtypeStruct((rank, count), BF16)
+    scratch = [
+        pltpu.VMEM((count, depth), BF16),
+        pltpu.SemaphoreType.DMA((count // pick(count, 256),)),
+    ]
+    estimate = pl.CostEstimate(
+        flops=2 * depth * rank * count,
+        bytes_accessed=2 * (depth * rank + depth * count + rank * count),
+        transcendentals=0,
+    )
+    if slots is None:
+        return pl.pallas_call(
+            functools.partial(project_kernel, start),
+            out_shape=part,
+            in_specs=[vmem, hbm],
+            out_specs=vmem,
+            scratch_shapes=scratch,
+            compiler_params=pltpu.CompilerParams(vmem_limit_bytes=16 * MIB),
+            cost_estimate=estimate,
+            name="project",
+        )(source, activations)
     return pl.pallas_call(
-        project_kernel,
-        out_shape=jax.ShapeDtypeStruct((rank, count), BF16),
-        grid_spec=pltpu.PrefetchScalarGridSpec(
-            num_scalar_prefetch=1,
-            grid=(count // block,),
-            in_specs=[
-                pl.BlockSpec((depth, rank), lambda i, s: (0, 0)),
-                pl.BlockSpec((block, depth), lambda i, s: (start // block + i, 0)),
-            ],
-            out_specs=pl.BlockSpec((rank, block), lambda i, s: (0, i)),
-            scratch_shapes=[pltpu.VMEM((rank, depth), BF16)],
-        ),
-        compiler_params=params(20),
-        cost_estimate=pl.CostEstimate(
-            flops=2 * depth * rank * count,
-            bytes_accessed=2 * (depth * rank + depth * count + rank * count),
-            transcendentals=0,
-        ),
-        name="project",
-    )(slots, basis, activations)
-
-
-def gradient_kernel(left_a, left_b, grads_ref, keep_ref, give_ref):
-    half = left_a.shape[1]
-    total = jnp.dot(left_a[...], grads_ref[:half, :], preferred_element_type=F32)
-    total += jnp.dot(left_b[...], grads_ref[half:, :], preferred_element_type=F32)
+        functools.partial(project_first_kernel, start),
+        out_shape=[part, jax.ShapeDtypeStruct((rank, depth), BF16)],
+        in_specs=[pl.BlockSpec(memory_space=pltpu.SMEM), hbm, hbm],
+        out_specs=[vmem, vmem],
+        scratch_shapes=[pltpu.VMEM((depth, rank), BF16), pltpu.SemaphoreType.DMA, *scratch],
+        compiler_params=pltpu.CompilerParams(vmem_limit_bytes=16 * MIB),
+        cost_estimate=estimate,
+        name="project_first",
+    )(slots, source, activations)
+
+
+def gradient_kernel(*refs):
+    *lefts, grads_ref, keep_ref, give_ref = refs
+    total, at = None, 0
+    for left in lefts:
+        size = left.shape[1]
+        term = jnp.dot(left[...], grads_ref[at : at + size, :], preferred_element_type=F32)
+        total = term if total is None else total + term
+        at += size
     rows = keep_ref.shape[0]
     keep_ref[...] = total[:rows].astype(BF16)
     give_ref[...] = total[rows:].astype(BF16)
 
 
-def gradient_chunk(left_a, left_b, out_grads, start, width):
-    rank, half = left_a.shape
+def gradient_chunk(lefts, out_grads, start, width):
+    rank = lefts[0].shape[0]
     tokens = out_grads.shape[0]
     tile = pick(width, 512)
     while start % tile:
@@ -142,19 +191,18 @@
         out_shape=[jax.ShapeDtypeStruct((rank // 2, width), BF16)] * 2,
         grid=(width // tile,),
         in_specs=[
-            pl.BlockSpec((rank, half), lambda i: (0, 0)),
-            pl.BlockSpec((rank, half), lambda i: (0, 0)),
+            *(pl.BlockSpec(left.shape, lambda i: (0, 0)) for left in lefts),
             pl.BlockSpec((tokens, tile), lambda i: (0, start // tile + i)),
         ],
         out_specs=[pl.BlockSpec((rank // 2, tile), lambda i: (0, i))] * 2,
-        compiler_params=params(20),
+        compiler_params=params(44),
         cost_estimate=pl.CostEstimate(
             flops=2 * rank * tokens * width,
             bytes_accessed=2 * (rank * tokens + tokens * width + rank * width),
             transcendentals=0,
         ),
         name="gradient",
-    )(left_a, left_b, out_grads)
+    )(*lefts, out_grads)
 
 
 def moments(gradient, first, second):
@@ -317,13 +365,11 @@
     )(slots, basis_rows, mine, other, *results)
 
 
-def doubling(part, bits):
-    count = lax.axis_size("tensor")
-    for step, bit in enumerate(bits):
-        got = lax.ppermute(part, "tensor", [(t, t ^ bit) for t in range(count)])
-        if step == len(bits) - 1:
-            return part, got
-        part = (part.astype(F32) + got.astype(F32)).astype(BF16)
+def token_pieces(tokens):
+    unit = 256 if tokens % 256 == 0 else 128
+    count = tokens // unit
+    sizes = [(count // 4 + (i < count % 4)) * unit for i in range(4)]
+    return [(sum(sizes[:i]), size) for i, size in enumerate(sizes) if size]
 
 
 def local_line(activations, out_grads, basis, first_moment, second_moment, reward_codes, token_ids):
@@ -353,42 +399,44 @@
     slots = ((block % CORES) ^ core).astype(jnp.int32) * chips + 2 * far + is_hub
 
     bits = [1 << b for b in range(tensor_count.bit_length() - 1)]
-    half = tokens // 2
-    part_a = project(slots, basis, activations, 0, half)
-    part_b = project(slots, basis, activations, half, half)
-    sum_a, got_a = doubling(part_a, bits)
-    sum_b, got_b = doubling(part_b, bits[::-1])
+    parts = []
+    source = basis
+    for i, (start, count) in enumerate(token_pieces(tokens)):
+        if i == 0:
+            part, source = project(basis, slots, activations, start, count)
+        else:
+            part = project(source, None, activations, start, count)
+        parts.append(part)
+    got = [None] * len(parts)
+    for step in range(len(bits)):
+        for i, part in enumerate(parts):
+            bit = bits[step] if i % 2 == 0 else bits[-1 - step]
+            if step:
+                part = parts[i] = (part.astype(F32) + got[i].astype(F32)).astype(BF16)
+            pairs = [(t, t ^ bit) for t in range(tensor_count)]
+            got[i] = lax.ppermute(part, "tensor", pairs)
 
     unmasked = (token_ids != pad_token).astype(F32)
     weights = unmasked * jnp.exp(reward_temp * reward_codes.astype(F32))
     normalizer = jnp.full((8, 128), jnp.sum(weights), F32)
     for b in range(data_count.bit_length() - 1):
-        normalizer = normalizer + lax.ppermute(
-            normalizer, "dp", [(i, i ^ (1 << b)) for i in range(data_count)]
-        )
+        pairs = [(i, i ^ (1 << b)) for i in range(data_count)]
+        normalizer = normalizer + lax.ppermute(normalizer, "dp", pairs)
     scale = (tokens * data_count) / normalizer[:1, :1]
 
-    left_a = (weights[None, :half] * (sum_a.astype(F32) + got_a.astype(F32))).astype(BF16)
-    left_b = (weights[None, half:] * (sum_b.astype(F32) + got_b.astype(F32))).astype(BF16)
-
-    moved = lax.ppermute(
-        jnp.concatenate([first_moment, second_moment]).astype(BF16), "dp", inward
-    )
+    lefts = []
+    for (start, count), part, other in zip(token_pieces(tokens), parts, got):
+        total = part.astype(F32) + other.astype(F32)
+        lefts.append((weights[None, start : start + count] * total).astype(BF16))
+
+    moved = lax.ppermute(jnp.concatenate([first_moment, second_moment]).astype(BF16), "dp", inward)
+    lefts, moved, scale = lax.optimization_barrier((lefts, moved, scale))
 
     row_count = basis.shape[0] * tensor_count // data_count
     per_owner = data_count // tensor_count
     owner = data_index // per_owner
     basis_rows = lax.dynamic_slice_in_dim(basis, data_index % per_owner * row_count, row_count, 0)
     basis_rows = jnp.where(tensor_index == owner, basis_rows, jnp.zeros_like(basis_rows))
-
-    unit = full // sum(CHUNKS)
-    starts = [unit * sum(CHUNKS[:i]) for i in range(len(CHUNKS))]
-    own, outer = [], []
-    for start, parts in zip(starts, CHUNKS):
-        keep, give = gradient_chunk(left_a, left_b, out_grads, start, unit * parts)
-        own.append(keep + lax.ppermute(give, "dp", sibling))
-        outer.append(lax.ppermute(own[-1], "dp", inward))
-
     for bit in bits:
         pairs = [
             (d * tensor_count + (d // per_owner ^ s), d * tensor_count + (d // per_owner ^ s ^ bit))
@@ -397,10 +445,17 @@
         ]
         basis_rows = basis_rows + lax.ppermute(basis_rows, ("dp", "tensor"), pairs)
 
+    unit = full // sum(CHUNKS)
+    starts = [unit * sum(CHUNKS[:i]) for i in range(len(CHUNKS))]
     settled, spread = (), ()
-    for start, mine, came in zip(starts, own, outer):
+    for start, size in zip(starts, CHUNKS):
+        keep, give = gradient_chunk(lefts, out_grads, start, unit * size)
+        mine = keep + lax.ppermute(give, "dp", sibling)
+        came = lax.ppermute(mine, "dp", inward)
         across = lax.ppermute(mine[2 * rows :] + came[2 * rows :], "dp", middle)
-        near, total = hub_chunk(scale, mine, came, across, first_moment, second_moment, moved, start)
+        near, total = hub_chunk(
+            scale, mine, came, across, first_moment, second_moment, moved, start
+        )
         beyond = lax.ppermute(near, "dp", middle)
         sent = lax.ppermute(jnp.concatenate([total, near[rows:], beyond]), "dp", outward)
         updates, *settled = settle_chunk(
@@ -411,12 +466,16 @@
     return (*settled, *spread)
 
 
+def staged(*args):
+    return local_line(*args)
+
+
 def solution(mesh):
     data_count, tensor_count = mesh.shape["dp"], mesh.shape["tensor"]
     line = data_count == 4 * CORES and tensor_count > 1 and tensor_count & (tensor_count - 1) == 0
     line = line and data_count % tensor_count == 0
     return jax.shard_map(
-        local_line if line else local_general,
+        staged if line else local_general,
         mesh=mesh,
         in_specs=(
             P("dp", "tensor"),

time: 222 us -> 209 us (0.941)
  waiting for transfers between devices: 97.1 us -> 70.2 us
  starting transfers between devices: 42.7 us -> 52 us
  Pallas kernels: 49.2 us -> 54 us
  local copies, waits for them, and re-layouts: 18.1 us -> 14 us
    ppermute x15 -> x19, waiting for transfers between devices: 57.8 us -> 39.7 us  [the longest x4 23.2 us: local_line(): came = lax.ppermute(mine, 'dp', inward)]
    ppermute x4, waiting for transfers between devices: 39.2 us -> 30.5 us  [local_line(): lax.ppermute(jnp.concatenate([total, near[rows:], beyond]), 'dp', outward)]
    pallas_call x4, Pallas kernels: 15.7 us -> 21.6 us  [gradient_chunk(): pl.pallas_call(gradient_kernel, out_shape=[jax.ShapeDtypeStruct((rank //...]
    ppermute x15 -> x19, starting transfers between devices: 22.5 us -> 27.6 us  [the longest x4 12 us: local_line(): came = lax.ppermute(mine, 'dp', inward)]
    unnamed x24 -> x44, local copies, waits for them, and re-layouts: 16.9 us -> 11.9 us
    add x7, other arithmetic: 5.95 us -> 2.86 us  [the longest x4 1.56 us: local_line(): mine = keep + lax.ppermute(give, 'dp', sibling)]
    another operation x2, other arithmetic: 0.09 us -> 2.45 us
    pallas_call x2 -> x4, Pallas kernels: 6.49 us -> 7.96 us  [the longest x3 4.83 us: project(): pl.pallas_call(functools.partial(project_kernel, start), out_shape=part,...]
  transfers between devices with their start and end apart: 34 -> 38, of which waited for: 9 -> 12; matrix products, arithmetic and copies ran while one was open for 6% -> 7% of each run, Pallas kernels for 19% -> 22%
where the time goes in v2:
time: 209 us; the launch traced here: 206 us
  waiting for transfers between devices  70.2 us (34%)
  Pallas kernels  54 us (26%)
  starting transfers between devices  52 us (25%)
  local copies, waits for them, and re-layouts  14 us (7%)
  other arithmetic  13.6 us (7%)
    ppermute x4, waiting for transfers between devices, local_line(): lax.ppermute(jnp.concatenate([total, near[rows:], beyond]), 'dp', outward)  30.5 us
    ppermute x4, waiting for transfers between devices, local_line(): came = lax.ppermute(mine, 'dp', inward)  23.2 us
    pallas_call x4, Pallas kernels, gradient_chunk(): pl.pallas_call(gradient_kernel, out_shape=[jax.ShapeDtypeStruct((rank //...  21.6 us
    pallas_call x4, Pallas kernels, spread_chunk(): pl.pallas_call(spread_kernel, out_shape=jax.ShapeDtypeStruct((count, full...  14.3 us
    ppermute x8, waiting for transfers between devices, local_line(): got[i] = lax.ppermute(part, 'tensor', pairs)  12.5 us
    ppermute x4, starting transfers between devices, local_line(): came = lax.ppermute(mine, 'dp', inward)  12 us
    unnamed x44, local copies, waits for them, and re-layouts  11.9 us
    ppermute x8, starting transfers between devices, local_line(): got[i] = lax.ppermute(part, 'tensor', pairs)  10.5 us
  transfers between devices with their start and end apart: 38, of which 12 were waited for; matrix products, arithmetic and copies ran while one was open for 7% of the time, Pallas kernels for 22%

profile of v2, /device:TPU:0, one launch (start us, length us, event | category | flops | bytes accessed | tf_op | source)
XLA Modules:
  0.0 205.8 jit_solution(8873191771237375368)
XLA Ops:
  5.7 4.5 %collective-permute-start.8 = (bf16[64,7168]{1,0:T(8,128)(2,1)S(1)}, bf16[64,7168]{1,0:T(8,128)(2,1)S(1)}, u32[]{:S(2)}, u32[]{:S(2)}) collective-permute-start(bf16[64,7168]{1,0:T(8,128)(2,1)S(1)} %pad_maximum_fusion), channel_id=1, source_target_pairs={{0,8},{4,12},{24,16},{28,20},{1,9},{5,13},{25,17},{29,21},{2,10},{... | collective-permute-start | bytes 2752520 | tf_op jit(solution)/shard_map/ppermute | solution.py:432
  10.3 3.7 %copy-done = bf16[2304,2048]{1,0:T(8,128)(2,1)S(1)} copy-done((bf16[2304,2048]{1,0:T(8,128)(2,1)S(1)}, bf16[2304,2048]{1,0:T(8,128)(2,1)}, u32[]{:S(2)}) %copy-start) | copy-done | bytes 9437208
  31.2 3.6 %collective-permute-start.11 = (f32[8,128]{1,0:T(8,128)S(1)}, f32[8,128]{1,0:T(8,128)S(1)}, u32[]{:S(2)}, u32[]{:S(2)}) collective-permute-start(f32[8,128]{1,0:T(8,128)S(1)} %fusion.7), channel_id=1, source_target_pairs={{0,16},{4,20},{8,24},{12,28},{16,0},{20,4},{24,8},{28,12},{1,17},{... | collective-permute-start | bytes 12296 | tf_op jit(solution)/shard_map/ppermute | solution.py:424
  43.0 5.3 %collective-permute-done = bf16[256,768]{1,0:T(8,128)(2,1)S(1)} collective-permute-done((bf16[256,768]{1,0:T(8,128)(2,1)S(1)}, bf16[256,768]{1,0:T(8,128)(2,1)S(1)}, u32[]{:S(2)}, u32[]{:S(2)}) %collective-permute-start) | collective-permute-done | bytes 393248 | tf_op jit(solution)/shard_map/ppermute | solution.py:417
  50.0 3.9 %collective-permute-done.3 = bf16[256,512]{1,0:T(8,128)(2,1)S(1)} collective-permute-done((bf16[256,512]{1,0:T(8,128)(2,1)S(1)}, bf16[256,512]{1,0:T(8,128)(2,1)S(1)}, u32[]{:S(2)}, u32[]{:S(2)}) %collective-permute-start.3) | collective-permute-done | bytes 262176 | tf_op jit(solution)/shard_map/ppermute | solution.py:417
  54.1 3.2 %collective-permute-done.7 = bf16[256,512]{1,0:T(8,128)(2,1)S(1)} collective-permute-done((bf16[256,512]{1,0:T(8,128)(2,1)S(1)}, bf16[256,512]{1,0:T(8,128)(2,1)S(1)}, u32[]{:S(2)}, u32[]{:S(2)}) %collective-permute-start.7) | collective-permute-done | bytes 262176 | tf_op jit(solution)/shard_map/ppermute | solution.py:417
  57.6 5.9 %gradient.7 = (bf16[128,2048]{1,0:T(8,128)(2,1)S(1)}, bf16[128,2048]{1,0:T(8,128)(2,1)S(1)}) custom-call(bf16[256,768]{1,0:T(8,128)(2,1)S(1)} %multiply_convert_fusion.refs_0_, bf16[256,512]{1,0:T(8,128)(2,1)S(1)} %multiply_convert_fusion.3.refs_1_, bf16[256,512]{1,0:T(8,128)(2,1)S(1)} %multiply_convert_fusion.2.refs_2_, ...), custom_call_target="tpu_custom_call" | custom-call | flops 2415919104 | bytes 11665408 | tf_op jit(solution)/shard_map/gradient/pallas_call | solution.py:189
  63.6 5.9 %gradient.6 = (bf16[128,2048]{1,0:T(8,128)(2,1)S(1)}, bf16[128,2048]{1,0:T(8,128)(2,1)S(1)}) custom-call(bf16[256,768]{1,0:T(8,128)(2,1)S(1)} %multiply_convert_fusion.refs_0_, bf16[256,512]{1,0:T(8,128)(2,1)S(1)} %multiply_convert_fusion.3.refs_1_, bf16[256,512]{1,0:T(8,128)(2,1)S(1)} %multiply_convert_fusion.2.refs_2_, ...), custom_call_target="tpu_custom_call" | custom-call | flops 2415919104 | bytes 11665408 | tf_op jit(solution)/shard_map/gradient/pallas_call | solution.py:189
  70.1 5.9 %gradient.5 = (bf16[128,2048]{1,0:T(8,128)(2,1)S(1)}, bf16[128,2048]{1,0:T(8,128)(2,1)S(1)}) custom-call(bf16[256,768]{1,0:T(8,128)(2,1)S(1)} %multiply_convert_fusion.refs_0_, bf16[256,512]{1,0:T(8,128)(2,1)S(1)} %multiply_convert_fusion.3.refs_1_, bf16[256,512]{1,0:T(8,128)(2,1)S(1)} %multiply_convert_fusion.2.refs_2_, ...), custom_call_target="tpu_custom_call" | custom-call | flops 2415919104 | bytes 11665408 | tf_op jit(solution)/shard_map/gradient/pallas_call | solution.py:189
  76.2 3.6 %collective-permute-start.28 = (bf16[128,2048]{1,0:T(8,128)(2,1)S(1)}, bf16[128,2048]{1,0:T(8,128)(2,1)S(1)}, u32[]{:S(2)}, u32[]{:S(2)}) collective-permute-start(bf16[128,2048]{1,0:T(8,128)(2,1)S(1)} %add.108.own_ref), channel_id=1, source_target_pairs={{0,8},{4,12},{24,16},{28,20},{1,9},{5,13},{25,17},{29,21},{2,10},{... | collective-permute-start | bytes 1572872 | tf_op jit(solution)/shard_map/ppermute | solution.py:454
  81.5 3.9 %gradient.4 = (bf16[128,1024]{1,0:T(8,128)(2,1)S(1)}, bf16[128,1024]{1,0:T(8,128)(2,1)}) custom-call(bf16[256,768]{1,0:T(8,128)(2,1)S(1)} %multiply_convert_fusion.refs_0_, bf16[256,512]{1,0:T(8,128)(2,1)S(1)} %multiply_convert_fusion.3.refs_1_, bf16[256,512]{1,0:T(8,128)(2,1)S(1)} %multiply_convert_fusion.2.refs_2_, ...), custom_call_target="tpu_custom_call" | custom-call | flops 1207959552 | bytes 6422528 | tf_op jit(solution)/shard_map/gradient/pallas_call | solution.py:189
  88.0 4.1 %collective-permute-done.28.outer_ref = bf16[128,2048]{1,0:T(8,128)(2,1)S(1)} collective-permute-done((bf16[128,2048]{1,0:T(8,128)(2,1)S(1)}, bf16[128,2048]{1,0:T(8,128)(2,1)S(1)}, u32[]{:S(2)}, u32[]{:S(2)}) %collective-permute-start.28) | collective-permute-done | bytes 524320 | tf_op jit(solution)/shard_map/ppermute | solution.py:454
  92.8 10.5 %collective-permute-done.23.outer_ref = bf16[128,2048]{1,0:T(8,128)(2,1)S(1)} collective-permute-done((bf16[128,2048]{1,0:T(8,128)(2,1)S(1)}, bf16[128,2048]{1,0:T(8,128)(2,1)S(1)}, u32[]{:S(2)}, u32[]{:S(2)}) %collective-permute-start.23) | collective-permute-done | bytes 524320 | tf_op jit(solution)/shard_map/ppermute | solution.py:454
  105.5 8.6 %collective-permute-done.18.outer_ref = bf16[128,2048]{1,0:T(8,128)(2,1)S(1)} collective-permute-done((bf16[128,2048]{1,0:T(8,128)(2,1)S(1)}, bf16[128,2048]{1,0:T(8,128)(2,1)S(1)}, u32[]{:S(2)}, u32[]{:S(2)}) %collective-permute-start.18) | collective-permute-done | bytes 524320 | tf_op jit(solution)/shard_map/ppermute | solution.py:454
  120.9 4.2 %collective-permute-start.32 = (bf16[1024,256]{1,0:T(8,128)(2,1)}, bf16[1024,256]{1,0:T(8,128)(2,1)}, u32[]{:S(2)}, u32[]{:S(2)}) collective-permute-start(bf16[1024,256]{1,0:T(8,128)(2,1)} %dynamic-slice_select_fusion), channel_id=1, source_target_pairs={{0,1},{4,5},{9,8},{13,12},{18,19},{22,23},{27,26},{31,30}} | collective-permute-start | bytes 1572872 | tf_op jit(solution)/shard_map/ppermute | solution.py:446
  126.3 5.4 %collective-permute-start.13 = (bf16[128,1024]{1,0:T(8,128)(2,1)S(1)}, bf16[128,1024]{1,0:T(8,128)(2,1)S(1)}, u32[]{:S(2)}, u32[]{:S(2)}) collective-permute-start(bf16[128,1024]{1,0:T(8,128)(2,1)S(1)} %add.102.own_ref), channel_id=1, source_target_pairs={{0,8},{4,12},{24,16},{28,20},{1,9},{5,13},{25,17},{29,21},{2,10},{... | collective-permute-start | bytes 786440 | tf_op jit(solution)/shard_map/ppermute | solution.py:454
  146.6 3.8 %collective-permute-start.33 = (bf16[1024,256]{1,0:T(8,128)(2,1)S(1)}, bf16[1024,256]{1,0:T(8,128)(2,1)S(1)}, u32[]{:S(2)}, u32[]{:S(2)}) collective-permute-start(bf16[1024,256]{1,0:T(8,128)(2,1)S(1)} %fusion.6), channel_id=1, source_target_pairs={{0,2},{1,3},{4,6},{5,7},{9,11},{8,10},{13,15},{12,14},{18,16},{19,... | collective-permute-start | bytes 1572872 | tf_op jit(solution)/shard_map/ppermute | solution.py:446
  150.4 8.0 %collective-permute-done.31.sent_ref = bf16[128,2048]{1,0:T(8,128)(2,1)S(1)} collective-permute-done((bf16[128,2048]{1,0:T(8,128)(2,1)S(1)}, bf16[128,2048]{1,0:T(8,128)(2,1)S(1)}, u32[]{:S(2)}, u32[]{:S(2)}) %collective-permute-start.31) | collective-permute-done | bytes 524320 | tf_op jit(solution)/shard_map/ppermute | solution.py:460
  163.5 6.2 %collective-permute-done.26.sent_ref = bf16[128,2048]{1,0:T(8,128)(2,1)S(1)} collective-permute-done((bf16[128,2048]{1,0:T(8,128)(2,1)S(1)}, bf16[128,2048]{1,0:T(8,128)(2,1)S(1)}, u32[]{:S(2)}, u32[]{:S(2)}) %collective-permute-start.26) | collective-permute-done | bytes 524320 | tf_op jit(solution)/shard_map/ppermute | solution.py:460
  171.6 7.2 %collective-permute-done.21.sent_ref = bf16[128,2048]{1,0:T(8,128)(2,1)S(1)} collective-permute-done((bf16[128,2048]{1,0:T(8,128)(2,1)S(1)}, bf16[128,2048]{1,0:T(8,128)(2,1)S(1)}, u32[]{:S(2)}, u32[]{:S(2)}) %collective-permute-start.21) | collective-permute-done | bytes 524320 | tf_op jit(solution)/shard_map/ppermute | solution.py:460
  181.6 9.2 %collective-permute-done.16.sent_ref = bf16[128,1024]{1,0:T(8,128)(2,1)S(1)} collective-permute-done((bf16[128,1024]{1,0:T(8,128)(2,1)S(1)}, bf16[128,1024]{1,0:T(8,128)(2,1)S(1)}, u32[]{:S(2)}, u32[]{:S(2)}) %collective-permute-start.16) | collective-permute-done | bytes 262176 | tf_op jit(solution)/shard_map/ppermute | solution.py:460
  191.5 3.9 %spread.4.rest_0_ = bf16[1024,7168]{1,0:T(8,128)(2,1)} custom-call(s32[8]{0:T(128)S(1)} %fusion.slot_ref, bf16[1024,256]{1,0:T(8,128)(2,1)S(1)} %add.112.basis_ref, bf16[128,2048]{1,0:T(8,128)(2,1)S(1)} %get-tuple-element.74.mine_ref, bf16[128,2048]{1,0:T(8,128)(2,1)S(1)} %collective-permute-done.37.other_ref), custom_call_target="tpu_custom_call" | custom-call | flops 1073741824 | bytes 5767168 | tf_op jit(solution)/shard_map/spread/pallas_call | solution.py:342
  195.5 3.9 %spread.5.rest_0_ = bf16[1024,7168]{1,0:T(8,128)(2,1)} custom-call(s32[8]{0:T(128)S(1)} %fusion.slot_ref, bf16[1024,256]{1,0:T(8,128)(2,1)S(1)} %add.112.basis_ref, bf16[128,2048]{1,0:T(8,128)(2,1)S(1)} %get-tuple-element.73.mine_ref, bf16[128,2048]{1,0:T(8,128)(2,1)S(1)} %collective-permute-done.36.other_ref, ...), custom_call_target="tpu_custom_call", output_to_operand_aliasing={{}: (4, {})} | custom-call | flops 1073741824 | bytes 5767168 | tf_op jit(solution)/shard_map/spread/pallas_call | solution.py:342
  199.4 3.9 %spread.6.rest_0_ = bf16[1024,7168]{1,0:T(8,128)(2,1)} custom-call(s32[8]{0:T(128)S(1)} %fusion.slot_ref, bf16[1024,256]{1,0:T(8,128)(2,1)S(1)} %add.112.basis_ref, bf16[128,2048]{1,0:T(8,128)(2,1)S(1)} %get-tuple-element.72.mine_ref, bf16[128,2048]{1,0:T(8,128)(2,1)S(1)} %collective-permute-done.35.other_ref, ...), custom_call_target="tpu_custom_call", output_to_operand_aliasing={{}: (4, {})} | custom-call | flops 1073741824 | bytes 5767168 | tf_op jit(solution)/shard_map/spread/pallas_call | solution.py:342
  (155 shorter events, 75.4 us)
Async XLA Ops:
  2.6 22.7 %collective-permute-start.9 = (f32[8,128]{1,0:T(8,128)S(1)}, f32[8,128]{1,0:T(8,128)S(1)}, u32[]{:S(2)}, u32[]{:S(2)}) collective-permute-start(f32[8,128]{1,0:T(8,128)S(1)} %broadcast_in_dim.4), channel_id=1, source_target_pairs={{0,4},{4,0},{8,12},{12,8},{16,20},{20,16},{24,28},{28,24},{1,5},{5... | collective-permute-start | bytes 12296 | tf_op jit(solution)/shard_map/ppermute | solution.py:424
  5.7 51.9 %collective-permute-start.8 = (bf16[64,7168]{1,0:T(8,128)(2,1)S(1)}, bf16[64,7168]{1,0:T(8,128)(2,1)S(1)}, u32[]{:S(2)}, u32[]{:S(2)}) collective-permute-start(bf16[64,7168]{1,0:T(8,128)(2,1)S(1)} %pad_maximum_fusion), channel_id=1, source_target_pairs={{0,8},{4,12},{24,16},{28,20},{1,9},{5,13},{25,17},{29,21},{2,10},{... | collective-permute-start | bytes 2752520 | tf_op jit(solution)/shard_map/ppermute | solution.py:432
  20.5 18.5 %collective-permute-start.2 = (bf16[256,512]{1,0:T(8,128)(2,1)S(1)}, bf16[256,512]{1,0:T(8,128)(2,1)S(1)}, u32[]{:S(2)}, u32[]{:S(2)}) collective-permute-start(bf16[256,512]{1,0:T(8,128)(2,1)S(1)} %project.3), channel_id=1, source_target_pairs={{0,2},{1,3},{2,0},{3,1},{4,6},{5,7},{6,4},{7,5},{8,10},{9,11},{10,... | collective-permute-start | bytes 786440 | tf_op jit(solution)/shard_map/ppermute | solution.py:417
  23.7 16.0 %collective-permute-start.4 = (bf16[256,512]{1,0:T(8,128)(2,1)S(1)}, bf16[256,512]{1,0:T(8,128)(2,1)S(1)}, u32[]{:S(2)}, u32[]{:S(2)}) collective-permute-start(bf16[256,512]{1,0:T(8,128)(2,1)S(1)} %project.4), channel_id=1, source_target_pairs={{0,1},{1,0},{2,3},{3,2},{4,5},{5,4},{6,7},{7,6},{8,9},{9,8},{10,11... | collective-permute-start | bytes 786440 | tf_op jit(solution)/shard_map/ppermute | solution.py:417
  41.5 15.9 %collective-permute-start.7 = (bf16[256,512]{1,0:T(8,128)(2,1)S(1)}, bf16[256,512]{1,0:T(8,128)(2,1)S(1)}, u32[]{:S(2)}, u32[]{:S(2)}) collective-permute-start(bf16[256,512]{1,0:T(8,128)(2,1)S(1)} %add_convert_fusion.1), channel_id=1, source_target_pairs={{0,1},{1,0},{2,3},{3,2},{4,5},{5,4},{6,7},{7,6},{8,9},{9,8},{10,11... | collective-permute-start | bytes 786440 | tf_op jit(solution)/shard_map/ppermute | solution.py:417
  76.2 15.9 %collective-permute-start.28 = (bf16[128,2048]{1,0:T(8,128)(2,1)S(1)}, bf16[128,2048]{1,0:T(8,128)(2,1)S(1)}, u32[]{:S(2)}, u32[]{:S(2)}) collective-permute-start(bf16[128,2048]{1,0:T(8,128)(2,1)S(1)} %add.108.own_ref), channel_id=1, source_target_pairs={{0,8},{4,12},{24,16},{28,20},{1,9},{5,13},{25,17},{29,21},{2,10},{... | collective-permute-start | bytes 1572872 | tf_op jit(solution)/shard_map/ppermute | solution.py:454
  80.0 23.3 %collective-permute-start.23 = (bf16[128,2048]{1,0:T(8,128)(2,1)S(1)}, bf16[128,2048]{1,0:T(8,128)(2,1)S(1)}, u32[]{:S(2)}, u32[]{:S(2)}) collective-permute-start(bf16[128,2048]{1,0:T(8,128)(2,1)S(1)} %add.106.own_ref), channel_id=1, source_target_pairs={{0,8},{4,12},{24,16},{28,20},{1,9},{5,13},{25,17},{29,21},{2,10},{... | collective-permute-start | bytes 1572872 | tf_op jit(solution)/shard_map/ppermute | solution.py:454
  86.1 39.0 %collective-permute-start.12 = (bf16[128,1024]{1,0:T(8,128)(2,1)}, bf16[128,1024]{1,0:T(8,128)(2,1)}, u32[]{:S(2)}, u32[]{:S(2)}) collective-permute-start(bf16[128,1024]{1,0:T(8,128)(2,1)} %get-tuple-element.47), channel_id=1, source_target_pairs={{0,4},{4,0},{8,12},{12,8},{16,20},{20,16},{24,28},{28,24},{1,5},{5... | collective-permute-start | bytes 786440 | tf_op jit(solution)/shard_map/ppermute | solution.py:453
  86.4 27.7 %collective-permute-start.18 = (bf16[128,2048]{1,0:T(8,128)(2,1)S(1)}, bf16[128,2048]{1,0:T(8,128)(2,1)S(1)}, u32[]{:S(2)}, u32[]{:S(2)}) collective-permute-start(bf16[128,2048]{1,0:T(8,128)(2,1)S(1)} %add.104.own_ref), channel_id=1, source_target_pairs={{0,8},{4,12},{24,16},{28,20},{1,9},{5,13},{25,17},{29,21},{2,10},{... | collective-permute-start | bytes 1572872 | tf_op jit(solution)/shard_map/ppermute | solution.py:454
  92.1 23.4 %collective-permute-start.29 = (bf16[64,2048]{1,0:T(8,128)(2,1)S(1)}, bf16[64,2048]{1,0:T(8,128)(2,1)S(1)}, u32[]{:S(2)}, u32[]{:S(2)}) collective-permute-start(bf16[64,2048]{1,0:T(8,128)(2,1)S(1)} %slice_add_fusion), channel_id=1, source_target_pairs={{8,16},{12,20},{16,8},{20,12},{9,17},{13,21},{17,9},{21,13},{10,18... | collective-permute-start | bytes 786440 | tf_op jit(solution)/shard_map/ppermute | solution.py:455
  104.1 28.4 %collective-permute-start.24 = (bf16[64,2048]{1,0:T(8,128)(2,1)}, bf16[64,2048]{1,0:T(8,128)(2,1)}, u32[]{:S(2)}, u32[]{:S(2)}) collective-permute-start(bf16[64,2048]{1,0:T(8,128)(2,1)} %slice_add_fusion.1), channel_id=1, source_target_pairs={{8,16},{12,20},{16,8},{20,12},{9,17},{13,21},{17,9},{21,13},{10,18... | collective-permute-start | bytes 786440 | tf_op jit(solution)/shard_map/ppermute | solution.py:455
  114.9 21.0 %collective-permute-start.19 = (bf16[64,2048]{1,0:T(8,128)(2,1)}, bf16[64,2048]{1,0:T(8,128)(2,1)S(1)}, u32[]{:S(2)}, u32[]{:S(2)}) collective-permute-start(bf16[64,2048]{1,0:T(8,128)(2,1)} %slice_add_fusion.2), channel_id=1, source_target_pairs={{8,16},{12,20},{16,8},{20,12},{9,17},{13,21},{17,9},{21,13},{10,18... | collective-permute-start | bytes 786440 | tf_op jit(solution)/shard_map/ppermute | solution.py:455
  117.6 21.9 %collective-permute-start.30 = (bf16[64,2048]{1,0:T(8,128)(2,1)}, bf16[64,2048]{1,0:T(8,128)(2,1)}, u32[]{:S(2)}, u32[]{:S(2)}) collective-permute-start(bf16[64,2048]{1,0:T(8,128)(2,1)} %get-tuple-element.61.near_ref), channel_id=1, source_target_pairs={{8,16},{12,20},{16,8},{20,12},{9,17},{13,21},{17,9},{21,13},{10,18... | collective-permute-start | bytes 786440 | tf_op jit(solution)/shard_map/ppermute | solution.py:459
  120.9 24.3 %collective-permute-start.32 = (bf16[1024,256]{1,0:T(8,128)(2,1)}, bf16[1024,256]{1,0:T(8,128)(2,1)}, u32[]{:S(2)}, u32[]{:S(2)}) collective-permute-start(bf16[1024,256]{1,0:T(8,128)(2,1)} %dynamic-slice_select_fusion), channel_id=1, source_target_pairs={{0,1},{4,5},{9,8},{13,12},{18,19},{22,23},{27,26},{31,30}} | collective-permute-start | bytes 1572872 | tf_op jit(solution)/shard_map/ppermute | solution.py:446
  126.3 18.2 %collective-permute-start.13 = (bf16[128,1024]{1,0:T(8,128)(2,1)S(1)}, bf16[128,1024]{1,0:T(8,128)(2,1)S(1)}, u32[]{:S(2)}, u32[]{:S(2)}) collective-permute-start(bf16[128,1024]{1,0:T(8,128)(2,1)S(1)} %add.102.own_ref), channel_id=1, source_target_pairs={{0,8},{4,12},{24,16},{28,20},{1,9},{5,13},{25,17},{29,21},{2,10},{... | collective-permute-start | bytes 786440 | tf_op jit(solution)/shard_map/ppermute | solution.py:454
  140.5 17.9 %collective-permute-start.31 = (bf16[128,2048]{1,0:T(8,128)(2,1)S(1)}, bf16[128,2048]{1,0:T(8,128)(2,1)S(1)}, u32[]{:S(2)}, u32[]{:S(2)}) collective-permute-start(bf16[128,2048]{1,0:T(8,128)(2,1)S(1)} %pad_maximum_fusion.3), channel_id=1, source_target_pairs={{8,0},{12,4},{16,24},{20,28},{9,1},{13,5},{17,25},{21,29},{10,2},{... | collective-permute-start | bytes 1572872 | tf_op jit(solution)/shard_map/ppermute | solution.py:460
  141.9 27.8 %collective-permute-start.26 = (bf16[128,2048]{1,0:T(8,128)(2,1)S(1)}, bf16[128,2048]{1,0:T(8,128)(2,1)S(1)}, u32[]{:S(2)}, u32[]{:S(2)}) collective-permute-start(bf16[128,2048]{1,0:T(8,128)(2,1)S(1)} %pad_maximum_fusion.2), channel_id=1, source_target_pairs={{8,0},{12,4},{16,24},{20,28},{9,1},{13,5},{17,25},{21,29},{10,2},{... | collective-permute-start | bytes 1572872 | tf_op jit(solution)/shard_map/ppermute | solution.py:460
  143.2 35.6 %collective-permute-start.21 = (bf16[128,2048]{1,0:T(8,128)(2,1)S(1)}, bf16[128,2048]{1,0:T(8,128)(2,1)S(1)}, u32[]{:S(2)}, u32[]{:S(2)}) collective-permute-start(bf16[128,2048]{1,0:T(8,128)(2,1)S(1)} %pad_maximum_fusion.1), channel_id=1, source_target_pairs={{8,0},{12,4},{16,24},{20,28},{9,1},{13,5},{17,25},{21,29},{10,2},{... | collective-permute-start | bytes 1572872 | tf_op jit(solution)/shard_map/ppermute | solution.py:460
  144.5 18.0 %collective-permute-start.14 = (bf16[64,1024]{1,0:T(8,128)(2,1)S(1)}, bf16[64,1024]{1,0:T(8,128)(2,1)S(1)}, u32[]{:S(2)}, u32[]{:S(2)}) collective-permute-start(bf16[64,1024]{1,0:T(8,128)(2,1)S(1)} %slice_add_fusion.3), channel_id=1, source_target_pairs={{8,16},{12,20},{16,8},{20,12},{9,17},{13,21},{17,9},{21,13},{10,18... | collective-permute-start | bytes 393224 | tf_op jit(solution)/shard_map/ppermute | solution.py:455
  146.6 34.8 %collective-permute-start.33 = (bf16[1024,256]{1,0:T(8,128)(2,1)S(1)}, bf16[1024,256]{1,0:T(8,128)(2,1)S(1)}, u32[]{:S(2)}, u32[]{:S(2)}) collective-permute-start(bf16[1024,256]{1,0:T(8,128)(2,1)S(1)} %fusion.6), channel_id=1, source_target_pairs={{0,2},{1,3},{4,6},{5,7},{9,11},{8,10},{13,15},{12,14},{18,16},{19,... | collective-permute-start | bytes 1572872 | tf_op jit(solution)/shard_map/ppermute | solution.py:446
  162.5 29.0 %collective-permute-start.37 = (bf16[128,2048]{1,0:T(8,128)(2,1)S(1)}, bf16[128,2048]{1,0:T(8,128)(2,1)S(1)}, u32[]{:S(2)}, u32[]{:S(2)}) collective-permute-start(bf16[128,2048]{1,0:T(8,128)(2,1)S(1)} %get-tuple-element.74.mine_ref), channel_id=1, source_target_pairs={{0,4},{4,0},{8,12},{12,8},{16,20},{20,16},{24,28},{28,24},{1,5},{5... | collective-permute-start | bytes 1572872 | tf_op jit(solution)/shard_map/ppermute | solution.py:464
  162.8 17.3 %collective-permute-start.15 = (bf16[64,1024]{1,0:T(8,128)(2,1)S(1)}, bf16[64,1024]{1,0:T(8,128)(2,1)S(1)}, u32[]{:S(2)}, u32[]{:S(2)}) collective-permute-start(bf16[64,1024]{1,0:T(8,128)(2,1)S(1)} %get-tuple-element.49.near_ref), channel_id=1, source_target_pairs={{8,16},{12,20},{16,8},{20,12},{9,17},{13,21},{17,9},{21,13},{10,18... | collective-permute-start | bytes 393224 | tf_op jit(solution)/shard_map/ppermute | solution.py:459
  171.6 23.9 %collective-permute-start.36 = (bf16[128,2048]{1,0:T(8,128)(2,1)S(1)}, bf16[128,2048]{1,0:T(8,128)(2,1)S(1)}, u32[]{:S(2)}, u32[]{:S(2)}) collective-permute-start(bf16[128,2048]{1,0:T(8,128)(2,1)S(1)} %get-tuple-element.73.mine_ref), channel_id=1, source_target_pairs={{0,4},{4,0},{8,12},{12,8},{16,20},{20,16},{24,28},{28,24},{1,5},{5... | collective-permute-start | bytes 1572872 | tf_op jit(solution)/shard_map/ppermute | solution.py:464
  180.1 19.3 %collective-permute-start.35 = (bf16[128,2048]{1,0:T(8,128)(2,1)S(1)}, bf16[128,2048]{1,0:T(8,128)(2,1)S(1)}, u32[]{:S(2)}, u32[]{:S(2)}) collective-permute-start(bf16[128,2048]{1,0:T(8,128)(2,1)S(1)} %get-tuple-element.72.mine_ref), channel_id=1, source_target_pairs={{0,4},{4,0},{8,12},{12,8},{16,20},{20,16},{24,28},{28,24},{1,5},{5... | collective-permute-start | bytes 1572872 | tf_op jit(solution)/shard_map/ppermute | solution.py:464
  (36 other events, 501.5 us)

commit v3 on v2

--- a/solution.py
+++ b/solution.py
@@ -22,7 +22,7 @@
 
 F32, BF16 = jnp.float32, jnp.bfloat16
 CORES = 2
-CHUNKS = (4, 4, 4, 2)
+CHUNKS = (3, 4, 4, 3)
 MIB = 1 << 20
 
 
@@ -74,12 +74,6 @@
         if value % w == 0:
             best = w
     return best
-
-
-def params(limit_mib):
-    return pltpu.CompilerParams(
-        dimension_semantics=("arbitrary",), vmem_limit_bytes=limit_mib * MIB
-    )
 
 
 def project_pieces(turned, act_hbm, out_ref, act_buf, act_sem, start):
@@ -151,7 +145,7 @@
             in_specs=[vmem, hbm],
             out_specs=vmem,
             scratch_shapes=scratch,
-            compiler_params=pltpu.CompilerParams(vmem_limit_bytes=16 * MIB),
+            compiler_params=pltpu.CompilerParams(vmem_limit_bytes=56 * MIB),
             cost_estimate=estimate,
             name="project",
         )(source, activations)
@@ -161,48 +155,91 @@
         in_specs=[pl.BlockSpec(memory_space=pltpu.SMEM), hbm, hbm],
         out_specs=[vmem, vmem],
         scratch_shapes=[pltpu.VMEM((depth, rank), BF16), pltpu.SemaphoreType.DMA, *scratch],
-        compiler_params=pltpu.CompilerParams(vmem_limit_bytes=16 * MIB),
+        compiler_params=pltpu.CompilerParams(vmem_limit_bytes=56 * MIB),
         cost_estimate=estimate,
         name="project_first",
     )(slots, source, activations)
 
 
-def gradient_kernel(*refs):
-    *lefts, grads_ref, keep_ref, give_ref = refs
-    total, at = None, 0
-    for left in lefts:
-        size = left.shape[1]
-        term = jnp.dot(left[...], grads_ref[at : at + size, :], preferred_element_type=F32)
-        total = term if total is None else total + term
-        at += size
-    rows = keep_ref.shape[0]
-    keep_ref[...] = total[:rows].astype(BF16)
-    give_ref[...] = total[rows:].astype(BF16)
-
-
-def gradient_chunk(lefts, out_grads, start, width):
+VMEM = pl.BlockSpec(memory_space=pltpu.VMEM)
+SMEM = pl.BlockSpec(memory_space=pltpu.SMEM)
+HBM = pl.BlockSpec(memory_space=pltpu.HBM)
+
+
+def small(limit_mib):
+    return pltpu.CompilerParams(vmem_limit_bytes=limit_mib * MIB)
+
+
+def load_kernel(start, source, out_ref, sem):
+    parts = sem.shape[0]
+    size = out_ref.shape[0] // parts
+    copies = [
+        pltpu.make_async_copy(
+            source.at[pl.ds(start + i * size, size)], out_ref.at[pl.ds(i * size, size)], sem.at[i]
+        )
+        for i in range(parts)
+    ]
+    for copy in copies:
+        copy.start()
+    for copy in copies:
+        copy.wait()
+
+
+def load_rows(source, start, count):
+    return pl.pallas_call(
+        functools.partial(load_kernel, start),
+        out_shape=jax.ShapeDtypeStruct((count, source.shape[1]), source.dtype),
+        in_specs=[HBM],
+        out_specs=VMEM,
+        scratch_shapes=[pltpu.SemaphoreType.DMA((count // 128,))],
+        compiler_params=small(16),
+        cost_estimate=pl.CostEstimate(
+            flops=count * 10**6, bytes_accessed=4 * count * source.shape[1], transcendentals=0
+        ),
+        name="load",
+    )(source)
+
+
+def gradient_kernel(start, tile, pieces, *refs):
+    lefts, grads = refs[:pieces], refs[pieces:-2]
+    keep_ref, give_ref = refs[-2:]
+    rows, width = keep_ref.shape
+
+    def body(i, _):
+        at = pl.multiple_of(i * tile, tile)
+        total, piece, row = None, 0, 0
+        for left in lefts:
+            count = left.shape[1]
+            if row == grads[piece].shape[0]:
+                piece, row = piece + 1, 0
+            term = jnp.dot(
+                left[...],
+                grads[piece][row : row + count, pl.ds(start + at, tile)],
+                preferred_element_type=F32,
+            )
+            row += count
+            total = term if total is None else total + term
+        keep_ref[:, pl.ds(at, tile)] = total[:rows].astype(BF16)
+        give_ref[:, pl.ds(at, tile)] = total[rows:].astype(BF16)
+        return 0
+
+    lax.fori_loop(0, width // tile, body, 0)
+
+
+def gradient_chunk(lefts, grads, start, width):
     rank = lefts[0].shape[0]
-    tokens = out_grads.shape[0]
-    tile = pick(width, 512)
-    while start % tile:
-        tile -= 128
+    tokens = sum(piece.shape[0] for piece in grads)
     return pl.pallas_call(
-        gradient_kernel,
+        functools.partial(gradient_kernel, start, pick(width, 512), len(lefts)),
         out_shape=[jax.ShapeDtypeStruct((rank // 2, width), BF16)] * 2,
-        grid=(width // tile,),
-        in_specs=[
-            *(pl.BlockSpec(left.shape, lambda i: (0, 0)) for left in lefts),
-            pl.BlockSpec((tokens, tile), lambda i: (0, start // tile + i)),
-        ],
-        out_specs=[pl.BlockSpec((rank // 2, tile), lambda i: (0, i))] * 2,
-        compiler_params=params(44),
+        in_specs=[VMEM] * (len(lefts) + len(grads)),
+        out_specs=[VMEM, VMEM],
+        compiler_params=small(4),
         cost_estimate=pl.CostEstimate(
-            flops=2 * rank * tokens * width,
-            bytes_accessed=2 * (rank * tokens + tokens * width + rank * width),
-            transcendentals=0,
+            flops=2 * rank * tokens * width, bytes_accessed=4 * rank * width, transcendentals=0
         ),
         name="gradient",
-    )(*lefts, out_grads)
+    )(*lefts, *grads)
 
 
 def moments(gradient, first, second):
@@ -212,113 +249,96 @@
     return new_first, new_second, update
 
 
-def hub_kernel(scale_ref, own_ref, outer_ref, far_ref, m_ref, v_ref, mv_ref, update_ref, sum_ref):
-    rows = m_ref.shape[0]
-    total = own_ref[...].astype(F32) + outer_ref[...].astype(F32) + far_ref[...].astype(F32)
+def hub_kernel(
+    start, scale_ref, own_ref, came_ref, far_ref, m_ref, v_ref, mv_ref, near_ref, sum_ref, mine_ref
+):
+    rows, width = mine_ref.shape
+    total = own_ref[: 2 * rows].astype(F32) + came_ref[: 2 * rows].astype(F32)
+    total = total + far_ref[...].astype(F32)
     sum_ref[...] = total[:rows].astype(BF16)
+    mine_ref[...] = total[rows:]
     gradient = total * scale_ref[0, 0]
-    mv = mv_ref[...].astype(F32)
-    update_ref[:rows] = moments(gradient[:rows], mv[:rows], mv[rows:])[2].astype(BF16)
-    update_ref[rows:] = moments(gradient[rows:], m_ref[...], v_ref[...])[2].astype(BF16)
-
-
-def hub_chunk(scale, own, outer, far, first, second, moved, start):
-    rows = first.shape[0]
-    width = own.shape[1]
-    tile = pick(width, 1024)
-    while start % tile:
-        tile -= 128
-    there = lambda i: (0, i)
-    shifted = lambda i: (0, start // tile + i)
-    two = pl.BlockSpec((2 * rows, tile), there)
+    cols = slice(start, start + width)
+    mv = mv_ref[:, cols].astype(F32)
+    near_ref[:rows] = moments(gradient[:rows], mv[:rows], mv[rows:])[2].astype(BF16)
+    near_ref[rows:] = moments(gradient[rows:], m_ref[:, cols], v_ref[:, cols])[2].astype(BF16)
+
+
+def hub_chunk(scale, own, came, far, first, second, moved, start):
+    rows, width = first.shape[0], own.shape[1]
     return pl.pallas_call(
-        hub_kernel,
+        functools.partial(hub_kernel, start),
         out_shape=[
             jax.ShapeDtypeStruct((2 * rows, width), BF16),
             jax.ShapeDtypeStruct((rows, width), BF16),
+            jax.ShapeDtypeStruct((rows, width), F32),
         ],
-        grid=(width // tile,),
-        in_specs=[
-            pl.BlockSpec(memory_space=pltpu.SMEM),
-            two,
-            two,
-            two,
-            pl.BlockSpec((rows, tile), shifted),
-            pl.BlockSpec((rows, tile), shifted),
-            pl.BlockSpec((2 * rows, tile), shifted),
-        ],
-        out_specs=[two, pl.BlockSpec((rows, tile), there)],
-        compiler_params=params(8),
+        in_specs=[SMEM] + [VMEM] * 6,
+        out_specs=[VMEM] * 3,
+        compiler_params=small(4),
         cost_estimate=pl.CostEstimate(
-            flops=40 * rows * width * 100, bytes_accessed=30 * rows * width, transcendentals=0
+            flops=4000 * rows * width, bytes_accessed=30 * rows * width, transcendentals=0
         ),
         name="hub",
-    )(scale, own, outer, far, first, second, moved)
+    )(scale, own, came, far, first, second, moved)
 
 
 def settle_kernel(
-    scale_ref, hub_ref, own_ref, outer_ref, far_ref, m_ref, v_ref, near_ref, across_ref, sent_ref, *rest
+    start, scale_ref, hub_ref, mine_ref, m_ref, v_ref, near_ref, across_ref, sent_ref, *rest
 ):
-    all_ref, first_ref, second_ref = rest[-3:]
-    rows = m_ref.shape[0]
+    all_ref, first_out, second_out, first_buf, second_buf, sem = rest[-6:]
+    rows, width = mine_ref.shape
+    cols = slice(start, start + width)
     hub = hub_ref[0, 0] == 1
-    total = own_ref[...].astype(F32) + outer_ref[...].astype(F32) + far_ref[...].astype(F32)
-    total = jnp.where(hub, total, sent_ref[:rows].astype(F32))
-    new_first, new_second, update = moments(total * scale_ref[0, 0], m_ref[...], v_ref[...])
-    first_ref[...] = new_first
-    second_ref[...] = new_second
+    total = jnp.where(hub, mine_ref[...], sent_ref[:rows].astype(F32))
+    new_first, new_second, update = moments(
+        total * scale_ref[0, 0], m_ref[:, cols], v_ref[:, cols]
+    )
+    first_buf[...] = new_first
+    second_buf[...] = new_second
+    copies = [
+        pltpu.make_async_copy(first_buf, first_out.at[:, pl.ds(start, width)], sem.at[0]),
+        pltpu.make_async_copy(second_buf, second_out.at[:, pl.ds(start, width)], sem.at[1]),
+    ]
+    for copy in copies:
+        copy.start()
     all_ref[:rows] = jnp.where(hub, near_ref[:rows], update.astype(BF16))
     all_ref[rows : 2 * rows] = jnp.where(hub, update.astype(BF16), sent_ref[rows : 2 * rows])
     all_ref[2 * rows :] = jnp.where(hub, across_ref[...], sent_ref[2 * rows :])
-
-
-def settle_chunk(scale, hub, own, outer, far, first, second, near, across, sent, start, results):
+    for copy in copies:
+        copy.wait()
+
+
+def settle_chunk(scale, hub, mine, first, second, near, across, sent, start, results):
     rows, full = first.shape
-    width = own.shape[1]
-    tile = pick(width, 1024)
-    while start % tile:
-        tile -= 128
-    there = lambda i: (0, i)
-    second_rows = lambda i: (1, i)
-    shifted = lambda i: (0, start // tile + i)
-    one = pl.BlockSpec((rows, tile), second_rows)
-    moment = pl.BlockSpec((rows, tile), shifted)
-    smem = pl.BlockSpec(memory_space=pltpu.SMEM)
-    whole = [pl.BlockSpec(memory_space=pl.ANY)] * len(results)
+    width = mine.shape[1]
     return pl.pallas_call(
-        settle_kernel,
+        functools.partial(settle_kernel, start),
         out_shape=[
             jax.ShapeDtypeStruct((4 * rows, width), BF16),
             jax.ShapeDtypeStruct((rows, full), F32),
             jax.ShapeDtypeStruct((rows, full), F32),
         ],
-        grid=(width // tile,),
-        in_specs=[
-            smem,
-            smem,
-            one,
-            one,
-            one,
-            moment,
-            moment,
-            pl.BlockSpec((2 * rows, tile), there),
-            pl.BlockSpec((2 * rows, tile), there),
-            pl.BlockSpec((4 * rows, tile), there),
-            *whole,
+        in_specs=[SMEM, SMEM] + [VMEM] * 6 + [HBM] * len(results),
+        out_specs=[VMEM, HBM, HBM],
+        input_output_aliases={8: 1, 9: 2} if results else {},
+        scratch_shapes=[
+            pltpu.VMEM((rows, width), F32),
+            pltpu.VMEM((rows, width), F32),
+            pltpu.SemaphoreType.DMA((2,)),
         ],
-        out_specs=[pl.BlockSpec((4 * rows, tile), there), moment, moment],
-        input_output_aliases={10: 1, 11: 2} if results else {},
-        compiler_params=params(8),
+        compiler_params=small(4),
         cost_estimate=pl.CostEstimate(
-            flops=30 * rows * width * 100, bytes_accessed=40 * rows * width, transcendentals=0
+            flops=4000 * rows * width, bytes_accessed=40 * rows * width, transcendentals=0
         ),
         name="settle",
-    )(scale, hub, own, outer, far, first, second, near, across, sent, *results)
-
-
-def spread_kernel(slot_ref, basis_ref, mine_ref, other_ref, *rest):
-    out_ref, updates = rest[-2:]
+    )(scale, hub, mine, first, second, near, across, sent, *results)
+
+
+def spread_kernel(start, slot_ref, basis_ref, mine_ref, other_ref, *rest):
+    out_ref, updates, buf, sem = rest[-4:]
     blocks = slot_ref.shape[0]
+    width = mine_ref.shape[1]
     rows = 2 * mine_ref.shape[0] // blocks
     side = blocks // 2
     for n in range(blocks):
@@ -327,35 +347,39 @@
         updates[n * rows : (n + 1) * rows, :] = jnp.where(
             at < side, mine_ref[pl.ds(inner, rows), :], other_ref[pl.ds(inner, rows), :]
         )
-    out_ref[...] = jnp.dot(
-        basis_ref[...], updates[...], preferred_element_type=F32
-    ).astype(BF16)
+    steps = sem.shape[0]
+    size = basis_ref.shape[0] // steps
+    copies = []
+    for i in range(steps):
+        part = pl.ds(i * size, size)
+        buf[part, :] = jnp.dot(
+            basis_ref[part, :], updates[...], preferred_element_type=F32
+        ).astype(BF16)
+        copies.append(
+            pltpu.make_async_copy(
+                buf.at[part], out_ref.at[part, pl.ds(start, width)], sem.at[i]
+            )
+        )
+        copies[-1].start()
+    for copy in copies:
+        copy.wait()
 
 
 def spread_chunk(slots, basis_rows, mine, other, start, full, results):
     count, rank = basis_rows.shape
     width = mine.shape[1]
-    tile = pick(width, 512)
-    while start % tile:
-        tile -= 128
-    there = lambda i, s: (0, i)
     return pl.pallas_call(
-        spread_kernel,
+        functools.partial(spread_kernel, start),
         out_shape=jax.ShapeDtypeStruct((count, full), BF16),
-        grid_spec=pltpu.PrefetchScalarGridSpec(
-            num_scalar_prefetch=1,
-            grid=(width // tile,),
-            in_specs=[
-                pl.BlockSpec((count, rank), lambda i, s: (0, 0)),
-                pl.BlockSpec((rank // 2, tile), there),
-                pl.BlockSpec((rank // 2, tile), there),
-                *([pl.BlockSpec(memory_space=pl.ANY)] * len(results)),
-            ],
-            out_specs=pl.BlockSpec((count, tile), lambda i, s: (0, start // tile + i)),
-            scratch_shapes=[pltpu.VMEM((rank, tile), BF16)],
-        ),
+        in_specs=[SMEM] + [VMEM] * 3 + [HBM] * len(results),
+        out_specs=HBM,
+        scratch_shapes=[
+            pltpu.VMEM((rank, width), BF16),
+            pltpu.VMEM((count, width), BF16),
+            pltpu.SemaphoreType.DMA((4 if count % 64 == 0 else 1,)),
+        ],
         input_output_aliases={4: 0} if results else {},
-        compiler_params=params(12),
+        compiler_params=small(9),
         cost_estimate=pl.CostEstimate(
             flops=2 * count * rank * width,
             bytes_accessed=2 * (count * rank + rank * width + count * width),
@@ -398,6 +422,11 @@
     is_hub = ((block_chip == 1) | (block_chip == 2)).astype(jnp.int32)
     slots = ((block % CORES) ^ core).astype(jnp.int32) * chips + 2 * far + is_hub
 
+    row_count = basis.shape[0] * tensor_count // data_count
+    per_owner = data_count // tensor_count
+    owner = data_index // per_owner
+    basis_rows = lax.dynamic_slice_in_dim(basis, data_index % per_owner * row_count, row_count, 0)
+    basis_rows = jnp.where(tensor_index == owner, basis_rows, jnp.zeros_like(basis_rows))
     bits = [1 << b for b in range(tensor_count.bit_length() - 1)]
     parts = []
     source = basis
@@ -431,12 +460,15 @@
 
     moved = lax.ppermute(jnp.concatenate([first_moment, second_moment]).astype(BF16), "dp", inward)
     lefts, moved, scale = lax.optimization_barrier((lefts, moved, scale))
-
-    row_count = basis.shape[0] * tensor_count // data_count
-    per_owner = data_count // tensor_count
-    owner = data_index // per_owner
-    basis_rows = lax.dynamic_slice_in_dim(basis, data_index % per_owner * row_count, row_count, 0)
-    basis_rows = jnp.where(tensor_index == owner, basis_rows, jnp.zeros_like(basis_rows))
+    out_grads, basis_rows, hub, slots = lax.optimization_barrier(
+        (out_grads, basis_rows, hub, slots)
+    )
+    grads = []
+    spans = token_pieces(tokens)
+    cut = spans[2][0]
+    for start, count in ((0, cut), (cut, tokens - cut)):
+        grads.append(load_rows(out_grads, start, count))
+
     for bit in bits:
         pairs = [
             (d * tensor_count + (d // per_owner ^ s), d * tensor_count + (d // per_owner ^ s ^ bit))
@@ -449,17 +481,17 @@
     starts = [unit * sum(CHUNKS[:i]) for i in range(len(CHUNKS))]
     settled, spread = (), ()
     for start, size in zip(starts, CHUNKS):
-        keep, give = gradient_chunk(lefts, out_grads, start, unit * size)
+        keep, give = gradient_chunk(lefts, grads, start, unit * size)
         mine = keep + lax.ppermute(give, "dp", sibling)
         came = lax.ppermute(mine, "dp", inward)
         across = lax.ppermute(mine[2 * rows :] + came[2 * rows :], "dp", middle)
-        near, total = hub_chunk(
+        near, total, held = hub_chunk(
             scale, mine, came, across, first_moment, second_moment, moved, start
         )
         beyond = lax.ppermute(near, "dp", middle)
         sent = lax.ppermute(jnp.concatenate([total, near[rows:], beyond]), "dp", outward)
         updates, *settled = settle_chunk(
-            scale, hub, mine, came, across, first_moment, second_moment, near, beyond, sent, start, settled
+            scale, hub, held, first_moment, second_moment, near, beyond, sent, start, settled
         )
         other = lax.ppermute(updates, "dp", sibling)
         spread = (spread_chunk(slots, basis_rows, updates, other, start, full, spread),)

time: 209 us -> 204 us (0.976); the launches traced: 206 us -> 203 us
  waiting for transfers between devices: 70.2 us -> 89.4 us
  local copies, waits for them, and re-layouts: 14 us -> 1.28 us
  starting transfers between devices: 52 us -> 40.6 us
  Pallas kernels: 54 us -> 58.9 us
  other arithmetic: 13.6 us -> 10.5 us
    ppermute x4, waiting for transfers between devices: 30.5 us -> 43.7 us  [local_line(): lax.ppermute(jnp.concatenate([total, near[rows:], beyond]), 'dp', outward)]
    unnamed x44 -> x16, local copies, waits for them, and re-layouts: 11.9 us -> 0.04 us
    ppermute x4, waiting for transfers between devices: 23.2 us -> 33.6 us  [local_line(): came = lax.ppermute(mine, 'dp', inward)]
    pallas_call x3, Pallas kernels: 4.83 us -> 13.9 us  [project(): pl.pallas_call(functools.partial(project_kernel, start), out_shape=part,...]
    pallas_call x16 -> x18, Pallas kernels: 46 us -> 39.4 us  [the longest x2 11.7 us: load_rows(): pl.pallas_call(functools.partial(load_kernel, start), out_shape=jax.Shape...]
    ppermute x4, starting transfers between devices: 12 us -> 6.19 us  [local_line(): came = lax.ppermute(mine, 'dp', inward)]
    ppermute x2, starting transfers between devices: 7.97 us -> 3.79 us  [local_line(): basis_rows = basis_rows + lax.ppermute(basis_rows, ('dp', 'tensor'), pairs)]
    ppermute x3, waiting for transfers between devices: 3.92 us -> 0.01 us  [local_line(): normalizer = normalizer + lax.ppermute(normalizer, 'dp', pairs)]
  transfers between devices with their start and end apart: 38 -> 38, of which waited for: 12 -> 9; matrix products, arithmetic and copies ran while one was open for 7% -> 5% of each run, Pallas kernels for 22% -> 25%
where the time goes in v3:
time: 204 us; the launch traced here: 203 us
  waiting for transfers between devices  89.4 us (44%)
  Pallas kernels  58.9 us (29%)
  starting transfers between devices  40.6 us (20%)
  other arithmetic  10.5 us (5%)
  between operations  2.37 us (1%)
    ppermute x4, waiting for transfers between devices, local_line(): lax.ppermute(jnp.concatenate([total, near[rows:], beyond]), 'dp', outward)  43.7 us
    ppermute x4, waiting for transfers between devices, local_line(): came = lax.ppermute(mine, 'dp', inward)  33.6 us
    pallas_call x3, Pallas kernels, project(): pl.pallas_call(functools.partial(project_kernel, start), out_shape=part,...  13.9 us
    pallas_call x2, Pallas kernels, load_rows(): pl.pallas_call(functools.partial(load_kernel, start), out_shape=jax.Shape...  11.7 us
    pallas_call x4, Pallas kernels, spread_chunk(): pl.pallas_call(functools.partial(spread_kernel, start), out_shape=jax.Sha...  11.4 us
    pallas_call x4, Pallas kernels, gradient_chunk(): pl.pallas_call(functools.partial(gradient_kernel, start, pick(width, 512)...  11 us
    ppermute x8, waiting for transfers between devices, local_line(): got[i] = lax.ppermute(part, 'tensor', pairs)  10.6 us
    ppermute x8, starting transfers between devices, local_line(): got[i] = lax.ppermute(part, 'tensor', pairs)  9.63 us
  transfers between devices with their start and end apart: 38, of which 9 were waited for; matrix products, arithmetic and copies ran while one was open for 5% of the time, Pallas kernels for 25%

profile of v3, /device:TPU:0, one launch (start us, length us, event | category | flops | bytes accessed | tf_op | source)
XLA Modules:
  0.0 203.0 jit_solution(11736057711480557698)
XLA Ops:
  5.8 4.5 %collective-permute-start.8 = (bf16[64,7168]{1,0:T(8,128)(2,1)S(1)}, bf16[64,7168]{1,0:T(8,128)(2,1)S(1)}, u32[]{:S(2)}, u32[]{:S(2)}) collective-permute-start(bf16[64,7168]{1,0:T(8,128)(2,1)S(1)} %pad_maximum_fusion), channel_id=1, source_target_pairs={{0,8},{4,12},{24,16},{28,20},{1,9},{5,13},{25,17},{29,21},{2,10},{... | collective-permute-start | bytes 2752520 | tf_op jit(solution)/shard_map/ppermute | solution.py:461
  11.0 5.6 %project_first.1 = (bf16[256,768]{1,0:T(8,128)(2,1)}, bf16[256,2048]{1,0:T(8,128)(2,1)}) custom-call(s32[8]{0:T(128)} %fusion.slot_ref, bf16[2048,256]{1,0:T(8,128)(2,1)} %basis_hbm.1, bf16[2304,2048]{1,0:T(8,128)(2,1)} %act_hbm.7), custom_call_target="tpu_custom_call" | custom-call | flops 805306368 | bytes 4587520 | tf_op jit(solution)/shard_map/project_first/pallas_call | solution.py:152
  16.6 4.7 %project.3 = bf16[256,512]{1,0:T(8,128)(2,1)} custom-call(bf16[256,2048]{1,0:T(8,128)(2,1)} %get-tuple-element.48.turned_ref, bf16[2304,2048]{1,0:T(8,128)(2,1)} %act_hbm.7), custom_call_target="tpu_custom_call" | custom-call | flops 536870912 | bytes 3407872 | tf_op jit(solution)/shard_map/project/pallas_call | solution.py:142
  22.9 4.6 %project.4 = bf16[256,512]{1,0:T(8,128)(2,1)} custom-call(bf16[256,2048]{1,0:T(8,128)(2,1)} %get-tuple-element.48.turned_ref, bf16[2304,2048]{1,0:T(8,128)(2,1)} %act_hbm.7), custom_call_target="tpu_custom_call" | custom-call | flops 536870912 | bytes 3407872 | tf_op jit(solution)/shard_map/project/pallas_call | solution.py:142
  29.1 4.6 %project.5 = bf16[256,512]{1,0:T(8,128)(2,1)} custom-call(bf16[256,2048]{1,0:T(8,128)(2,1)} %get-tuple-element.48.turned_ref, bf16[2304,2048]{1,0:T(8,128)(2,1)} %act_hbm.7), custom_call_target="tpu_custom_call" | custom-call | flops 536870912 | bytes 3407872 | tf_op jit(solution)/shard_map/project/pallas_call | solution.py:142
  35.1 6.4 %load.2.refs_4_ = bf16[1280,7168]{1,0:T(8,128)(2,1)S(1)} custom-call(bf16[2304,7168]{1,0:T(8,128)(2,1)} %source.1), custom_call_target="tpu_custom_call" | custom-call | flops 1280000000 | bytes 36700160 | tf_op jit(solution)/shard_map/load/pallas_call | solution.py:189
  42.3 3.1 %collective-permute-start.11 = (f32[8,128]{1,0:T(8,128)S(1)}, f32[8,128]{1,0:T(8,128)S(1)}, u32[]{:S(2)}, u32[]{:S(2)}) collective-permute-start(f32[8,128]{1,0:T(8,128)S(1)} %fusion.6), channel_id=1, source_target_pairs={{0,16},{4,20},{8,24},{12,28},{16,0},{20,4},{24,8},{28,12},{1,17},{... | collective-permute-start | bytes 12296 | tf_op jit(solution)/shard_map/ppermute | solution.py:453
  45.4 5.3 %load.3.refs_5_ = bf16[1024,7168]{1,0:T(8,128)(2,1)S(1)} custom-call(bf16[2304,7168]{1,0:T(8,128)(2,1)} %source.1), custom_call_target="tpu_custom_call" | custom-call | flops 1024000000 | bytes 29360128 | tf_op jit(solution)/shard_map/load/pallas_call | solution.py:189
  59.3 3.4 %collective-permute-done = bf16[256,768]{1,0:T(8,128)(2,1)S(1)} collective-permute-done((bf16[256,768]{1,0:T(8,128)(2,1)S(1)}, bf16[256,768]{1,0:T(8,128)(2,1)S(1)}, u32[]{:S(2)}, u32[]{:S(2)}) %collective-permute-start) | collective-permute-done | bytes 393248 | tf_op jit(solution)/shard_map/ppermute | solution.py:446
  64.4 3.9 %collective-permute-done.3 = bf16[256,512]{1,0:T(8,128)(2,1)S(1)} collective-permute-done((bf16[256,512]{1,0:T(8,128)(2,1)S(1)}, bf16[256,512]{1,0:T(8,128)(2,1)S(1)}, u32[]{:S(2)}, u32[]{:S(2)}) %collective-permute-start.3) | collective-permute-done | bytes 262176 | tf_op jit(solution)/shard_map/ppermute | solution.py:446
  68.6 3.3 %collective-permute-done.7 = bf16[256,512]{1,0:T(8,128)(2,1)S(1)} collective-permute-done((bf16[256,512]{1,0:T(8,128)(2,1)S(1)}, bf16[256,512]{1,0:T(8,128)(2,1)S(1)}, u32[]{:S(2)}, u32[]{:S(2)}) %collective-permute-start.7) | collective-permute-done | bytes 262176 | tf_op jit(solution)/shard_map/ppermute | solution.py:446
  72.1 2.3 %gradient.7 = (bf16[128,1536]{1,0:T(8,128)(2,1)S(1)}, bf16[128,1536]{1,0:T(8,128)(2,1)S(1)}) custom-call(bf16[256,768]{1,0:T(8,128)(2,1)S(1)} %multiply_convert_fusion.refs_0_, bf16[256,512]{1,0:T(8,128)(2,1)S(1)} %multiply_convert_fusion.3.refs_1_, bf16[256,512]{1,0:T(8,128)(2,1)S(1)} %multiply_convert_fusion.2.refs_2_, ...), custom_call_target="tpu_custom_call" | custom-call | flops 1811939328 | bytes 1572864 | tf_op jit(solution)/shard_map/gradient/pallas_call | solution.py:232
  74.4 3.1 %gradient.6 = (bf16[128,2048]{1,0:T(8,128)(2,1)S(1)}, bf16[128,2048]{1,0:T(8,128)(2,1)S(1)}) custom-call(bf16[256,768]{1,0:T(8,128)(2,1)S(1)} %multiply_convert_fusion.refs_0_, bf16[256,512]{1,0:T(8,128)(2,1)S(1)} %multiply_convert_fusion.3.refs_1_, bf16[256,512]{1,0:T(8,128)(2,1)S(1)} %multiply_convert_fusion.2.refs_2_, ...), custom_call_target="tpu_custom_call" | custom-call | flops 2415919104 | bytes 2097152 | tf_op jit(solution)/shard_map/gradient/pallas_call | solution.py:232
  78.1 3.1 %gradient.5 = (bf16[128,2048]{1,0:T(8,128)(2,1)S(1)}, bf16[128,2048]{1,0:T(8,128)(2,1)S(1)}) custom-call(bf16[256,768]{1,0:T(8,128)(2,1)S(1)} %multiply_convert_fusion.refs_0_, bf16[256,512]{1,0:T(8,128)(2,1)S(1)} %multiply_convert_fusion.3.refs_1_, bf16[256,512]{1,0:T(8,128)(2,1)S(1)} %multiply_convert_fusion.2.refs_2_, ...), custom_call_target="tpu_custom_call" | custom-call | flops 2415919104 | bytes 2097152 | tf_op jit(solution)/shard_map/gradient/pallas_call | solution.py:232
  81.4 2.4 %gradient.4 = (bf16[128,1536]{1,0:T(8,128)(2,1)S(1)}, bf16[128,1536]{1,0:T(8,128)(2,1)S(1)}) custom-call(bf16[256,768]{1,0:T(8,128)(2,1)S(1)} %multiply_convert_fusion.refs_0_, bf16[256,512]{1,0:T(8,128)(2,1)S(1)} %multiply_convert_fusion.3.refs_1_, bf16[256,512]{1,0:T(8,128)(2,1)S(1)} %multiply_convert_fusion.2.refs_2_, ...), custom_call_target="tpu_custom_call" | custom-call | flops 1811939328 | bytes 1572864 | tf_op jit(solution)/shard_map/gradient/pallas_call | solution.py:232
  91.0 5.0 %collective-permute-done.28.came_ref = bf16[128,1536]{1,0:T(8,128)(2,1)S(1)} collective-permute-done((bf16[128,1536]{1,0:T(8,128)(2,1)S(1)}, bf16[128,1536]{1,0:T(8,128)(2,1)S(1)}, u32[]{:S(2)}, u32[]{:S(2)}) %collective-permute-start.28) | collective-permute-done | bytes 393248 | tf_op jit(solution)/shard_map/ppermute | solution.py:486
  96.8 10.5 %collective-permute-done.23.came_ref = bf16[128,2048]{1,0:T(8,128)(2,1)S(1)} collective-permute-done((bf16[128,2048]{1,0:T(8,128)(2,1)S(1)}, bf16[128,2048]{1,0:T(8,128)(2,1)S(1)}, u32[]{:S(2)}, u32[]{:S(2)}) %collective-permute-start.23) | collective-permute-done | bytes 524320 | tf_op jit(solution)/shard_map/ppermute | solution.py:486
  108.1 18.0 %collective-permute-done.18.came_ref = bf16[128,2048]{1,0:T(8,128)(2,1)S(1)} collective-permute-done((bf16[128,2048]{1,0:T(8,128)(2,1)S(1)}, bf16[128,2048]{1,0:T(8,128)(2,1)S(1)}, u32[]{:S(2)}, u32[]{:S(2)}) %collective-permute-start.18) | collective-permute-done | bytes 524320 | tf_op jit(solution)/shard_map/ppermute | solution.py:486
  128.8 2.5 %collective-permute-start.32 = (bf16[1024,256]{1,0:T(8,128)(2,1)S(1)}, bf16[1024,256]{1,0:T(8,128)(2,1)S(1)}, u32[]{:S(2)}, u32[]{:S(2)}) collective-permute-start(bf16[1024,256]{1,0:T(8,128)(2,1)S(1)} %dynamic-slice_select_fusion), channel_id=1, source_target_pairs={{0,1},{4,5},{9,8},{13,12},{18,19},{22,23},{27,26},{31,30}} | collective-permute-start | bytes 1572872 | tf_op jit(solution)/shard_map/ppermute | solution.py:478
  143.3 42.9 %collective-permute-done.31.sent_ref = bf16[128,1536]{1,0:T(8,128)(2,1)S(1)} collective-permute-done((bf16[128,1536]{1,0:T(8,128)(2,1)S(1)}, bf16[128,1536]{1,0:T(8,128)(2,1)S(1)}, u32[]{:S(2)}, u32[]{:S(2)}) %collective-permute-start.31) | collective-permute-done | bytes 393248 | tf_op jit(solution)/shard_map/ppermute | solution.py:492
  191.4 2.6 %spread.4.rest_0_ = bf16[1024,7168]{1,0:T(8,128)(2,1)} custom-call(s32[8]{0:T(128)S(1)} %copy-done.2, bf16[1024,256]{1,0:T(8,128)(2,1)S(1)} %add.112.basis_ref, bf16[128,1536]{1,0:T(8,128)(2,1)S(1)} %get-tuple-element.90.mine_ref, bf16[128,1536]{1,0:T(8,128)(2,1)S(1)} %collective-permute-done.37.other_ref), custom_call_target="tpu_custom_call" | custom-call | flops 805306368 | bytes 4456448 | tf_op jit(solution)/shard_map/spread/pallas_call | solution.py:371
  194.1 3.1 %spread.5.rest_0_ = bf16[1024,7168]{1,0:T(8,128)(2,1)} custom-call(s32[8]{0:T(128)S(1)} %copy-done.2, bf16[1024,256]{1,0:T(8,128)(2,1)S(1)} %add.112.basis_ref, bf16[128,2048]{1,0:T(8,128)(2,1)S(1)} %get-tuple-element.89.mine_ref, bf16[128,2048]{1,0:T(8,128)(2,1)S(1)} %collective-permute-done.36.other_ref, ...), custom_call_target="tpu_custom_call", output_to_operand_aliasing={{}: (4, {})} | custom-call | flops 1073741824 | bytes 5767168 | tf_op jit(solution)/shard_map/spread/pallas_call | solution.py:371
  197.2 3.1 %spread.6.rest_0_ = bf16[1024,7168]{1,0:T(8,128)(2,1)} custom-call(s32[8]{0:T(128)S(1)} %copy-done.2, bf16[1024,256]{1,0:T(8,128)(2,1)S(1)} %add.112.basis_ref, bf16[128,2048]{1,0:T(8,128)(2,1)S(1)} %get-tuple-element.88.mine_ref, bf16[128,2048]{1,0:T(8,128)(2,1)S(1)} %collective-permute-done.35.other_ref, ...), custom_call_target="tpu_custom_call", output_to_operand_aliasing={{}: (4, {})} | custom-call | flops 1073741824 | bytes 5767168 | tf_op jit(solution)/shard_map/spread/pallas_call | solution.py:371
  200.3 2.6 %spread.7 = bf16[1024,7168]{1,0:T(8,128)(2,1)} custom-call(s32[8]{0:T(128)S(1)} %copy-done.2, bf16[1024,256]{1,0:T(8,128)(2,1)S(1)} %add.112.basis_ref, bf16[128,1536]{1,0:T(8,128)(2,1)S(1)} %get-tuple-element.87.mine_ref, bf16[128,1536]{1,0:T(8,128)(2,1)S(1)} %collective-permute-done.34.other_ref, ...), custom_call_target="tpu_custom_call", output_to_operand_aliasing={{}: (4, {})} | custom-call | flops 805306368 | bytes 4456448 | tf_op jit(solution)/shard_map/spread/pallas_call | solution.py:371
  (129 shorter events, 49.9 us)
Async XLA Ops:
  2.7 31.6 %collective-permute-start.9 = (f32[8,128]{1,0:T(8,128)S(1)}, f32[8,128]{1,0:T(8,128)S(1)}, u32[]{:S(2)}, u32[]{:S(2)}) collective-permute-start(f32[8,128]{1,0:T(8,128)S(1)} %broadcast_in_dim.4), channel_id=1, source_target_pairs={{0,4},{4,0},{8,12},{12,8},{16,20},{20,16},{24,28},{28,24},{1,5},{5... | collective-permute-start | bytes 12296 | tf_op jit(solution)/shard_map/ppermute | solution.py:453
  5.8 66.2 %collective-permute-start.8 = (bf16[64,7168]{1,0:T(8,128)(2,1)S(1)}, bf16[64,7168]{1,0:T(8,128)(2,1)S(1)}, u32[]{:S(2)}, u32[]{:S(2)}) collective-permute-start(bf16[64,7168]{1,0:T(8,128)(2,1)S(1)} %pad_maximum_fusion), channel_id=1, source_target_pairs={{0,8},{4,12},{24,16},{28,20},{1,9},{5,13},{25,17},{29,21},{2,10},{... | collective-permute-start | bytes 2752520 | tf_op jit(solution)/shard_map/ppermute | solution.py:461
  21.3 31.2 %collective-permute-start.2 = (bf16[256,512]{1,0:T(8,128)(2,1)}, bf16[256,512]{1,0:T(8,128)(2,1)}, u32[]{:S(2)}, u32[]{:S(2)}) collective-permute-start(bf16[256,512]{1,0:T(8,128)(2,1)} %project.3), channel_id=1, source_target_pairs={{0,2},{1,3},{2,0},{3,1},{4,6},{5,7},{6,4},{7,5},{8,10},{9,11},{10,... | collective-permute-start | bytes 786440 | tf_op jit(solution)/shard_map/ppermute | solution.py:446
  27.5 27.6 %collective-permute-start.4 = (bf16[256,512]{1,0:T(8,128)(2,1)}, bf16[256,512]{1,0:T(8,128)(2,1)}, u32[]{:S(2)}, u32[]{:S(2)}) collective-permute-start(bf16[256,512]{1,0:T(8,128)(2,1)} %project.4), channel_id=1, source_target_pairs={{0,1},{1,0},{2,3},{3,2},{4,5},{5,4},{6,7},{7,6},{8,9},{9,8},{10,11... | collective-permute-start | bytes 786440 | tf_op jit(solution)/shard_map/ppermute | solution.py:446
  33.7 24.0 %collective-permute-start.6 = (bf16[256,512]{1,0:T(8,128)(2,1)}, bf16[256,512]{1,0:T(8,128)(2,1)}, u32[]{:S(2)}, u32[]{:S(2)}) collective-permute-start(bf16[256,512]{1,0:T(8,128)(2,1)} %project.5), channel_id=1, source_target_pairs={{0,2},{1,3},{2,0},{3,1},{4,6},{5,7},{6,4},{7,5},{8,10},{9,11},{10,... | collective-permute-start | bytes 786440 | tf_op jit(solution)/shard_map/ppermute | solution.py:446
  50.7 12.1 %collective-permute-start = (bf16[256,768]{1,0:T(8,128)(2,1)S(1)}, bf16[256,768]{1,0:T(8,128)(2,1)S(1)}, u32[]{:S(2)}, u32[]{:S(2)}) collective-permute-start(bf16[256,768]{1,0:T(8,128)(2,1)S(1)} %copy-done.7), channel_id=1, source_target_pairs={{0,1},{1,0},{2,3},{3,2},{4,5},{5,4},{6,7},{7,6},{8,9},{9,8},{10,11... | collective-permute-start | bytes 1179656 | tf_op jit(solution)/shard_map/ppermute | solution.py:446
  53.5 14.8 %collective-permute-start.3 = (bf16[256,512]{1,0:T(8,128)(2,1)S(1)}, bf16[256,512]{1,0:T(8,128)(2,1)S(1)}, u32[]{:S(2)}, u32[]{:S(2)}) collective-permute-start(bf16[256,512]{1,0:T(8,128)(2,1)S(1)} %add_convert_fusion.3), channel_id=1, source_target_pairs={{0,1},{1,0},{2,3},{3,2},{4,5},{5,4},{6,7},{7,6},{8,9},{9,8},{10,11... | collective-permute-start | bytes 786440 | tf_op jit(solution)/shard_map/ppermute | solution.py:446
  56.1 12.3 %collective-permute-start.5 = (bf16[256,512]{1,0:T(8,128)(2,1)S(1)}, bf16[256,512]{1,0:T(8,128)(2,1)S(1)}, u32[]{:S(2)}, u32[]{:S(2)}) collective-permute-start(bf16[256,512]{1,0:T(8,128)(2,1)S(1)} %add_convert_fusion.2), channel_id=1, source_target_pairs={{0,2},{1,3},{2,0},{3,1},{4,6},{5,7},{6,4},{7,5},{8,10},{9,11},{10,... | collective-permute-start | bytes 786440 | tf_op jit(solution)/shard_map/ppermute | solution.py:446
  58.7 13.1 %collective-permute-start.7 = (bf16[256,512]{1,0:T(8,128)(2,1)S(1)}, bf16[256,512]{1,0:T(8,128)(2,1)S(1)}, u32[]{:S(2)}, u32[]{:S(2)}) collective-permute-start(bf16[256,512]{1,0:T(8,128)(2,1)S(1)} %add_convert_fusion.1), channel_id=1, source_target_pairs={{0,1},{1,0},{2,3},{3,2},{4,5},{5,4},{6,7},{7,6},{8,9},{9,8},{10,11... | collective-permute-start | bytes 786440 | tf_op jit(solution)/shard_map/ppermute | solution.py:446
  62.9 9.1 %collective-permute-start.1 = (bf16[256,768]{1,0:T(8,128)(2,1)S(1)}, bf16[256,768]{1,0:T(8,128)(2,1)S(1)}, u32[]{:S(2)}, u32[]{:S(2)}) collective-permute-start(bf16[256,768]{1,0:T(8,128)(2,1)S(1)} %add_convert_fusion), channel_id=1, source_target_pairs={{0,2},{1,3},{2,0},{3,1},{4,6},{5,7},{6,4},{7,5},{8,10},{9,11},{10,... | collective-permute-start | bytes 1179656 | tf_op jit(solution)/shard_map/ppermute | solution.py:446
  77.6 9.0 %collective-permute-start.22 = (bf16[128,2048]{1,0:T(8,128)(2,1)S(1)}, bf16[128,2048]{1,0:T(8,128)(2,1)S(1)}, u32[]{:S(2)}, u32[]{:S(2)}) collective-permute-start(bf16[128,2048]{1,0:T(8,128)(2,1)S(1)} %get-tuple-element.68), channel_id=1, source_target_pairs={{0,4},{4,0},{8,12},{12,8},{16,20},{20,16},{24,28},{28,24},{1,5},{5... | collective-permute-start | bytes 1572872 | tf_op jit(solution)/shard_map/ppermute | solution.py:485
  84.4 11.7 %collective-permute-start.28 = (bf16[128,1536]{1,0:T(8,128)(2,1)S(1)}, bf16[128,1536]{1,0:T(8,128)(2,1)S(1)}, u32[]{:S(2)}, u32[]{:S(2)}) collective-permute-start(bf16[128,1536]{1,0:T(8,128)(2,1)S(1)} %add.109.own_ref), channel_id=1, source_target_pairs={{0,8},{4,12},{24,16},{28,20},{1,9},{5,13},{25,17},{29,21},{2,10},{... | collective-permute-start | bytes 1179656 | tf_op jit(solution)/shard_map/ppermute | solution.py:486
  86.8 20.6 %collective-permute-start.23 = (bf16[128,2048]{1,0:T(8,128)(2,1)S(1)}, bf16[128,2048]{1,0:T(8,128)(2,1)S(1)}, u32[]{:S(2)}, u32[]{:S(2)}) collective-permute-start(bf16[128,2048]{1,0:T(8,128)(2,1)S(1)} %add.107.own_ref), channel_id=1, source_target_pairs={{0,8},{4,12},{24,16},{28,20},{1,9},{5,13},{25,17},{29,21},{2,10},{... | collective-permute-start | bytes 1572872 | tf_op jit(solution)/shard_map/ppermute | solution.py:486
  88.2 39.9 %collective-permute-start.13 = (bf16[128,1536]{1,0:T(8,128)(2,1)S(1)}, bf16[128,1536]{1,0:T(8,128)(2,1)S(1)}, u32[]{:S(2)}, u32[]{:S(2)}) collective-permute-start(bf16[128,1536]{1,0:T(8,128)(2,1)S(1)} %add.103.own_ref), channel_id=1, source_target_pairs={{0,8},{4,12},{24,16},{28,20},{1,9},{5,13},{25,17},{29,21},{2,10},{... | collective-permute-start | bytes 1179656 | tf_op jit(solution)/shard_map/ppermute | solution.py:486
  89.7 36.4 %collective-permute-start.18 = (bf16[128,2048]{1,0:T(8,128)(2,1)S(1)}, bf16[128,2048]{1,0:T(8,128)(2,1)S(1)}, u32[]{:S(2)}, u32[]{:S(2)}) collective-permute-start(bf16[128,2048]{1,0:T(8,128)(2,1)S(1)} %add.105.own_ref), channel_id=1, source_target_pairs={{0,8},{4,12},{24,16},{28,20},{1,9},{5,13},{25,17},{29,21},{2,10},{... | collective-permute-start | bytes 1572872 | tf_op jit(solution)/shard_map/ppermute | solution.py:486
  96.1 36.4 %collective-permute-start.29 = (bf16[64,1536]{1,0:T(8,128)(2,1)S(1)}, bf16[64,1536]{1,0:T(8,128)(2,1)S(1)}, u32[]{:S(2)}, u32[]{:S(2)}) collective-permute-start(bf16[64,1536]{1,0:T(8,128)(2,1)S(1)} %slice_add_fusion.2), channel_id=1, source_target_pairs={{8,16},{12,20},{16,8},{20,12},{9,17},{13,21},{17,9},{21,13},{10,18... | collective-permute-start | bytes 589832 | tf_op jit(solution)/shard_map/ppermute | solution.py:487
  107.4 19.5 %collective-permute-start.24 = (bf16[64,2048]{1,0:T(8,128)(2,1)S(1)}, bf16[64,2048]{1,0:T(8,128)(2,1)S(1)}, u32[]{:S(2)}, u32[]{:S(2)}) collective-permute-start(bf16[64,2048]{1,0:T(8,128)(2,1)S(1)} %slice_add_fusion), channel_id=1, source_target_pairs={{8,16},{12,20},{16,8},{20,12},{9,17},{13,21},{17,9},{21,13},{10,18... | collective-permute-start | bytes 786440 | tf_op jit(solution)/shard_map/ppermute | solution.py:487
  128.8 13.0 %collective-permute-start.32 = (bf16[1024,256]{1,0:T(8,128)(2,1)S(1)}, bf16[1024,256]{1,0:T(8,128)(2,1)S(1)}, u32[]{:S(2)}, u32[]{:S(2)}) collective-permute-start(bf16[1024,256]{1,0:T(8,128)(2,1)S(1)} %dynamic-slice_select_fusion), channel_id=1, source_target_pairs={{0,1},{4,5},{9,8},{13,12},{18,19},{22,23},{27,26},{31,30}} | collective-permute-start | bytes 1572872 | tf_op jit(solution)/shard_map/ppermute | solution.py:478
  134.9 52.1 %collective-permute-start.26 = (bf16[128,2048]{1,0:T(8,128)(2,1)S(1)}, bf16[128,2048]{1,0:T(8,128)(2,1)S(1)}, u32[]{:S(2)}, u32[]{:S(2)}) collective-permute-start(bf16[128,2048]{1,0:T(8,128)(2,1)S(1)} %pad_maximum_fusion.2), channel_id=1, source_target_pairs={{8,0},{12,4},{16,24},{20,28},{9,1},{13,5},{17,25},{21,29},{10,2},{... | collective-permute-start | bytes 1572872 | tf_op jit(solution)/shard_map/ppermute | solution.py:492
  136.4 52.0 %collective-permute-start.21 = (bf16[128,2048]{1,0:T(8,128)(2,1)S(1)}, bf16[128,2048]{1,0:T(8,128)(2,1)S(1)}, u32[]{:S(2)}, u32[]{:S(2)}) collective-permute-start(bf16[128,2048]{1,0:T(8,128)(2,1)S(1)} %pad_maximum_fusion.1), channel_id=1, source_target_pairs={{8,0},{12,4},{16,24},{20,28},{9,1},{13,5},{17,25},{21,29},{10,2},{... | collective-permute-start | bytes 1572872 | tf_op jit(solution)/shard_map/ppermute | solution.py:492
  137.8 48.4 %collective-permute-start.31 = (bf16[128,1536]{1,0:T(8,128)(2,1)S(1)}, bf16[128,1536]{1,0:T(8,128)(2,1)S(1)}, u32[]{:S(2)}, u32[]{:S(2)}) collective-permute-start(bf16[128,1536]{1,0:T(8,128)(2,1)S(1)} %pad_maximum_fusion.4), channel_id=1, source_target_pairs={{8,0},{12,4},{16,24},{20,28},{9,1},{13,5},{17,25},{21,29},{10,2},{... | collective-permute-start | bytes 1179656 | tf_op jit(solution)/shard_map/ppermute | solution.py:492
  139.1 51.2 %collective-permute-start.16 = (bf16[128,1536]{1,0:T(8,128)(2,1)S(1)}, bf16[128,1536]{1,0:T(8,128)(2,1)S(1)}, u32[]{:S(2)}, u32[]{:S(2)}) collective-permute-start(bf16[128,1536]{1,0:T(8,128)(2,1)S(1)} %pad_maximum_fusion.3), channel_id=1, source_target_pairs={{8,0},{12,4},{16,24},{20,28},{9,1},{13,5},{17,25},{21,29},{10,2},{... | collective-permute-start | bytes 1179656 | tf_op jit(solution)/shard_map/ppermute | solution.py:492
  142.0 49.3 %collective-permute-start.33 = (bf16[1024,256]{1,0:T(8,128)(2,1)S(1)}, bf16[1024,256]{1,0:T(8,128)(2,1)S(1)}, u32[]{:S(2)}, u32[]{:S(2)}) collective-permute-start(bf16[1024,256]{1,0:T(8,128)(2,1)S(1)} %add.111), channel_id=1, source_target_pairs={{0,2},{1,3},{4,6},{5,7},{9,11},{8,10},{13,15},{12,14},{18,16},{19,... | collective-permute-start | bytes 1572872 | tf_op jit(solution)/shard_map/ppermute | solution.py:478
  191.2 9.1 %collective-permute-start.34 = (bf16[128,1536]{1,0:T(8,128)(2,1)S(1)}, bf16[128,1536]{1,0:T(8,128)(2,1)S(1)}, u32[]{:S(2)}, u32[]{:S(2)}) collective-permute-start(bf16[128,1536]{1,0:T(8,128)(2,1)S(1)} %get-tuple-element.87.mine_ref), channel_id=1, source_target_pairs={{0,4},{4,0},{8,12},{12,8},{16,20},{20,16},{24,28},{28,24},{1,5},{5... | collective-permute-start | bytes 1179656 | tf_op jit(solution)/shard_map/ppermute | solution.py:496
  (22 other events, 298.4 us)

commit v4 on v3

--- a/solution.py
+++ b/solution.py
@@ -24,6 +24,10 @@
 CORES = 2
 CHUNKS = (3, 4, 4, 3)
 MIB = 1 << 20
+
+VMEM = pl.BlockSpec(memory_space=pltpu.VMEM)
+SMEM = pl.BlockSpec(memory_space=pltpu.SMEM)
+HBM = pl.BlockSpec(memory_space=pltpu.HBM)
 
 
 def from_root(block, axis, owner):
@@ -76,94 +80,60 @@
     return best
 
 
-def project_pieces(turned, act_hbm, out_ref, act_buf, act_sem, start):
+def project_kernel(slot_ref, basis_hbm, act_hbm, *refs):
+    *outs, turned, basis_buf, basis_sem, act_buf, act_sem = refs
+    rows = basis_buf.shape[1] // slot_ref.shape[0]
     pieces = act_sem.shape[0]
     size = act_buf.shape[0] // pieces
+    copy = pltpu.make_async_copy(basis_hbm, basis_buf, basis_sem)
+    copy.start()
     copies = []
     for i in range(pieces):
-        copies.append(
-            pltpu.make_async_copy(
-                act_hbm.at[pl.ds(start + i * size, size)],
-                act_buf.at[pl.ds(i * size, size)],
-                act_sem.at[i],
-            )
-        )
+        part = pl.ds(i * size, size)
+        copies.append(pltpu.make_async_copy(act_hbm.at[part], act_buf.at[part], act_sem.at[i]))
         copies[-1].start()
-    yield
-    for i, copy in enumerate(copies):
-        copy.wait()
-        out_ref[:, i * size : (i + 1) * size] = lax.dot_general(
-            turned[...],
-            act_buf[i * size : (i + 1) * size, :],
-            (((1,), (1,)), ((), ())),
-            preferred_element_type=F32,
-        ).astype(out_ref.dtype)
-    yield
-
-
-def project_first_kernel(
-    start, slot_ref, basis_hbm, act_hbm, out_ref, turned_ref, basis_buf, basis_sem, act_buf, act_sem
-):
-    rows = basis_buf.shape[1] // slot_ref.shape[0]
-    copy = pltpu.make_async_copy(basis_hbm, basis_buf, basis_sem)
-    copy.start()
-    work = project_pieces(turned_ref, act_hbm, out_ref, act_buf, act_sem, start)
-    next(work)
     copy.wait()
     flipped = basis_buf[...].T
     for n in range(slot_ref.shape[0]):
         at = pl.multiple_of(slot_ref[n] * rows, rows)
-        turned_ref[pl.ds(at, rows), :] = flipped[n * rows : (n + 1) * rows, :]
-    next(work)
-
-
-def project_kernel(start, turned_ref, act_hbm, out_ref, act_buf, act_sem):
-    work = project_pieces(turned_ref, act_hbm, out_ref, act_buf, act_sem, start)
-    next(work)
-    next(work)
-
-
-def project(source, slots, activations, start, count):
-    depth = activations.shape[1]
-    rank = source.shape[1] if slots is not None else source.shape[0]
-    hbm = pl.BlockSpec(memory_space=pltpu.HBM)
-    vmem = pl.BlockSpec(memory_space=pltpu.VMEM)
-    part = jax.ShapeDtypeStruct((rank, count), BF16)
-    scratch = [
-        pltpu.VMEM((count, depth), BF16),
-        pltpu.SemaphoreType.DMA((count // pick(count, 256),)),
-    ]
-    estimate = pl.CostEstimate(
-        flops=2 * depth * rank * count,
-        bytes_accessed=2 * (depth * rank + depth * count + rank * count),
-        transcendentals=0,
-    )
-    if slots is None:
-        return pl.pallas_call(
-            functools.partial(project_kernel, start),
-            out_shape=part,
-            in_specs=[vmem, hbm],
-            out_specs=vmem,
-            scratch_shapes=scratch,
-            compiler_params=pltpu.CompilerParams(vmem_limit_bytes=56 * MIB),
-            cost_estimate=estimate,
-            name="project",
-        )(source, activations)
-    return pl.pallas_call(
-        functools.partial(project_first_kernel, start),
-        out_shape=[part, jax.ShapeDtypeStruct((rank, depth), BF16)],
-        in_specs=[pl.BlockSpec(memory_space=pltpu.SMEM), hbm, hbm],
-        out_specs=[vmem, vmem],
-        scratch_shapes=[pltpu.VMEM((depth, rank), BF16), pltpu.SemaphoreType.DMA, *scratch],
-        compiler_params=pltpu.CompilerParams(vmem_limit_bytes=56 * MIB),
-        cost_estimate=estimate,
-        name="project_first",
-    )(slots, source, activations)
-
-
-VMEM = pl.BlockSpec(memory_space=pltpu.VMEM)
-SMEM = pl.BlockSpec(memory_space=pltpu.SMEM)
-HBM = pl.BlockSpec(memory_space=pltpu.HBM)
+        turned[pl.ds(at, rows), :] = flipped[n * rows : (n + 1) * rows, :]
+    i = 0
+    for out_ref in outs:
+        for at in range(0, out_ref.shape[1], size):
+            copies[i].wait()
+            out_ref[:, at : at + size] = lax.dot_general(
+                turned[...],
+                act_buf[i * size : (i + 1) * size, :],
+                (((1,), (1,)), ((), ())),
+                preferred_element_type=F32,
+            ).astype(out_ref.dtype)
+            i += 1
+
+
+def project(slots, basis, activations, spans):
+    tokens, depth = activations.shape
+    rank = basis.shape[1]
+    size = 256 if all(count % 256 == 0 for _, count in spans) else 128
+    return pl.pallas_call(
+        project_kernel,
+        out_shape=[jax.ShapeDtypeStruct((rank, count), BF16) for _, count in spans],
+        in_specs=[SMEM, HBM, HBM],
+        out_specs=[VMEM] * len(spans),
+        scratch_shapes=[
+            pltpu.VMEM((rank, depth), BF16),
+            pltpu.VMEM((depth, rank), BF16),
+            pltpu.SemaphoreType.DMA,
+            pltpu.VMEM((tokens, depth), BF16),
+            pltpu.SemaphoreType.DMA((tokens // size,)),
+        ],
+        compiler_params=pltpu.CompilerParams(vmem_limit_bytes=52 * MIB),
+        cost_estimate=pl.CostEstimate(
+            flops=2 * depth * rank * tokens,
+            bytes_accessed=2 * (depth * rank + depth * tokens + rank * tokens),
+            transcendentals=0,
+        ),
+        name="project",
+    )(slots, basis, activations)
 
 
 def small(limit_mib):
@@ -250,18 +220,20 @@
 
 
 def hub_kernel(
-    start, scale_ref, own_ref, came_ref, far_ref, m_ref, v_ref, mv_ref, near_ref, sum_ref, mine_ref
+    start, scale_ref, own_ref, came_ref, far_ref, m_ref, v_ref, mv_ref, near_ref, out_ref, mine_ref
 ):
     rows, width = mine_ref.shape
     total = own_ref[: 2 * rows].astype(F32) + came_ref[: 2 * rows].astype(F32)
     total = total + far_ref[...].astype(F32)
-    sum_ref[...] = total[:rows].astype(BF16)
+    out_ref[:rows] = total[:rows].astype(BF16)
     mine_ref[...] = total[rows:]
     gradient = total * scale_ref[0, 0]
     cols = slice(start, start + width)
     mv = mv_ref[:, cols].astype(F32)
     near_ref[:rows] = moments(gradient[:rows], mv[:rows], mv[rows:])[2].astype(BF16)
-    near_ref[rows:] = moments(gradient[rows:], m_ref[:, cols], v_ref[:, cols])[2].astype(BF16)
+    update = moments(gradient[rows:], m_ref[:, cols], v_ref[:, cols])[2].astype(BF16)
+    near_ref[rows:] = update
+    out_ref[rows:] = update
 
 
 def hub_chunk(scale, own, came, far, first, second, moved, start):
@@ -270,7 +242,7 @@
         functools.partial(hub_kernel, start),
         out_shape=[
             jax.ShapeDtypeStruct((2 * rows, width), BF16),
-            jax.ShapeDtypeStruct((rows, width), BF16),
+            jax.ShapeDtypeStruct((2 * rows, width), BF16),
             jax.ShapeDtypeStruct((rows, width), F32),
         ],
         in_specs=[SMEM] + [VMEM] * 6,
@@ -284,7 +256,7 @@
 
 
 def settle_kernel(
-    start, scale_ref, hub_ref, mine_ref, m_ref, v_ref, near_ref, across_ref, sent_ref, *rest
+    start, scale_ref, hub_ref, mine_ref, m_ref, v_ref, near_ref, across_ref, sent_ref, more_ref, *rest
 ):
     all_ref, first_out, second_out, first_buf, second_buf, sem = rest[-6:]
     rows, width = mine_ref.shape
@@ -304,12 +276,12 @@
         copy.start()
     all_ref[:rows] = jnp.where(hub, near_ref[:rows], update.astype(BF16))
     all_ref[rows : 2 * rows] = jnp.where(hub, update.astype(BF16), sent_ref[rows : 2 * rows])
-    all_ref[2 * rows :] = jnp.where(hub, across_ref[...], sent_ref[2 * rows :])
+    all_ref[2 * rows :] = jnp.where(hub, across_ref[...], more_ref[...])
     for copy in copies:
         copy.wait()
 
 
-def settle_chunk(scale, hub, mine, first, second, near, across, sent, start, results):
+def settle_chunk(scale, hub, mine, first, second, near, across, sent, more, start, results):
     rows, full = first.shape
     width = mine.shape[1]
     return pl.pallas_call(
@@ -319,9 +291,9 @@
             jax.ShapeDtypeStruct((rows, full), F32),
             jax.ShapeDtypeStruct((rows, full), F32),
         ],
-        in_specs=[SMEM, SMEM] + [VMEM] * 6 + [HBM] * len(results),
+        in_specs=[SMEM, SMEM] + [VMEM] * 7 + [HBM] * len(results),
         out_specs=[VMEM, HBM, HBM],
-        input_output_aliases={8: 1, 9: 2} if results else {},
+        input_output_aliases={9: 1, 10: 2} if results else {},
         scratch_shapes=[
             pltpu.VMEM((rows, width), F32),
             pltpu.VMEM((rows, width), F32),
@@ -332,7 +304,7 @@
             flops=4000 * rows * width, bytes_accessed=40 * rows * width, transcendentals=0
         ),
         name="settle",
-    )(scale, hub, mine, first, second, near, across, sent, *results)
+    )(scale, hub, mine, first, second, near, across, sent, more, *results)
 
 
 def spread_kernel(start, slot_ref, basis_ref, mine_ref, other_ref, *rest):
@@ -428,14 +400,7 @@
     basis_rows = lax.dynamic_slice_in_dim(basis, data_index % per_owner * row_count, row_count, 0)
     basis_rows = jnp.where(tensor_index == owner, basis_rows, jnp.zeros_like(basis_rows))
     bits = [1 << b for b in range(tensor_count.bit_length() - 1)]
-    parts = []
-    source = basis
-    for i, (start, count) in enumerate(token_pieces(tokens)):
-        if i == 0:
-            part, source = project(basis, slots, activations, start, count)
-        else:
-            part = project(source, None, activations, start, count)
-        parts.append(part)
+    parts = list(project(slots, basis, activations, token_pieces(tokens)))
     got = [None] * len(parts)
     for step in range(len(bits)):
         for i, part in enumerate(parts):
@@ -485,13 +450,14 @@
         mine = keep + lax.ppermute(give, "dp", sibling)
         came = lax.ppermute(mine, "dp", inward)
         across = lax.ppermute(mine[2 * rows :] + came[2 * rows :], "dp", middle)
-        near, total, held = hub_chunk(
+        near, ready, held = hub_chunk(
             scale, mine, came, across, first_moment, second_moment, moved, start
         )
         beyond = lax.ppermute(near, "dp", middle)
-        sent = lax.ppermute(jnp.concatenate([total, near[rows:], beyond]), "dp", outward)
+        sent = lax.ppermute(ready, "dp", outward)
+        more = lax.ppermute(beyond, "dp", outward)
         updates, *settled = settle_chunk(
-            scale, hub, held, first_moment, second_moment, near, beyond, sent, start, settled
+            scale, hub, held, first_moment, second_moment, near, beyond, sent, more, start, settled
         )
         other = lax.ppermute(updates, "dp", sibling)
         spread = (spread_chunk(slots, basis_rows, updates, other, start, full, spread),)

time: 204 us -> 195 us (0.956)
  Pallas kernels: 58.9 us -> 50.2 us
  starting transfers between devices: 40.6 us -> 47.1 us
  waiting for transfers between devices: 89.4 us -> 83.1 us
    pallas_call x4 -> x1, Pallas kernels: 19.5 us -> 10.9 us  [project(): pl.pallas_call(project_kernel, out_shape=[jax.ShapeDtypeStruct((rank, cou...]
    ppermute x4 -> x8, starting transfers between devices: 5.35 us -> 10.5 us  [the longest x4 5.34 us: local_line(): more = lax.ppermute(beyond, 'dp', outward)]
    ppermute x4 -> x8, waiting for transfers between devices: 43.7 us -> 40.3 us  [the longest x4 25 us: local_line(): more = lax.ppermute(beyond, 'dp', outward)]
    ppermute x4, waiting for transfers between devices: 33.6 us -> 31.2 us  [local_line(): came = lax.ppermute(mine, 'dp', inward)]
    ppermute x2, starting transfers between devices: 3.79 us -> 5.93 us  [local_line(): basis_rows = basis_rows + lax.ppermute(basis_rows, ('dp', 'tensor'), pairs)]
  transfers between devices with their start and end apart: 38 -> 42, of which waited for: 9 -> 11; matrix products, arithmetic and copies ran while one was open for 5% -> 5% of each run, Pallas kernels for 25% -> 22%
where the time goes in v4:
time: 195 us; the launch traced here: 194 us
  waiting for transfers between devices  83.1 us (43%)
  Pallas kernels  50.2 us (26%)
  starting transfers between devices  47.1 us (24%)
  other arithmetic  10.4 us (5%)
  between operations  2.28 us (1%)
    ppermute x4, waiting for transfers between devices, local_line(): came = lax.ppermute(mine, 'dp', inward)  31.2 us
    ppermute x4, waiting for transfers between devices, local_line(): more = lax.ppermute(beyond, 'dp', outward)  25 us
    ppermute x4, waiting for transfers between devices, local_line(): sent = lax.ppermute(ready, 'dp', outward)  15.3 us
    pallas_call x2, Pallas kernels, load_rows(): pl.pallas_call(functools.partial(load_kernel, start), out_shape=jax.Shape...  11.7 us
    ppermute x8, waiting for transfers between devices, local_line(): got[i] = lax.ppermute(part, 'tensor', pairs)  11.6 us
    pallas_call x4, Pallas kernels, spread_chunk(): pl.pallas_call(functools.partial(spread_kernel, start), out_shape=jax.Sha...  11.3 us
    pallas_call x4, Pallas kernels, gradient_chunk(): pl.pallas_call(functools.partial(gradient_kernel, start, pick(width, 512)...  11 us
    pallas_call x1, Pallas kernels, project(): pl.pallas_call(project_kernel, out_shape=[jax.ShapeDtypeStruct((rank, cou...  10.9 us
  transfers between devices with their start and end apart: 42, of which 11 were waited for; matrix products, arithmetic and copies ran while one was open for 5% of the time, Pallas kernels for 22%

profile of v4, /device:TPU:0, one launch (start us, length us, event | category | flops | bytes accessed | tf_op | source)
XLA Modules:
  0.0 194.4 jit_solution(1145549130107184533)
XLA Ops:
  6.7 4.5 %collective-permute-start.8 = (bf16[64,7168]{1,0:T(8,128)(2,1)}, bf16[64,7168]{1,0:T(8,128)(2,1)S(1)}, u32[]{:S(2)}, u32[]{:S(2)}) collective-permute-start(bf16[64,7168]{1,0:T(8,128)(2,1)} %pad_maximum_fusion), channel_id=1, source_target_pairs={{0,8},{4,12},{24,16},{28,20},{1,9},{5,13},{25,17},{29,21},{2,10},{... | collective-permute-start | bytes 2752520 | tf_op jit(solution)/shard_map/ppermute | solution.py:426
  11.3 10.9 %project.1 = (bf16[256,768]{1,0:T(8,128)(2,1)S(1)}, bf16[256,512]{1,0:T(8,128)(2,1)S(1)}, bf16[256,512]{1,0:T(8,128)(2,1)S(1)}, bf16[256,512]{1,0:T(8,128)(2,1)S(1)}) custom-call(s32[8]{0:T(128)S(1)} %fusion.slot_ref, bf16[2048,256]{1,0:T(8,128)(2,1)} %basis_hbm.1, bf16[2304,2048]{1,0:T(8,128)(2,1)} %act_hbm.1), custom_call_target="tpu_custom_call" | custom-call | flops 2415919104 | bytes 11665408 | tf_op jit(solution)/shard_map/project/pallas_call | solution.py:117
  27.5 6.4 %load.2.refs_4_ = bf16[1280,7168]{1,0:T(8,128)(2,1)S(1)} custom-call(bf16[2304,7168]{1,0:T(8,128)(2,1)} %source.1), custom_call_target="tpu_custom_call" | custom-call | flops 1280000000 | bytes 36700160 | tf_op jit(solution)/shard_map/load/pallas_call | solution.py:159
  34.5 3.1 %collective-permute-start.11 = (f32[8,128]{1,0:T(8,128)S(1)}, f32[8,128]{1,0:T(8,128)S(1)}, u32[]{:S(2)}, u32[]{:S(2)}) collective-permute-start(f32[8,128]{1,0:T(8,128)S(1)} %fusion.6), channel_id=1, source_target_pairs={{0,16},{4,20},{8,24},{12,28},{16,0},{20,4},{24,8},{28,12},{1,17},{... | collective-permute-start | bytes 12296 | tf_op jit(solution)/shard_map/ppermute | solution.py:418
  37.6 5.3 %load.3.refs_5_ = bf16[1024,7168]{1,0:T(8,128)(2,1)S(1)} custom-call(bf16[2304,7168]{1,0:T(8,128)(2,1)} %source.1), custom_call_target="tpu_custom_call" | custom-call | flops 1024000000 | bytes 29360128 | tf_op jit(solution)/shard_map/load/pallas_call | solution.py:159
  50.6 4.4 %collective-permute-done = bf16[256,768]{1,0:T(8,128)(2,1)S(1)} collective-permute-done((bf16[256,768]{1,0:T(8,128)(2,1)S(1)}, bf16[256,768]{1,0:T(8,128)(2,1)S(1)}, u32[]{:S(2)}, u32[]{:S(2)}) %collective-permute-start) | collective-permute-done | bytes 393248 | tf_op jit(solution)/shard_map/ppermute | solution.py:411
  56.7 3.9 %collective-permute-done.3 = bf16[256,512]{1,0:T(8,128)(2,1)S(1)} collective-permute-done((bf16[256,512]{1,0:T(8,128)(2,1)S(1)}, bf16[256,512]{1,0:T(8,128)(2,1)S(1)}, u32[]{:S(2)}, u32[]{:S(2)}) %collective-permute-start.3) | collective-permute-done | bytes 262176 | tf_op jit(solution)/shard_map/ppermute | solution.py:411
  60.8 3.3 %collective-permute-done.7 = bf16[256,512]{1,0:T(8,128)(2,1)S(1)} collective-permute-done((bf16[256,512]{1,0:T(8,128)(2,1)S(1)}, bf16[256,512]{1,0:T(8,128)(2,1)S(1)}, u32[]{:S(2)}, u32[]{:S(2)}) %collective-permute-start.7) | collective-permute-done | bytes 262176 | tf_op jit(solution)/shard_map/ppermute | solution.py:411
  66.7 3.1 %gradient.6 = (bf16[128,2048]{1,0:T(8,128)(2,1)S(1)}, bf16[128,2048]{1,0:T(8,128)(2,1)S(1)}) custom-call(bf16[256,768]{1,0:T(8,128)(2,1)S(1)} %multiply_convert_fusion.refs_0_, bf16[256,512]{1,0:T(8,128)(2,1)S(1)} %multiply_convert_fusion.3.refs_1_, bf16[256,512]{1,0:T(8,128)(2,1)S(1)} %multiply_convert_fusion.2.refs_2_, ...), custom_call_target="tpu_custom_call" | custom-call | flops 2415919104 | bytes 2097152 | tf_op jit(solution)/shard_map/gradient/pallas_call | solution.py:202
  70.4 3.1 %gradient.5 = (bf16[128,2048]{1,0:T(8,128)(2,1)S(1)}, bf16[128,2048]{1,0:T(8,128)(2,1)S(1)}) custom-call(bf16[256,768]{1,0:T(8,128)(2,1)S(1)} %multiply_convert_fusion.refs_0_, bf16[256,512]{1,0:T(8,128)(2,1)S(1)} %multiply_convert_fusion.3.refs_1_, bf16[256,512]{1,0:T(8,128)(2,1)S(1)} %multiply_convert_fusion.2.refs_2_, ...), custom_call_target="tpu_custom_call" | custom-call | flops 2415919104 | bytes 2097152 | tf_op jit(solution)/shard_map/gradient/pallas_call | solution.py:202
  73.7 2.4 %gradient.4 = (bf16[128,1536]{1,0:T(8,128)(2,1)S(1)}, bf16[128,1536]{1,0:T(8,128)(2,1)S(1)}) custom-call(bf16[256,768]{1,0:T(8,128)(2,1)S(1)} %multiply_convert_fusion.refs_0_, bf16[256,512]{1,0:T(8,128)(2,1)S(1)} %multiply_convert_fusion.3.refs_1_, bf16[256,512]{1,0:T(8,128)(2,1)S(1)} %multiply_convert_fusion.2.refs_2_, ...), custom_call_target="tpu_custom_call" | custom-call | flops 1811939328 | bytes 1572864 | tf_op jit(solution)/shard_map/gradient/pallas_call | solution.py:202
  80.4 2.5 %collective-permute-start.36 = (bf16[1024,256]{1,0:T(8,128)(2,1)S(1)}, bf16[1024,256]{1,0:T(8,128)(2,1)S(1)}, u32[]{:S(2)}, u32[]{:S(2)}) collective-permute-start(bf16[1024,256]{1,0:T(8,128)(2,1)S(1)} %copy-done.3), channel_id=1, source_target_pairs={{0,1},{4,5},{9,8},{13,12},{18,19},{22,23},{27,26},{31,30}} | collective-permute-start | bytes 1572872 | tf_op jit(solution)/shard_map/ppermute | solution.py:443
  85.8 2.6 %collective-permute-done.31.came_ref = bf16[128,1536]{1,0:T(8,128)(2,1)S(1)} collective-permute-done((bf16[128,1536]{1,0:T(8,128)(2,1)S(1)}, bf16[128,1536]{1,0:T(8,128)(2,1)S(1)}, u32[]{:S(2)}, u32[]{:S(2)}) %collective-permute-start.31) | collective-permute-done | bytes 393248 | tf_op jit(solution)/shard_map/ppermute | solution.py:451
  89.1 10.5 %collective-permute-done.25.came_ref = bf16[128,2048]{1,0:T(8,128)(2,1)S(1)} collective-permute-done((bf16[128,2048]{1,0:T(8,128)(2,1)S(1)}, bf16[128,2048]{1,0:T(8,128)(2,1)S(1)}, u32[]{:S(2)}, u32[]{:S(2)}) %collective-permute-start.25) | collective-permute-done | bytes 524320 | tf_op jit(solution)/shard_map/ppermute | solution.py:451
  100.3 18.1 %collective-permute-done.19.came_ref = bf16[128,2048]{1,0:T(8,128)(2,1)S(1)} collective-permute-done((bf16[128,2048]{1,0:T(8,128)(2,1)S(1)}, bf16[128,2048]{1,0:T(8,128)(2,1)S(1)}, u32[]{:S(2)}, u32[]{:S(2)}) %collective-permute-start.19) | collective-permute-done | bytes 524320 | tf_op jit(solution)/shard_map/ppermute | solution.py:451
  128.7 14.1 %collective-permute-done.34.sent_ref = bf16[64,1536]{1,0:T(8,128)(2,1)S(1)} collective-permute-done((bf16[64,1536]{1,0:T(8,128)(2,1)S(1)}, bf16[64,1536]{1,0:T(8,128)(2,1)S(1)}, u32[]{:S(2)}, u32[]{:S(2)}) %collective-permute-start.34) | collective-permute-done | bytes 196640 | tf_op jit(solution)/shard_map/ppermute | solution.py:457
  146.0 14.1 %collective-permute-done.35.more_ref = bf16[64,1536]{1,0:T(8,128)(2,1)S(1)} collective-permute-done((bf16[64,1536]{1,0:T(8,128)(2,1)S(1)}, bf16[64,1536]{1,0:T(8,128)(2,1)S(1)}, u32[]{:S(2)}, u32[]{:S(2)}) %collective-permute-start.35) | collective-permute-done | bytes 196640 | tf_op jit(solution)/shard_map/ppermute | solution.py:458
  162.2 3.5 %collective-permute-start.37 = (bf16[1024,256]{1,0:T(8,128)(2,1)S(1)}, bf16[1024,256]{1,0:T(8,128)(2,1)S(1)}, u32[]{:S(2)}, u32[]{:S(2)}) collective-permute-start(bf16[1024,256]{1,0:T(8,128)(2,1)S(1)} %add.111), channel_id=1, source_target_pairs={{0,2},{1,3},{4,6},{5,7},{9,11},{8,10},{13,15},{12,14},{18,16},{19,... | collective-permute-start | bytes 1572872 | tf_op jit(solution)/shard_map/ppermute | solution.py:443
  167.4 3.0 %collective-permute-done.23.more_ref = bf16[64,2048]{1,0:T(8,128)(2,1)S(1)} collective-permute-done((bf16[64,2048]{1,0:T(8,128)(2,1)S(1)}, bf16[64,2048]{1,0:T(8,128)(2,1)S(1)}, u32[]{:S(2)}, u32[]{:S(2)}) %collective-permute-start.23) | collective-permute-done | bytes 262176 | tf_op jit(solution)/shard_map/ppermute | solution.py:458
  173.8 7.9 %collective-permute-done.17.more_ref = bf16[64,1536]{1,0:T(8,128)(2,1)S(1)} collective-permute-done((bf16[64,1536]{1,0:T(8,128)(2,1)S(1)}, bf16[64,1536]{1,0:T(8,128)(2,1)S(1)}, u32[]{:S(2)}, u32[]{:S(2)}) %collective-permute-start.17) | collective-permute-done | bytes 196640 | tf_op jit(solution)/shard_map/ppermute | solution.py:458
  182.8 2.6 %spread.4.rest_0_ = bf16[1024,7168]{1,0:T(8,128)(2,1)} custom-call(s32[8]{0:T(128)S(1)} %fusion.slot_ref, bf16[1024,256]{1,0:T(8,128)(2,1)S(1)} %add.112.basis_ref, bf16[128,1536]{1,0:T(8,128)(2,1)S(1)} %get-tuple-element.94.mine_ref, bf16[128,1536]{1,0:T(8,128)(2,1)S(1)} %collective-permute-done.41.other_ref), custom_call_target="tpu_custom_call" | custom-call | flops 805306368 | bytes 4456448 | tf_op jit(solution)/shard_map/spread/pallas_call | solution.py:343
  185.4 3.0 %spread.5.rest_0_ = bf16[1024,7168]{1,0:T(8,128)(2,1)} custom-call(s32[8]{0:T(128)S(1)} %fusion.slot_ref, bf16[1024,256]{1,0:T(8,128)(2,1)S(1)} %add.112.basis_ref, bf16[128,2048]{1,0:T(8,128)(2,1)S(1)} %get-tuple-element.93.mine_ref, bf16[128,2048]{1,0:T(8,128)(2,1)S(1)} %collective-permute-done.40.other_ref, ...), custom_call_target="tpu_custom_call", output_to_operand_aliasing={{}: (4, {})} | custom-call | flops 1073741824 | bytes 5767168 | tf_op jit(solution)/shard_map/spread/pallas_call | solution.py:343
  188.5 3.0 %spread.6.rest_0_ = bf16[1024,7168]{1,0:T(8,128)(2,1)} custom-call(s32[8]{0:T(128)S(1)} %fusion.slot_ref, bf16[1024,256]{1,0:T(8,128)(2,1)S(1)} %add.112.basis_ref, bf16[128,2048]{1,0:T(8,128)(2,1)S(1)} %get-tuple-element.92.mine_ref, bf16[128,2048]{1,0:T(8,128)(2,1)S(1)} %collective-permute-done.39.other_ref, ...), custom_call_target="tpu_custom_call", output_to_operand_aliasing={{}: (4, {})} | custom-call | flops 1073741824 | bytes 5767168 | tf_op jit(solution)/shard_map/spread/pallas_call | solution.py:343
  191.6 2.6 %spread.7 = bf16[1024,7168]{1,0:T(8,128)(2,1)} custom-call(s32[8]{0:T(128)S(1)} %fusion.slot_ref, bf16[1024,256]{1,0:T(8,128)(2,1)S(1)} %add.112.basis_ref, bf16[128,1536]{1,0:T(8,128)(2,1)S(1)} %get-tuple-element.91.mine_ref, bf16[128,1536]{1,0:T(8,128)(2,1)S(1)} %collective-permute-done.38.other_ref, ...), custom_call_target="tpu_custom_call", output_to_operand_aliasing={{}: (4, {})} | custom-call | flops 805306368 | bytes 4456448 | tf_op jit(solution)/shard_map/spread/pallas_call | solution.py:343
  (118 shorter events, 54.2 us)
Async XLA Ops:
  2.7 24.0 %collective-permute-start.9 = (f32[8,128]{1,0:T(8,128)S(1)}, f32[8,128]{1,0:T(8,128)S(1)}, u32[]{:S(2)}, u32[]{:S(2)}) collective-permute-start(f32[8,128]{1,0:T(8,128)S(1)} %broadcast_in_dim.4), channel_id=1, source_target_pairs={{0,4},{4,0},{8,12},{12,8},{16,20},{20,16},{24,28},{28,24},{1,5},{5... | collective-permute-start | bytes 12296 | tf_op jit(solution)/shard_map/ppermute | solution.py:418
  6.7 57.6 %collective-permute-start.8 = (bf16[64,7168]{1,0:T(8,128)(2,1)}, bf16[64,7168]{1,0:T(8,128)(2,1)S(1)}, u32[]{:S(2)}, u32[]{:S(2)}) collective-permute-start(bf16[64,7168]{1,0:T(8,128)(2,1)} %pad_maximum_fusion), channel_id=1, source_target_pairs={{0,8},{4,12},{24,16},{28,20},{1,9},{5,13},{25,17},{29,21},{2,10},{... | collective-permute-start | bytes 2752520 | tf_op jit(solution)/shard_map/ppermute | solution.py:426
  22.3 22.5 %collective-permute-start.2 = (bf16[256,512]{1,0:T(8,128)(2,1)S(1)}, bf16[256,512]{1,0:T(8,128)(2,1)}, u32[]{:S(2)}, u32[]{:S(2)}) collective-permute-start(bf16[256,512]{1,0:T(8,128)(2,1)S(1)} %get-tuple-element.50), channel_id=1, source_target_pairs={{0,2},{1,3},{2,0},{3,1},{4,6},{5,7},{6,4},{7,5},{8,10},{9,11},{10,... | collective-permute-start | bytes 786440 | tf_op jit(solution)/shard_map/ppermute | solution.py:411
  23.9 23.5 %collective-permute-start.4 = (bf16[256,512]{1,0:T(8,128)(2,1)S(1)}, bf16[256,512]{1,0:T(8,128)(2,1)}, u32[]{:S(2)}, u32[]{:S(2)}) collective-permute-start(bf16[256,512]{1,0:T(8,128)(2,1)S(1)} %get-tuple-element.51), channel_id=1, source_target_pairs={{0,1},{1,0},{2,3},{3,2},{4,5},{5,4},{6,7},{7,6},{8,9},{9,8},{10,11... | collective-permute-start | bytes 786440 | tf_op jit(solution)/shard_map/ppermute | solution.py:411
  25.4 24.6 %collective-permute-start.6 = (bf16[256,512]{1,0:T(8,128)(2,1)S(1)}, bf16[256,512]{1,0:T(8,128)(2,1)S(1)}, u32[]{:S(2)}, u32[]{:S(2)}) collective-permute-start(bf16[256,512]{1,0:T(8,128)(2,1)S(1)} %get-tuple-element.52), channel_id=1, source_target_pairs={{0,2},{1,3},{2,0},{3,1},{4,6},{5,7},{6,4},{7,5},{8,10},{9,11},{10,... | collective-permute-start | bytes 786440 | tf_op jit(solution)/shard_map/ppermute | solution.py:411
  45.8 14.8 %collective-permute-start.3 = (bf16[256,512]{1,0:T(8,128)(2,1)S(1)}, bf16[256,512]{1,0:T(8,128)(2,1)S(1)}, u32[]{:S(2)}, u32[]{:S(2)}) collective-permute-start(bf16[256,512]{1,0:T(8,128)(2,1)S(1)} %add_convert_fusion.3), channel_id=1, source_target_pairs={{0,1},{1,0},{2,3},{3,2},{4,5},{5,4},{6,7},{7,6},{8,9},{9,8},{10,11... | collective-permute-start | bytes 786440 | tf_op jit(solution)/shard_map/ppermute | solution.py:411
  50.0 14.1 %collective-permute-start.7 = (bf16[256,512]{1,0:T(8,128)(2,1)S(1)}, bf16[256,512]{1,0:T(8,128)(2,1)S(1)}, u32[]{:S(2)}, u32[]{:S(2)}) collective-permute-start(bf16[256,512]{1,0:T(8,128)(2,1)S(1)} %add_convert_fusion.1), channel_id=1, source_target_pairs={{0,1},{1,0},{2,3},{3,2},{4,5},{5,4},{6,7},{7,6},{8,9},{9,8},{10,11... | collective-permute-start | bytes 786440 | tf_op jit(solution)/shard_map/ppermute | solution.py:411
  79.0 20.6 %collective-permute-start.25 = (bf16[128,2048]{1,0:T(8,128)(2,1)S(1)}, bf16[128,2048]{1,0:T(8,128)(2,1)S(1)}, u32[]{:S(2)}, u32[]{:S(2)}) collective-permute-start(bf16[128,2048]{1,0:T(8,128)(2,1)S(1)} %add.107.own_ref), channel_id=1, source_target_pairs={{0,8},{4,12},{24,16},{28,20},{1,9},{5,13},{25,17},{29,21},{2,10},{... | collective-permute-start | bytes 1572872 | tf_op jit(solution)/shard_map/ppermute | solution.py:451
  80.4 43.1 %collective-permute-start.36 = (bf16[1024,256]{1,0:T(8,128)(2,1)S(1)}, bf16[1024,256]{1,0:T(8,128)(2,1)S(1)}, u32[]{:S(2)}, u32[]{:S(2)}) collective-permute-start(bf16[1024,256]{1,0:T(8,128)(2,1)S(1)} %copy-done.3), channel_id=1, source_target_pairs={{0,1},{4,5},{9,8},{13,12},{18,19},{22,23},{27,26},{31,30}} | collective-permute-start | bytes 1572872 | tf_op jit(solution)/shard_map/ppermute | solution.py:443
  83.0 37.4 %collective-permute-start.13 = (bf16[128,1536]{1,0:T(8,128)(2,1)S(1)}, bf16[128,1536]{1,0:T(8,128)(2,1)S(1)}, u32[]{:S(2)}, u32[]{:S(2)}) collective-permute-start(bf16[128,1536]{1,0:T(8,128)(2,1)S(1)} %add.103.own_ref), channel_id=1, source_target_pairs={{0,8},{4,12},{24,16},{28,20},{1,9},{5,13},{25,17},{29,21},{2,10},{... | collective-permute-start | bytes 1179656 | tf_op jit(solution)/shard_map/ppermute | solution.py:451
  84.5 33.9 %collective-permute-start.19 = (bf16[128,2048]{1,0:T(8,128)(2,1)S(1)}, bf16[128,2048]{1,0:T(8,128)(2,1)S(1)}, u32[]{:S(2)}, u32[]{:S(2)}) collective-permute-start(bf16[128,2048]{1,0:T(8,128)(2,1)S(1)} %add.105.own_ref), channel_id=1, source_target_pairs={{0,8},{4,12},{24,16},{28,20},{1,9},{5,13},{25,17},{29,21},{2,10},{... | collective-permute-start | bytes 1572872 | tf_op jit(solution)/shard_map/ppermute | solution.py:451
  88.4 32.7 %collective-permute-start.32 = (bf16[64,1536]{1,0:T(8,128)(2,1)S(1)}, bf16[64,1536]{1,0:T(8,128)(2,1)S(1)}, u32[]{:S(2)}, u32[]{:S(2)}) collective-permute-start(bf16[64,1536]{1,0:T(8,128)(2,1)S(1)} %slice_add_fusion.2), channel_id=1, source_target_pairs={{8,16},{12,20},{16,8},{20,12},{9,17},{13,21},{17,9},{21,13},{10,18... | collective-permute-start | bytes 589832 | tf_op jit(solution)/shard_map/ppermute | solution.py:452
  99.6 19.5 %collective-permute-start.26 = (bf16[64,2048]{1,0:T(8,128)(2,1)S(1)}, bf16[64,2048]{1,0:T(8,128)(2,1)S(1)}, u32[]{:S(2)}, u32[]{:S(2)}) collective-permute-start(bf16[64,2048]{1,0:T(8,128)(2,1)S(1)} %slice_add_fusion), channel_id=1, source_target_pairs={{8,16},{12,20},{16,8},{20,12},{9,17},{13,21},{17,9},{21,13},{10,18... | collective-permute-start | bytes 786440 | tf_op jit(solution)/shard_map/ppermute | solution.py:452
  122.8 21.3 %collective-permute-start.21 = (bf16[64,2048]{1,0:T(8,128)(2,1)S(1)}, bf16[64,2048]{1,0:T(8,128)(2,1)S(1)}, u32[]{:S(2)}, u32[]{:S(2)}) collective-permute-start(bf16[64,2048]{1,0:T(8,128)(2,1)S(1)} %get-tuple-element.69.near_ref), channel_id=1, source_target_pairs={{8,16},{12,20},{16,8},{20,12},{9,17},{13,21},{17,9},{21,13},{10,18... | collective-permute-start | bytes 786440 | tf_op jit(solution)/shard_map/ppermute | solution.py:456
  123.5 19.3 %collective-permute-start.34 = (bf16[64,1536]{1,0:T(8,128)(2,1)S(1)}, bf16[64,1536]{1,0:T(8,128)(2,1)S(1)}, u32[]{:S(2)}, u32[]{:S(2)}) collective-permute-start(bf16[64,1536]{1,0:T(8,128)(2,1)S(1)} %get-tuple-element.80), channel_id=1, source_target_pairs={{8,0},{12,4},{16,24},{20,28},{9,1},{13,5},{17,25},{21,29},{10,2},{... | collective-permute-start | bytes 589832 | tf_op jit(solution)/shard_map/ppermute | solution.py:457
  124.8 36.6 %collective-permute-start.28 = (bf16[64,2048]{1,0:T(8,128)(2,1)S(1)}, bf16[64,2048]{1,0:T(8,128)(2,1)S(1)}, u32[]{:S(2)}, u32[]{:S(2)}) collective-permute-start(bf16[64,2048]{1,0:T(8,128)(2,1)S(1)} %get-tuple-element.75), channel_id=1, source_target_pairs={{8,0},{12,4},{16,24},{20,28},{9,1},{13,5},{17,25},{21,29},{10,2},{... | collective-permute-start | bytes 786440 | tf_op jit(solution)/shard_map/ppermute | solution.py:457
  126.1 36.1 %collective-permute-start.29 = (bf16[64,2048]{1,0:T(8,128)(2,1)S(1)}, bf16[64,2048]{1,0:T(8,128)(2,1)S(1)}, u32[]{:S(2)}, u32[]{:S(2)}) collective-permute-start(bf16[64,2048]{1,0:T(8,128)(2,1)S(1)} %collective-permute-done.27.across_ref), channel_id=1, source_target_pairs={{8,0},{12,4},{16,24},{20,28},{9,1},{13,5},{17,25},{21,29},{10,2},{... | collective-permute-start | bytes 786440 | tf_op jit(solution)/shard_map/ppermute | solution.py:458
  127.4 32.7 %collective-permute-start.35 = (bf16[64,1536]{1,0:T(8,128)(2,1)S(1)}, bf16[64,1536]{1,0:T(8,128)(2,1)S(1)}, u32[]{:S(2)}, u32[]{:S(2)}) collective-permute-start(bf16[64,1536]{1,0:T(8,128)(2,1)S(1)} %collective-permute-done.33.across_ref), channel_id=1, source_target_pairs={{8,0},{12,4},{16,24},{20,28},{9,1},{13,5},{17,25},{21,29},{10,2},{... | collective-permute-start | bytes 589832 | tf_op jit(solution)/shard_map/ppermute | solution.py:458
  142.8 24.6 %collective-permute-start.22 = (bf16[64,2048]{1,0:T(8,128)(2,1)S(1)}, bf16[64,2048]{1,0:T(8,128)(2,1)S(1)}, u32[]{:S(2)}, u32[]{:S(2)}) collective-permute-start(bf16[64,2048]{1,0:T(8,128)(2,1)S(1)} %get-tuple-element.70), channel_id=1, source_target_pairs={{8,0},{12,4},{16,24},{20,28},{9,1},{13,5},{17,25},{21,29},{10,2},{... | collective-permute-start | bytes 786440 | tf_op jit(solution)/shard_map/ppermute | solution.py:457
  144.1 26.4 %collective-permute-start.23 = (bf16[64,2048]{1,0:T(8,128)(2,1)S(1)}, bf16[64,2048]{1,0:T(8,128)(2,1)S(1)}, u32[]{:S(2)}, u32[]{:S(2)}) collective-permute-start(bf16[64,2048]{1,0:T(8,128)(2,1)S(1)} %collective-permute-done.21.across_ref), channel_id=1, source_target_pairs={{8,0},{12,4},{16,24},{20,28},{9,1},{13,5},{17,25},{21,29},{10,2},{... | collective-permute-start | bytes 786440 | tf_op jit(solution)/shard_map/ppermute | solution.py:458
  160.1 12.5 %collective-permute-start.16 = (bf16[64,1536]{1,0:T(8,128)(2,1)S(1)}, bf16[64,1536]{1,0:T(8,128)(2,1)S(1)}, u32[]{:S(2)}, u32[]{:S(2)}) collective-permute-start(bf16[64,1536]{1,0:T(8,128)(2,1)S(1)} %get-tuple-element.65), channel_id=1, source_target_pairs={{8,0},{12,4},{16,24},{20,28},{9,1},{13,5},{17,25},{21,29},{10,2},{... | collective-permute-start | bytes 589832 | tf_op jit(solution)/shard_map/ppermute | solution.py:457
  162.2 20.5 %collective-permute-start.37 = (bf16[1024,256]{1,0:T(8,128)(2,1)S(1)}, bf16[1024,256]{1,0:T(8,128)(2,1)S(1)}, u32[]{:S(2)}, u32[]{:S(2)}) collective-permute-start(bf16[1024,256]{1,0:T(8,128)(2,1)S(1)} %add.111), channel_id=1, source_target_pairs={{0,2},{1,3},{4,6},{5,7},{9,11},{8,10},{13,15},{12,14},{18,16},{19,... | collective-permute-start | bytes 1572872 | tf_op jit(solution)/shard_map/ppermute | solution.py:443
  167.4 18.1 %collective-permute-start.40 = (bf16[128,2048]{1,0:T(8,128)(2,1)S(1)}, bf16[128,2048]{1,0:T(8,128)(2,1)S(1)}, u32[]{:S(2)}, u32[]{:S(2)}) collective-permute-start(bf16[128,2048]{1,0:T(8,128)(2,1)S(1)} %get-tuple-element.93.mine_ref), channel_id=1, source_target_pairs={{0,4},{4,0},{8,12},{12,8},{16,20},{20,16},{24,28},{28,24},{1,5},{5... | collective-permute-start | bytes 1572872 | tf_op jit(solution)/shard_map/ppermute | solution.py:462
  172.5 16.0 %collective-permute-start.39 = (bf16[128,2048]{1,0:T(8,128)(2,1)S(1)}, bf16[128,2048]{1,0:T(8,128)(2,1)S(1)}, u32[]{:S(2)}, u32[]{:S(2)}) collective-permute-start(bf16[128,2048]{1,0:T(8,128)(2,1)S(1)} %get-tuple-element.92.mine_ref), channel_id=1, source_target_pairs={{0,4},{4,0},{8,12},{12,8},{16,20},{20,16},{24,28},{28,24},{1,5},{5... | collective-permute-start | bytes 1572872 | tf_op jit(solution)/shard_map/ppermute | solution.py:462
  (22 other events, 278.7 us)

commit v5 on v4

--- a/solution.py
+++ b/solution.py
@@ -22,7 +22,7 @@
 
 F32, BF16 = jnp.float32, jnp.bfloat16
 CORES = 2
-CHUNKS = (3, 4, 4, 3)
+CHUNKS = (3, 4, 5, 2)
 MIB = 1 << 20
 
 VMEM = pl.BlockSpec(memory_space=pltpu.VMEM)
@@ -80,51 +80,81 @@
     return best
 
 
-def project_kernel(slot_ref, basis_hbm, act_hbm, *refs):
-    *outs, turned, basis_buf, basis_sem, act_buf, act_sem = refs
+def project_kernel(spans, slot_ref, codes_ref, ids_ref, basis_hbm, act_hbm, m_hbm, v_hbm, *refs):
+    outs, refs = refs[: len(spans)], refs[len(spans) :]
+    weights_ref, sum_ref, mv_ref, turned, basis_buf, basis_sem, act_buf, act_sem = refs[:8]
+    m_buf, v_buf, m_sem, v_sem = refs[8:]
     rows = basis_buf.shape[1] // slot_ref.shape[0]
-    pieces = act_sem.shape[0]
-    size = act_buf.shape[0] // pieces
     copy = pltpu.make_async_copy(basis_hbm, basis_buf, basis_sem)
     copy.start()
     copies = []
-    for i in range(pieces):
-        part = pl.ds(i * size, size)
+    for i, (start, count) in enumerate(spans):
+        part = pl.ds(start, count)
         copies.append(pltpu.make_async_copy(act_hbm.at[part], act_buf.at[part], act_sem.at[i]))
         copies[-1].start()
+    m_copy = pltpu.make_async_copy(m_hbm, m_buf, m_sem)
+    v_copy = pltpu.make_async_copy(v_hbm, v_buf, v_sem)
+    m_copy.start()
+    v_copy.start()
+    unmasked = (ids_ref[...] != pad_token).astype(F32)
+    weights = unmasked * jnp.exp(reward_temp * codes_ref[...].astype(F32))
+    weights_ref[...] = weights
+    sum_ref[...] = jnp.broadcast_to(jnp.sum(weights, axis=1, keepdims=True), sum_ref.shape)
     copy.wait()
     flipped = basis_buf[...].T
     for n in range(slot_ref.shape[0]):
         at = pl.multiple_of(slot_ref[n] * rows, rows)
         turned[pl.ds(at, rows), :] = flipped[n * rows : (n + 1) * rows, :]
+    largest = max(count for _, count in spans)
     i = 0
-    for out_ref in outs:
-        for at in range(0, out_ref.shape[1], size):
-            copies[i].wait()
-            out_ref[:, at : at + size] = lax.dot_general(
-                turned[...],
-                act_buf[i * size : (i + 1) * size, :],
-                (((1,), (1,)), ((), ())),
-                preferred_element_type=F32,
-            ).astype(out_ref.dtype)
-            i += 1
-
-
-def project(slots, basis, activations, spans):
+    while i < len(spans):
+        group = [i]
+        while group[-1] + 1 < len(spans) and sum(spans[k][1] for k in group) + spans[group[-1] + 1][1] <= largest:
+            group.append(group[-1] + 1)
+        for k in group:
+            copies[k].wait()
+        first, last = spans[group[0]][0], sum(spans[group[-1]])
+        product = lax.dot_general(
+            turned[...],
+            act_buf[first:last, :],
+            (((1,), (1,)), ((), ())),
+            preferred_element_type=F32,
+        ).astype(BF16)
+        for k in group:
+            start, count = spans[k]
+            outs[k][...] = product[:, start - first : start - first + count]
+        i = group[-1] + 1
+    count = m_buf.shape[0]
+    m_copy.wait()
+    mv_ref[:count] = m_buf[...].astype(BF16)
+    v_copy.wait()
+    mv_ref[count:] = v_buf[...].astype(BF16)
+
+
+def project(slots, codes, ids, basis, activations, first, second, spans):
     tokens, depth = activations.shape
     rank = basis.shape[1]
-    size = 256 if all(count % 256 == 0 for _, count in spans) else 128
+    rows, full = first.shape
     return pl.pallas_call(
-        project_kernel,
-        out_shape=[jax.ShapeDtypeStruct((rank, count), BF16) for _, count in spans],
-        in_specs=[SMEM, HBM, HBM],
-        out_specs=[VMEM] * len(spans),
+        functools.partial(project_kernel, spans),
+        out_shape=[
+            *(jax.ShapeDtypeStruct((rank, count), BF16) for _, count in spans),
+            jax.ShapeDtypeStruct((1, tokens), F32),
+            jax.ShapeDtypeStruct((8, 128), F32),
+            jax.ShapeDtypeStruct((2 * rows, full), BF16),
+        ],
+        in_specs=[SMEM, VMEM, VMEM, HBM, HBM, HBM, HBM],
+        out_specs=[VMEM] * (len(spans) + 3),
         scratch_shapes=[
             pltpu.VMEM((rank, depth), BF16),
             pltpu.VMEM((depth, rank), BF16),
             pltpu.SemaphoreType.DMA,
             pltpu.VMEM((tokens, depth), BF16),
-            pltpu.SemaphoreType.DMA((tokens // size,)),
+            pltpu.SemaphoreType.DMA((len(spans),)),
+            pltpu.VMEM((rows, full), F32),
+            pltpu.VMEM((rows, full), F32),
+            pltpu.SemaphoreType.DMA,
+            pltpu.SemaphoreType.DMA,
         ],
         compiler_params=pltpu.CompilerParams(vmem_limit_bytes=52 * MIB),
         cost_estimate=pl.CostEstimate(
@@ -133,7 +163,7 @@
             transcendentals=0,
         ),
         name="project",
-    )(slots, basis, activations)
+    )(slots, codes, ids, basis, activations, first, second)
 
 
 def small(limit_mib):
@@ -362,10 +392,12 @@
 
 
 def token_pieces(tokens):
-    unit = 256 if tokens % 256 == 0 else 128
-    count = tokens // unit
-    sizes = [(count // 4 + (i < count % 4)) * unit for i in range(4)]
-    return [(sum(sizes[:i]), size) for i, size in enumerate(sizes) if size]
+    if tokens % (6 * 128) == 0:
+        sizes = [tokens // 3, tokens // 3, tokens // 6, tokens // 6]
+    else:
+        count = tokens // 128
+        sizes = [(count // 4 + (i < count % 4)) * 128 for i in range(4)]
+    return [(sum(sizes[:i]), size) for i, size in enumerate(sizes)]
 
 
 def local_line(activations, out_grads, basis, first_moment, second_moment, reward_codes, token_ids):
@@ -400,7 +432,16 @@
     basis_rows = lax.dynamic_slice_in_dim(basis, data_index % per_owner * row_count, row_count, 0)
     basis_rows = jnp.where(tensor_index == owner, basis_rows, jnp.zeros_like(basis_rows))
     bits = [1 << b for b in range(tensor_count.bit_length() - 1)]
-    parts = list(project(slots, basis, activations, token_pieces(tokens)))
+    *parts, weights, normalizer, packed = project(
+        slots,
+        reward_codes.reshape(1, tokens),
+        token_ids.reshape(1, tokens),
+        basis,
+        activations,
+        first_moment,
+        second_moment,
+        token_pieces(tokens),
+    )
     got = [None] * len(parts)
     for step in range(len(bits)):
         for i, part in enumerate(parts):
@@ -410,9 +451,6 @@
             pairs = [(t, t ^ bit) for t in range(tensor_count)]
             got[i] = lax.ppermute(part, "tensor", pairs)
 
-    unmasked = (token_ids != pad_token).astype(F32)
-    weights = unmasked * jnp.exp(reward_temp * reward_codes.astype(F32))
-    normalizer = jnp.full((8, 128), jnp.sum(weights), F32)
     for b in range(data_count.bit_length() - 1):
         pairs = [(i, i ^ (1 << b)) for i in range(data_count)]
         normalizer = normalizer + lax.ppermute(normalizer, "dp", pairs)
@@ -421,10 +459,9 @@
     lefts = []
     for (start, count), part, other in zip(token_pieces(tokens), parts, got):
         total = part.astype(F32) + other.astype(F32)
-        lefts.append((weights[None, start : start + count] * total).astype(BF16))
-
-    moved = lax.ppermute(jnp.concatenate([first_moment, second_moment]).astype(BF16), "dp", inward)
-    lefts, moved, scale = lax.optimization_barrier((lefts, moved, scale))
+        lefts.append((weights[:, start : start + count] * total).astype(BF16))
+
+    moved = lax.ppermute(packed, "dp", inward)
     out_grads, basis_rows, hub, slots = lax.optimization_barrier(
         (out_grads, basis_rows, hub, slots)
     )

time: 195 us -> 211 us (1.082)
  waiting for transfers between devices: 83.1 us -> 104 us
  other arithmetic: 10.4 us -> 2.65 us
  starting transfers between devices: 47.1 us -> 50.9 us
    ppermute x4, waiting for transfers between devices: 15.3 us -> 41.7 us  [local_line(): sent = lax.ppermute(ready, 'dp', outward)]
    ppermute x4, waiting for transfers between devices: 25 us -> 5.52 us  [local_line(): more = lax.ppermute(beyond, 'dp', outward)]
    ppermute x3, waiting for transfers between devices: 0.01 us -> 17.9 us  [local_line(): normalizer = normalizer + lax.ppermute(normalizer, 'dp', pairs)]
    ppermute x4, waiting for transfers between devices: 31.2 us -> 24.7 us  [local_line(): came = lax.ppermute(mine, 'dp', inward)]
    ppermute x4, starting transfers between devices: 6.19 us -> 12.5 us  [local_line(): came = lax.ppermute(mine, 'dp', inward)]
    ppermute x2, waiting for transfers between devices: 0.01 us -> 3.17 us  [local_line(): basis_rows = basis_rows + lax.ppermute(basis_rows, ('dp', 'tensor'), pairs)]
    pallas_call x1, Pallas kernels: 10.9 us -> 7.89 us  [project(): pl.pallas_call(functools.partial(project_kernel, spans), out_shape=[*(jax...]
    ppermute x3, starting transfers between devices: 3.71 us -> 0.67 us  [local_line(): normalizer = normalizer + lax.ppermute(normalizer, 'dp', pairs)]
  transfers between devices with their start and end apart: 42 -> 42, of which waited for: 11 -> 14; matrix products, arithmetic and copies ran while one was open for 5% -> 1% of each run, Pallas kernels for 22% -> 16%
where the time goes in v5:
time: 211 us; the launch traced here: 210 us
  waiting for transfers between devices  104 us (49%)
  starting transfers between devices  50.9 us (24%)
  Pallas kernels  48.2 us (23%)
  other arithmetic  2.65 us (1%)
  between operations  2.24 us (1%)
    ppermute x4, waiting for transfers between devices, local_line(): sent = lax.ppermute(ready, 'dp', outward)  41.7 us
    ppermute x4, waiting for transfers between devices, local_line(): came = lax.ppermute(mine, 'dp', inward)  24.7 us
    ppermute x3, waiting for transfers between devices, local_line(): normalizer = normalizer + lax.ppermute(normalizer, 'dp', pairs)  17.9 us
    ppermute x4, starting transfers between devices, local_line(): came = lax.ppermute(mine, 'dp', inward)  12.5 us
    pallas_call x4, Pallas kernels, gradient_chunk(): pl.pallas_call(functools.partial(gradient_kernel, start, pick(width, 512)...  12 us
    pallas_call x2, Pallas kernels, load_rows(): pl.pallas_call(functools.partial(load_kernel, start), out_shape=jax.Shape...  11.7 us
    pallas_call x4, Pallas kernels, spread_chunk(): pl.pallas_call(functools.partial(spread_kernel, start), out_shape=jax.Sha...  11.3 us
    ppermute x8, waiting for transfers between devices, local_line(): got[i] = lax.ppermute(part, 'tensor', pairs)  11 us
  transfers between devices with their start and end apart: 42, of which 14 were waited for; matrix products, arithmetic and copies ran while one was open for 1% of the time, Pallas kernels for 16%

profile of v5, /device:TPU:0, one launch (start us, length us, event | category | flops | bytes accessed | tf_op | source)
XLA Modules:
  0.0 210.0 jit_solution(13851142379791328928)
XLA Ops:
  2.1 7.9 %project.1 = (bf16[256,768]{1,0:T(8,128)(2,1)S(1)}, bf16[256,768]{1,0:T(8,128)(2,1)S(1)}, bf16[256,384]{1,0:T(8,128)(2,1)S(1)}, bf16[256,384]{1,0:T(8,128)(2,1)S...) custom-call(s32[8]{0:T(128)S(1)} %fusion.slot_ref, s32[1,2304]{1,0:T(1,128)S(1)} %reshape.18.codes_ref, ...), custom_call_target="tpu_custom_call" | custom-call | flops 2415919104 | bytes 11665408 | tf_op jit(solution)/shard_map/project/pallas_call | solution.py:138
  10.0 3.0 %collective-permute-start.7 = (bf16[256,384]{1,0:T(8,128)(2,1)S(1)}, bf16[256,384]{1,0:T(8,128)(2,1)S(1)}, u32[]{:S(2)}, u32[]{:S(2)}) collective-permute-start(bf16[256,384]{1,0:T(8,128)(2,1)S(1)} %get-tuple-element.51), channel_id=1, source_target_pairs={{0,1},{1,0},{2,3},{3,2},{4,5},{5,4},{6,7},{7,6},{8,9},{9,8},{10,11... | collective-permute-start | bytes 589832 | tf_op jit(solution)/shard_map/ppermute | solution.py:452
  16.4 4.3 %load.3.refs_5_ = bf16[768,7168]{1,0:T(8,128)(2,1)S(1)} custom-call(bf16[2304,7168]{1,0:T(8,128)(2,1)} %source.1), custom_call_target="tpu_custom_call" | custom-call | flops 768000000 | bytes 22020096 | tf_op jit(solution)/shard_map/load/pallas_call | solution.py:189
  20.6 7.4 %load.2.refs_4_ = bf16[1536,7168]{1,0:T(8,128)(2,1)S(1)} custom-call(bf16[2304,7168]{1,0:T(8,128)(2,1)} %source.1), custom_call_target="tpu_custom_call" | custom-call | flops 1536000000 | bytes 44040192 | tf_op jit(solution)/shard_map/load/pallas_call | solution.py:189
  32.7 2.7 %collective-permute-done.8 = bf16[256,384]{1,0:T(8,128)(2,1)S(1)} collective-permute-done((bf16[256,384]{1,0:T(8,128)(2,1)S(1)}, bf16[256,384]{1,0:T(8,128)(2,1)S(1)}, u32[]{:S(2)}, u32[]{:S(2)}) %collective-permute-start.8) | collective-permute-done | bytes 196640 | tf_op jit(solution)/shard_map/ppermute | solution.py:452
  38.1 4.3 %collective-permute-done.4 = bf16[256,768]{1,0:T(8,128)(2,1)S(1)} collective-permute-done((bf16[256,768]{1,0:T(8,128)(2,1)S(1)}, bf16[256,768]{1,0:T(8,128)(2,1)S(1)}, u32[]{:S(2)}, u32[]{:S(2)}) %collective-permute-start.4) | collective-permute-done | bytes 393248 | tf_op jit(solution)/shard_map/ppermute | solution.py:452
  44.1 4.3 %gradient.5 = (bf16[128,2560]{1,0:T(8,128)(2,1)S(1)}, bf16[128,2560]{1,0:T(8,128)(2,1)S(1)}) custom-call(bf16[256,768]{1,0:T(8,128)(2,1)S(1)} %multiply_convert_fusion.1.refs_0_, bf16[256,768]{1,0:T(8,128)(2,1)S(1)} %multiply_convert_fusion.refs_1_, bf16[256,384]{1,0:T(8,128)(2,1)S(1)} %multiply_convert_fusion.3.refs_2_, ...), custom_call_target="tpu_custom_call" | custom-call | flops 3019898880 | bytes 2621440 | tf_op jit(solution)/shard_map/gradient/pallas_call | solution.py:232
  51.6 3.4 %gradient.6 = (bf16[128,2048]{1,0:T(8,128)(2,1)S(1)}, bf16[128,2048]{1,0:T(8,128)(2,1)S(1)}) custom-call(bf16[256,768]{1,0:T(8,128)(2,1)S(1)} %multiply_convert_fusion.1.refs_0_, bf16[256,768]{1,0:T(8,128)(2,1)S(1)} %multiply_convert_fusion.refs_1_, bf16[256,384]{1,0:T(8,128)(2,1)S(1)} %multiply_convert_fusion.3.refs_2_, ...), custom_call_target="tpu_custom_call" | custom-call | flops 2415919104 | bytes 2097152 | tf_op jit(solution)/shard_map/gradient/pallas_call | solution.py:232
  55.3 3.5 %collective-permute-start.31 = (bf16[128,1536]{1,0:T(8,128)(2,1)S(1)}, bf16[128,1536]{1,0:T(8,128)(2,1)S(1)}, u32[]{:S(2)}, u32[]{:S(2)}) collective-permute-start(bf16[128,1536]{1,0:T(8,128)(2,1)S(1)} %add.109.own_ref), channel_id=1, source_target_pairs={{0,8},{4,12},{24,16},{28,20},{1,9},{5,13},{25,17},{29,21},{2,10},{... | collective-permute-start | bytes 1179656 | tf_op jit(solution)/shard_map/ppermute | solution.py:488
  61.5 3.4 %collective-permute-start.36 = (bf16[1024,256]{1,0:T(8,128)(2,1)S(1)}, bf16[1024,256]{1,0:T(8,128)(2,1)S(1)}, u32[]{:S(2)}, u32[]{:S(2)}) collective-permute-start(bf16[1024,256]{1,0:T(8,128)(2,1)S(1)} %dynamic-slice_select_fusion), channel_id=1, source_target_pairs={{0,1},{4,5},{9,8},{13,12},{18,19},{22,23},{27,26},{31,30}} | collective-permute-start | bytes 1572872 | tf_op jit(solution)/shard_map/ppermute | solution.py:480
  65.0 16.9 %collective-permute-done.1 = f32[8,128]{1,0:T(8,128)S(1)} collective-permute-done((f32[8,128]{1,0:T(8,128)S(1)}, f32[8,128]{1,0:T(8,128)S(1)}, u32[]{:S(2)}, u32[]{:S(2)}) %collective-permute-start.1) | collective-permute-done | bytes 4128 | tf_op jit(solution)/shard_map/ppermute | solution.py:456
  81.9 4.4 %collective-permute-start.14 = (bf16[64,7168]{1,0:T(8,128)(2,1)S(1)}, bf16[64,7168]{1,0:T(8,128)(2,1)S(1)}, u32[]{:S(2)}, u32[]{:S(2)}) collective-permute-start(bf16[64,7168]{1,0:T(8,128)(2,1)S(1)} %copy-done.2), channel_id=1, source_target_pairs={{0,8},{4,12},{24,16},{28,20},{1,9},{5,13},{25,17},{29,21},{2,10},{... | collective-permute-start | bytes 2752520 | tf_op jit(solution)/shard_map/ppermute | solution.py:464
  86.9 4.6 %collective-permute-start.25 = (bf16[128,2048]{1,0:T(8,128)(2,1)S(1)}, bf16[128,2048]{1,0:T(8,128)(2,1)S(1)}, u32[]{:S(2)}, u32[]{:S(2)}) collective-permute-start(bf16[128,2048]{1,0:T(8,128)(2,1)S(1)} %add.107.own_ref), channel_id=1, source_target_pairs={{0,8},{4,12},{24,16},{28,20},{1,9},{5,13},{25,17},{29,21},{2,10},{... | collective-permute-start | bytes 1572872 | tf_op jit(solution)/shard_map/ppermute | solution.py:488
  92.3 24.7 %collective-permute-done.25.came_ref = bf16[128,2048]{1,0:T(8,128)(2,1)S(1)} collective-permute-done((bf16[128,2048]{1,0:T(8,128)(2,1)S(1)}, bf16[128,2048]{1,0:T(8,128)(2,1)S(1)}, u32[]{:S(2)}, u32[]{:S(2)}) %collective-permute-start.25) | collective-permute-done | bytes 524320 | tf_op jit(solution)/shard_map/ppermute | solution.py:488
  130.5 18.2 %collective-permute-done.34.sent_ref = bf16[64,1536]{1,0:T(8,128)(2,1)S(1)} collective-permute-done((bf16[64,1536]{1,0:T(8,128)(2,1)S(1)}, bf16[64,1536]{1,0:T(8,128)(2,1)S(1)}, u32[]{:S(2)}, u32[]{:S(2)}) %collective-permute-start.34) | collective-permute-done | bytes 196640 | tf_op jit(solution)/shard_map/ppermute | solution.py:494
  152.8 3.1 %collective-permute-start.12 = (bf16[128,1024]{1,0:T(8,128)(2,1)S(1)}, bf16[128,1024]{1,0:T(8,128)(2,1)S(1)}, u32[]{:S(2)}, u32[]{:S(2)}) collective-permute-start(bf16[128,1024]{1,0:T(8,128)(2,1)S(1)} %add.103.own_ref), channel_id=1, source_target_pairs={{0,8},{4,12},{24,16},{28,20},{1,9},{5,13},{25,17},{29,21},{2,10},{... | collective-permute-start | bytes 786440 | tf_op jit(solution)/shard_map/ppermute | solution.py:488
  156.9 15.6 %collective-permute-done.28.sent_ref = bf16[64,2048]{1,0:T(8,128)(2,1)S(1)} collective-permute-done((bf16[64,2048]{1,0:T(8,128)(2,1)S(1)}, bf16[64,2048]{1,0:T(8,128)(2,1)S(1)}, u32[]{:S(2)}, u32[]{:S(2)}) %collective-permute-start.28) | collective-permute-done | bytes 262176 | tf_op jit(solution)/shard_map/ppermute | solution.py:494
  172.5 3.1 %collective-permute-start.37 = (bf16[1024,256]{1,0:T(8,128)(2,1)S(1)}, bf16[1024,256]{1,0:T(8,128)(2,1)S(1)}, u32[]{:S(2)}, u32[]{:S(2)}) collective-permute-start(bf16[1024,256]{1,0:T(8,128)(2,1)S(1)} %add.111), channel_id=1, source_target_pairs={{0,2},{1,3},{4,6},{5,7},{9,11},{8,10},{13,15},{12,14},{18,16},{19,... | collective-permute-start | bytes 1572872 | tf_op jit(solution)/shard_map/ppermute | solution.py:480
  181.1 3.2 %collective-permute-done.37 = bf16[1024,256]{1,0:T(8,128)(2,1)S(1)} collective-permute-done((bf16[1024,256]{1,0:T(8,128)(2,1)S(1)}, bf16[1024,256]{1,0:T(8,128)(2,1)S(1)}, u32[]{:S(2)}, u32[]{:S(2)}) %collective-permute-start.37) | collective-permute-done | bytes 524320 | tf_op jit(solution)/shard_map/ppermute | solution.py:480
  187.1 7.9 %collective-permute-done.16.sent_ref = bf16[64,1024]{1,0:T(8,128)(2,1)S(1)} collective-permute-done((bf16[64,1024]{1,0:T(8,128)(2,1)S(1)}, bf16[64,1024]{1,0:T(8,128)(2,1)S(1)}, u32[]{:S(2)}, u32[]{:S(2)}) %collective-permute-start.16) | collective-permute-done | bytes 131104 | tf_op jit(solution)/shard_map/ppermute | solution.py:494
  195.0 2.6 %collective-permute-done.17.more_ref = bf16[64,1024]{1,0:T(8,128)(2,1)S(1)} collective-permute-done((bf16[64,1024]{1,0:T(8,128)(2,1)S(1)}, bf16[64,1024]{1,0:T(8,128)(2,1)S(1)}, u32[]{:S(2)}, u32[]{:S(2)}) %collective-permute-start.17) | collective-permute-done | bytes 131104 | tf_op jit(solution)/shard_map/ppermute | solution.py:495
  198.5 2.6 %spread.4.rest_0_ = bf16[1024,7168]{1,0:T(8,128)(2,1)} custom-call(s32[8]{0:T(128)S(1)} %fusion.slot_ref, bf16[1024,256]{1,0:T(8,128)(2,1)S(1)} %add.112.basis_ref, bf16[128,1536]{1,0:T(8,128)(2,1)S(1)} %get-tuple-element.88.mine_ref, bf16[128,1536]{1,0:T(8,128)(2,1)S(1)} %collective-permute-done.41.other_ref), custom_call_target="tpu_custom_call" | custom-call | flops 805306368 | bytes 4456448 | tf_op jit(solution)/shard_map/spread/pallas_call | solution.py:373
  201.1 3.0 %spread.5.rest_0_ = bf16[1024,7168]{1,0:T(8,128)(2,1)} custom-call(s32[8]{0:T(128)S(1)} %fusion.slot_ref, bf16[1024,256]{1,0:T(8,128)(2,1)S(1)} %add.112.basis_ref, bf16[128,2048]{1,0:T(8,128)(2,1)S(1)} %get-tuple-element.87.mine_ref, bf16[128,2048]{1,0:T(8,128)(2,1)S(1)} %collective-permute-done.40.other_ref, ...), custom_call_target="tpu_custom_call", output_to_operand_aliasing={{}: (4, {})} | custom-call | flops 1073741824 | bytes 5767168 | tf_op jit(solution)/shard_map/spread/pallas_call | solution.py:373
  204.2 3.5 %spread.6.rest_0_ = bf16[1024,7168]{1,0:T(8,128)(2,1)} custom-call(s32[8]{0:T(128)S(1)} %fusion.slot_ref, bf16[1024,256]{1,0:T(8,128)(2,1)S(1)} %add.112.basis_ref, bf16[128,2560]{1,0:T(8,128)(2,1)S(1)} %get-tuple-element.86.mine_ref, bf16[128,2560]{1,0:T(8,128)(2,1)S(1)} %collective-permute-done.39.other_ref, ...), custom_call_target="tpu_custom_call", output_to_operand_aliasing={{}: (4, {})} | custom-call | flops 1342177280 | bytes 7077888 | tf_op jit(solution)/shard_map/spread/pallas_call | solution.py:373
  (113 shorter events, 50.0 us)
Async XLA Ops:
  10.0 18.1 %collective-permute-start.7 = (bf16[256,384]{1,0:T(8,128)(2,1)S(1)}, bf16[256,384]{1,0:T(8,128)(2,1)S(1)}, u32[]{:S(2)}, u32[]{:S(2)}) collective-permute-start(bf16[256,384]{1,0:T(8,128)(2,1)S(1)} %get-tuple-element.51), channel_id=1, source_target_pairs={{0,1},{1,0},{2,3},{3,2},{4,5},{5,4},{6,7},{7,6},{8,9},{9,8},{10,11... | collective-permute-start | bytes 589832 | tf_op jit(solution)/shard_map/ppermute | solution.py:452
  13.0 17.1 %collective-permute-start.9 = (bf16[256,384]{1,0:T(8,128)(2,1)S(1)}, bf16[256,384]{1,0:T(8,128)(2,1)S(1)}, u32[]{:S(2)}, u32[]{:S(2)}) collective-permute-start(bf16[256,384]{1,0:T(8,128)(2,1)S(1)} %get-tuple-element.52), channel_id=1, source_target_pairs={{0,2},{1,3},{2,0},{3,1},{4,6},{5,7},{6,4},{7,5},{8,10},{9,11},{10,... | collective-permute-start | bytes 589832 | tf_op jit(solution)/shard_map/ppermute | solution.py:452
  14.6 17.2 %collective-permute-start.3 = (bf16[256,768]{1,0:T(8,128)(2,1)S(1)}, bf16[256,768]{1,0:T(8,128)(2,1)S(1)}, u32[]{:S(2)}, u32[]{:S(2)}) collective-permute-start(bf16[256,768]{1,0:T(8,128)(2,1)S(1)} %get-tuple-element.49), channel_id=1, source_target_pairs={{0,1},{1,0},{2,3},{3,2},{4,5},{5,4},{6,7},{7,6},{8,9},{9,8},{10,11... | collective-permute-start | bytes 1179656 | tf_op jit(solution)/shard_map/ppermute | solution.py:452
  15.1 17.4 %collective-permute-start.5 = (bf16[256,768]{1,0:T(8,128)(2,1)S(1)}, bf16[256,768]{1,0:T(8,128)(2,1)S(1)}, u32[]{:S(2)}, u32[]{:S(2)}) collective-permute-start(bf16[256,768]{1,0:T(8,128)(2,1)S(1)} %get-tuple-element.50), channel_id=1, source_target_pairs={{0,2},{1,3},{2,0},{3,1},{4,6},{5,7},{6,4},{7,5},{8,10},{9,11},{10,... | collective-permute-start | bytes 1179656 | tf_op jit(solution)/shard_map/ppermute | solution.py:452
  55.1 31.3 %collective-permute-start.24 = (bf16[128,2048]{1,0:T(8,128)(2,1)S(1)}, bf16[128,2048]{1,0:T(8,128)(2,1)S(1)}, u32[]{:S(2)}, u32[]{:S(2)}) collective-permute-start(bf16[128,2048]{1,0:T(8,128)(2,1)S(1)} %get-tuple-element.66), channel_id=1, source_target_pairs={{0,4},{4,0},{8,12},{12,8},{16,20},{20,16},{24,28},{28,24},{1,5},{5... | collective-permute-start | bytes 1572872 | tf_op jit(solution)/shard_map/ppermute | solution.py:487
  55.3 31.6 %collective-permute-start.31 = (bf16[128,1536]{1,0:T(8,128)(2,1)S(1)}, bf16[128,1536]{1,0:T(8,128)(2,1)S(1)}, u32[]{:S(2)}, u32[]{:S(2)}) collective-permute-start(bf16[128,1536]{1,0:T(8,128)(2,1)S(1)} %add.109.own_ref), channel_id=1, source_target_pairs={{0,8},{4,12},{24,16},{28,20},{1,9},{5,13},{25,17},{29,21},{2,10},{... | collective-permute-start | bytes 1179656 | tf_op jit(solution)/shard_map/ppermute | solution.py:488
  59.0 32.6 %collective-permute-start.19 = (bf16[128,2560]{1,0:T(8,128)(2,1)S(1)}, bf16[128,2560]{1,0:T(8,128)(2,1)S(1)}, u32[]{:S(2)}, u32[]{:S(2)}) collective-permute-start(bf16[128,2560]{1,0:T(8,128)(2,1)S(1)} %add.105.own_ref), channel_id=1, source_target_pairs={{0,8},{4,12},{24,16},{28,20},{1,9},{5,13},{25,17},{29,21},{2,10},{... | collective-permute-start | bytes 1966088 | tf_op jit(solution)/shard_map/ppermute | solution.py:488
  61.5 20.4 %collective-permute-start.1 = (f32[8,128]{1,0:T(8,128)S(1)}, f32[8,128]{1,0:T(8,128)S(1)}, u32[]{:S(2)}, u32[]{:S(2)}) collective-permute-start(f32[8,128]{1,0:T(8,128)S(1)} %add.91), channel_id=1, source_target_pairs={{0,8},{4,12},{8,0},{12,4},{16,24},{20,28},{24,16},{28,20},{1,9},{5... | collective-permute-start | bytes 12296 | tf_op jit(solution)/shard_map/ppermute | solution.py:456
  61.5 63.7 %collective-permute-start.36 = (bf16[1024,256]{1,0:T(8,128)(2,1)S(1)}, bf16[1024,256]{1,0:T(8,128)(2,1)S(1)}, u32[]{:S(2)}, u32[]{:S(2)}) collective-permute-start(bf16[1024,256]{1,0:T(8,128)(2,1)S(1)} %dynamic-slice_select_fusion), channel_id=1, source_target_pairs={{0,1},{4,5},{9,8},{13,12},{18,19},{22,23},{27,26},{31,30}} | collective-permute-start | bytes 1572872 | tf_op jit(solution)/shard_map/ppermute | solution.py:480
  81.9 37.7 %collective-permute-start.14 = (bf16[64,7168]{1,0:T(8,128)(2,1)S(1)}, bf16[64,7168]{1,0:T(8,128)(2,1)S(1)}, u32[]{:S(2)}, u32[]{:S(2)}) collective-permute-start(bf16[64,7168]{1,0:T(8,128)(2,1)S(1)} %copy-done.2), channel_id=1, source_target_pairs={{0,8},{4,12},{24,16},{28,20},{1,9},{5,13},{25,17},{29,21},{2,10},{... | collective-permute-start | bytes 2752520 | tf_op jit(solution)/shard_map/ppermute | solution.py:464
  86.4 31.3 %collective-permute-start.2 = (f32[8,128]{1,0:T(8,128)S(1)}, f32[8,128]{1,0:T(8,128)S(1)}, u32[]{:S(2)}, u32[]{:S(2)}) collective-permute-start(f32[8,128]{1,0:T(8,128)S(1)} %add.92), channel_id=1, source_target_pairs={{0,16},{4,20},{8,24},{12,28},{16,0},{20,4},{24,8},{28,12},{1,17},{... | collective-permute-start | bytes 12296 | tf_op jit(solution)/shard_map/ppermute | solution.py:456
  86.9 30.1 %collective-permute-start.25 = (bf16[128,2048]{1,0:T(8,128)(2,1)S(1)}, bf16[128,2048]{1,0:T(8,128)(2,1)S(1)}, u32[]{:S(2)}, u32[]{:S(2)}) collective-permute-start(bf16[128,2048]{1,0:T(8,128)(2,1)S(1)} %add.107.own_ref), channel_id=1, source_target_pairs={{0,8},{4,12},{24,16},{28,20},{1,9},{5,13},{25,17},{29,21},{2,10},{... | collective-permute-start | bytes 1572872 | tf_op jit(solution)/shard_map/ppermute | solution.py:488
  91.6 28.0 %collective-permute-start.32 = (bf16[64,1536]{1,0:T(8,128)(2,1)S(1)}, bf16[64,1536]{1,0:T(8,128)(2,1)S(1)}, u32[]{:S(2)}, u32[]{:S(2)}) collective-permute-start(bf16[64,1536]{1,0:T(8,128)(2,1)S(1)} %slice_add_fusion.2), channel_id=1, source_target_pairs={{8,16},{12,20},{16,8},{20,12},{9,17},{13,21},{17,9},{21,13},{10,18... | collective-permute-start | bytes 589832 | tf_op jit(solution)/shard_map/ppermute | solution.py:489
  124.5 25.4 %collective-permute-start.27 = (bf16[64,2048]{1,0:T(8,128)(2,1)S(1)}, bf16[64,2048]{1,0:T(8,128)(2,1)S(1)}, u32[]{:S(2)}, u32[]{:S(2)}) collective-permute-start(bf16[64,2048]{1,0:T(8,128)(2,1)S(1)} %get-tuple-element.68.near_ref), channel_id=1, source_target_pairs={{8,16},{12,20},{16,8},{20,12},{9,17},{13,21},{17,9},{21,13},{10,18... | collective-permute-start | bytes 786440 | tf_op jit(solution)/shard_map/ppermute | solution.py:493
  125.2 23.4 %collective-permute-start.34 = (bf16[64,1536]{1,0:T(8,128)(2,1)S(1)}, bf16[64,1536]{1,0:T(8,128)(2,1)S(1)}, u32[]{:S(2)}, u32[]{:S(2)}) collective-permute-start(bf16[64,1536]{1,0:T(8,128)(2,1)S(1)} %get-tuple-element.74), channel_id=1, source_target_pairs={{8,0},{12,4},{16,24},{20,28},{9,1},{13,5},{17,25},{21,29},{10,2},{... | collective-permute-start | bytes 589832 | tf_op jit(solution)/shard_map/ppermute | solution.py:494
  126.5 26.3 %collective-permute-start.35 = (bf16[64,1536]{1,0:T(8,128)(2,1)S(1)}, bf16[64,1536]{1,0:T(8,128)(2,1)S(1)}, u32[]{:S(2)}, u32[]{:S(2)}) collective-permute-start(bf16[64,1536]{1,0:T(8,128)(2,1)S(1)} %collective-permute-done.33.across_ref), channel_id=1, source_target_pairs={{8,0},{12,4},{16,24},{20,28},{9,1},{13,5},{17,25},{21,29},{10,2},{... | collective-permute-start | bytes 589832 | tf_op jit(solution)/shard_map/ppermute | solution.py:495
  127.8 50.0 %collective-permute-start.22 = (bf16[64,2560]{1,0:T(8,128)(2,1)S(1)}, bf16[64,2560]{1,0:T(8,128)(2,1)S(1)}, u32[]{:S(2)}, u32[]{:S(2)}) collective-permute-start(bf16[64,2560]{1,0:T(8,128)(2,1)S(1)} %get-tuple-element.64), channel_id=1, source_target_pairs={{8,0},{12,4},{16,24},{20,28},{9,1},{13,5},{17,25},{21,29},{10,2},{... | collective-permute-start | bytes 983048 | tf_op jit(solution)/shard_map/ppermute | solution.py:494
  129.2 48.7 %collective-permute-start.23 = (bf16[64,2560]{1,0:T(8,128)(2,1)S(1)}, bf16[64,2560]{1,0:T(8,128)(2,1)S(1)}, u32[]{:S(2)}, u32[]{:S(2)}) collective-permute-start(bf16[64,2560]{1,0:T(8,128)(2,1)S(1)} %collective-permute-done.21.across_ref), channel_id=1, source_target_pairs={{8,0},{12,4},{16,24},{20,28},{9,1},{13,5},{17,25},{21,29},{10,2},{... | collective-permute-start | bytes 983048 | tf_op jit(solution)/shard_map/ppermute | solution.py:495
  148.6 23.9 %collective-permute-start.28 = (bf16[64,2048]{1,0:T(8,128)(2,1)S(1)}, bf16[64,2048]{1,0:T(8,128)(2,1)S(1)}, u32[]{:S(2)}, u32[]{:S(2)}) collective-permute-start(bf16[64,2048]{1,0:T(8,128)(2,1)S(1)} %get-tuple-element.69), channel_id=1, source_target_pairs={{8,0},{12,4},{16,24},{20,28},{9,1},{13,5},{17,25},{21,29},{10,2},{... | collective-permute-start | bytes 786440 | tf_op jit(solution)/shard_map/ppermute | solution.py:494
  149.9 27.0 %collective-permute-start.29 = (bf16[64,2048]{1,0:T(8,128)(2,1)S(1)}, bf16[64,2048]{1,0:T(8,128)(2,1)S(1)}, u32[]{:S(2)}, u32[]{:S(2)}) collective-permute-start(bf16[64,2048]{1,0:T(8,128)(2,1)S(1)} %collective-permute-done.27.across_ref), channel_id=1, source_target_pairs={{8,0},{12,4},{16,24},{20,28},{9,1},{13,5},{17,25},{21,29},{10,2},{... | collective-permute-start | bytes 786440 | tf_op jit(solution)/shard_map/ppermute | solution.py:495
  152.8 26.5 %collective-permute-start.12 = (bf16[128,1024]{1,0:T(8,128)(2,1)S(1)}, bf16[128,1024]{1,0:T(8,128)(2,1)S(1)}, u32[]{:S(2)}, u32[]{:S(2)}) collective-permute-start(bf16[128,1024]{1,0:T(8,128)(2,1)S(1)} %add.103.own_ref), channel_id=1, source_target_pairs={{0,8},{4,12},{24,16},{28,20},{1,9},{5,13},{25,17},{29,21},{2,10},{... | collective-permute-start | bytes 786440 | tf_op jit(solution)/shard_map/ppermute | solution.py:488
  177.8 23.3 %collective-permute-start.40 = (bf16[128,2048]{1,0:T(8,128)(2,1)S(1)}, bf16[128,2048]{1,0:T(8,128)(2,1)S(1)}, u32[]{:S(2)}, u32[]{:S(2)}) collective-permute-start(bf16[128,2048]{1,0:T(8,128)(2,1)S(1)} %get-tuple-element.87.mine_ref), channel_id=1, source_target_pairs={{0,4},{4,0},{8,12},{12,8},{16,20},{20,16},{24,28},{28,24},{1,5},{5... | collective-permute-start | bytes 1572872 | tf_op jit(solution)/shard_map/ppermute | solution.py:499
  178.8 25.3 %collective-permute-start.39 = (bf16[128,2560]{1,0:T(8,128)(2,1)S(1)}, bf16[128,2560]{1,0:T(8,128)(2,1)S(1)}, u32[]{:S(2)}, u32[]{:S(2)}) collective-permute-start(bf16[128,2560]{1,0:T(8,128)(2,1)S(1)} %get-tuple-element.86.mine_ref), channel_id=1, source_target_pairs={{0,4},{4,0},{8,12},{12,8},{16,20},{20,16},{24,28},{28,24},{1,5},{5... | collective-permute-start | bytes 1966088 | tf_op jit(solution)/shard_map/ppermute | solution.py:499
  180.1 18.4 %collective-permute-start.41 = (bf16[128,1536]{1,0:T(8,128)(2,1)S(1)}, bf16[128,1536]{1,0:T(8,128)(2,1)S(1)}, u32[]{:S(2)}, u32[]{:S(2)}) collective-permute-start(bf16[128,1536]{1,0:T(8,128)(2,1)S(1)} %get-tuple-element.88.mine_ref), channel_id=1, source_target_pairs={{0,4},{4,0},{8,12},{12,8},{16,20},{20,16},{24,28},{28,24},{1,5},{5... | collective-permute-start | bytes 1179656 | tf_op jit(solution)/shard_map/ppermute | solution.py:499
  (21 other events, 298.6 us)
